TPU v7x, 32 devices: a 4x2x2 block of a 4x4x8 slice. The times are simulated.
32 devices in a mesh: dp: 4 (over y, z), ep: 8 (over x, core).
Axes of the slice: x: 4, y: 2, z: 2, core: 2. Of those that a mesh axis runs over, the one named last changes fastest.
The devices are a block of a 4x4x8 slice.
Arguments:
- hidden_in: bfloat16 [32768, 1536], P(('dp', 'ep')), parts along dimension 0
- topk_idx: int32 [32768, 6], P(('dp', 'ep')), parts along dimension 0
- norm_gain: bfloat16 [1536], replicated
- w_router: bfloat16 [1536, 64], replicated
- w_sgate: bfloat16 [1536, 1], replicated
- s_gate: bfloat16 [1536, 1024], replicated
- s_up: bfloat16 [1536, 1024], replicated
- s_down: bfloat16 [1024, 1536], replicated
- w_gate: bfloat16 [64, 1536, 512], P('ep')
- w_up: bfloat16 [64, 1536, 512], P('ep')
- w_down: bfloat16 [64, 512, 1536], P('ep')
Outputs:
- output: bfloat16 [32768, 1536], P(('dp', 'ep')), parts along dimension 0
There are 4 independent parts. A program takes and returns all parts, laid end to end along the dimension named above; an argument that names none is the same for every part.
All inputs are finite; a program needn't handle non-finite values.
Results may differ from a plain program's by a relative error of at most 0.001.
Values are sent between devices in bfloat16 or wider.
A program may use at most 768 MiB of HBM per device.

v0:
```python
import functools

import jax
import jax.numpy as jnp
from jax import lax
from jax.experimental import pallas as pl
from jax.experimental.pallas import tpu as pltpu
from jax.sharding import PartitionSpec as P


F32, BF16 = jnp.float32, jnp.bfloat16
CLASSES = (64, 128, 192)


def norm_kernel(x_ref, gain_ref, ha_ref, hb_ref):
    gain = gain_ref[...].astype(F32)
    for i, out_ref in enumerate((ha_ref, hb_ref)):
        x = x_ref[i].astype(F32)
        inv_rms = lax.rsqrt(jnp.mean(x * x, axis=-1, keepdims=True) + 1e-6)
        out_ref[...] = (x * inv_rms * gain).astype(BF16)


def norm_call(hidden_in, norm_gain):
    toks, hidden = hidden_in.shape
    half, rows = toks // 2, 128
    out = jax.ShapeDtypeStruct((half, hidden), BF16)
    block = pl.BlockSpec((rows, hidden), lambda i: (i, 0))
    return pl.pallas_call(
        norm_kernel,
        grid=(half // rows,),
        out_shape=(out, out),
        in_specs=[pl.BlockSpec((2, rows, hidden), lambda i: (0, i, 0)), pl.BlockSpec((1, hidden), lambda i: (0, 0))],
        out_specs=(block, block),
        compiler_params=pltpu.CompilerParams(dimension_semantics=("arbitrary",)),
        cost_estimate=pl.CostEstimate(flops=4 * toks * hidden, transcendentals=toks, bytes_accessed=4 * toks * hidden),
        name="norm",
    )(hidden_in.reshape(2, half, hidden), norm_gain.reshape(1, hidden))


def final_kernel(base_a, base_b, za_ref, zb_ref, out_ref):
    out_ref[0] = (base_a[...] + za_ref[...]).astype(BF16)
    out_ref[1] = (base_b[...] + zb_ref[...]).astype(BF16)


def final_call(base_a, base_b, za, zb):
    half, hidden = za.shape
    rows = 128
    block = pl.BlockSpec((rows, hidden), lambda i: (i, 0))
    out = pl.pallas_call(
        final_kernel,
        grid=(half // rows,),
        out_shape=jax.ShapeDtypeStruct((2, half, hidden), BF16),
        in_specs=[block] * 4,
        out_specs=pl.BlockSpec((2, rows, hidden), lambda i: (0, i, 0)),
        compiler_params=pltpu.CompilerParams(dimension_semantics=("arbitrary",)),
        cost_estimate=pl.CostEstimate(flops=2 * half * hidden, transcendentals=0, bytes_accessed=20 * half * hidden),
        name="final",
    )(base_a, base_b, za, zb)
    return out.reshape(2 * half, hidden)


def shared_expert(normed, w_sgate, s_gate, s_up, s_down):
    shared_act = (jax.nn.silu(jnp.dot(normed, s_gate, preferred_element_type=F32))
                  * jnp.dot(normed, s_up, preferred_element_type=F32)).astype(BF16)
    shared_val = jnp.dot(shared_act, s_down, preferred_element_type=F32)
    return jax.nn.sigmoid(jnp.dot(normed, w_sgate, preferred_element_type=F32)) * shared_val


def route_kernel(geom, ids_ref, own_ref, sib_ref, next_ref, far_ref, prev_ref, slot_ref, gate_ref, list_ref, count_ref, hot_ref):
    top_k, slots_dev, capacity, local_max = geom
    toks = own_ref.shape[1]
    slots = 2 * slots_dev
    chip, core = ids_ref[8], ids_ref[9]
    order = lax.broadcasted_iota(jnp.int32, (slots, 1), 0)
    slot_id = chip * slots + jnp.where(order < slots_dev, core * slots_dev + order, (1 - core) * slots_dev + order - slots_dev)
    slot_id = slot_id.astype(F32)
    tables = []
    for j, ref in enumerate((own_ref, next_ref, far_ref, prev_ref)):
        pair = (own_ref[...], sib_ref[...]) if j == 0 else (ref[0], ref[1])
        tables.append(pair)
    counts = []
    for j in range(4):
        for i in range(2):
            table = tables[j][i]
            hot = jnp.zeros((slots, toks), F32)
            gate = jnp.zeros((slots, toks), F32)
            for k in range(top_k):
                hit = table[k:k + 1, :] == slot_id
                hot = hot + jnp.where(hit, 1.0, 0.0)
                if i == 0:
                    gate = gate + jnp.where(hit, table[top_k + k:top_k + k + 1, :], 0.0)
            counts.append(jnp.sum(hot, axis=1, keepdims=True))
            if i == 0:
                hot_ref[pl.ds(j * slots, slots), :] = hot
                gate_ref[j] = gate
    hot_all = hot_ref[...]
    hot_bf = hot_all.astype(BF16)
    tile = 256
    for c in range(toks // tile):
        rows = lax.broadcasted_iota(jnp.int32, (toks, tile), 0)
        cols = lax.broadcasted_iota(jnp.int32, (toks, tile), 1) + c * tile
        before = jnp.where(rows < cols, 1.0, 0.0).astype(BF16)
        pos = jnp.dot(hot_bf, before, preferred_element_type=F32)
        for j in range(4):
            lower = jnp.zeros((slots, 1), F32)
            for q in range(8):
                lower = lower + counts[q] * (ids_ref[q] < ids_ref[2 * j]).astype(F32)
            part = pos[j * slots:(j + 1) * slots]
            kept = (hot_all[j * slots:(j + 1) * slots, c * tile:(c + 1) * tile] > 0.0) & (part + lower < capacity)
            slot_ref[j, :, c * tile:(c + 1) * tile] = jnp.where(kept, part, -1.0)
            if c == 0:
                count_ref[j] = jnp.broadcast_to(jnp.clip(capacity - lower, 0.0, counts[2 * j]), (slots, 128))
    token = lax.broadcasted_iota(jnp.int32, (8, toks), 1)
    high, low = token // 32, token % 32
    row8 = lax.broadcasted_iota(jnp.int32, (8, toks), 0)
    digits = jnp.where(row8 == 0, high, low).astype(F32).astype(BF16)
    row_of = lax.broadcasted_iota(jnp.int32, (slots, toks), 0)
    count_row = lax.broadcasted_iota(jnp.int32, (slots, 128), 0)

    def lists(e, carry):
        for j in range(4):
            pos = jnp.sum(jnp.where(row_of == e, slot_ref[j], 0.0), axis=0, keepdims=True)
            want = lax.broadcasted_iota(jnp.int32, (local_max, toks), 0).astype(F32)
            pick = jnp.where(want == pos, 1.0, 0.0).astype(BF16)
            got = lax.dot_general(digits, pick, (((1,), (1,)), ((), ())), preferred_element_type=F32)
            found = 32.0 * got[0:1] + got[1:2]
            held = jnp.sum(jnp.where(count_row == e, count_ref[j], 0.0), axis=0, keepdims=True)[:, 0:1]
            lane = lax.broadcasted_iota(jnp.int32, (1, local_max), 1).astype(F32)
            found = jnp.where(lane < held, found, float(toks)).astype(jnp.int32)
            list_ref[j, e] = jnp.broadcast_to(found, (8, local_max))
        return carry

    lax.fori_loop(0, slots, lists, 0)


def route_call(ids, own, sib, nxt, far, prv, top_k, slots_dev, capacity, local_max):
    toks = own.shape[1]
    slots = 2 * slots_dev
    vmem = pl.BlockSpec(memory_space=pltpu.VMEM)
    return pl.pallas_call(
        functools.partial(route_kernel, (top_k, slots_dev, capacity, local_max)),
        out_shape=(jax.ShapeDtypeStruct((4, slots, toks), F32), jax.ShapeDtypeStruct((4, slots, toks), F32),
                   jax.ShapeDtypeStruct((4, slots, 8, local_max), jnp.int32), jax.ShapeDtypeStruct((4, slots, 128), F32)),
        in_specs=[pl.BlockSpec(memory_space=pltpu.SMEM)] + [vmem] * 5,
        out_specs=(vmem,) * 4,
        scratch_shapes=[pltpu.VMEM((4 * slots, toks), F32)],
        cost_estimate=pl.CostEstimate(flops=1_000_000, transcendentals=0, bytes_accessed=2_000_000),
        name="route",
    )(ids, own, sib, nxt, far, prv)


def expert_kernel(n_src, classes, slots_dev, depth, *refs):
    refs = list(refs)

    def take(n):
        got = refs[:n]
        del refs[:n]
        return got

    lists, counts = take(n_src), take(n_src)
    ha, hb, slot_refs, gate_refs = take(n_src), take(n_src), take(n_src), take(n_src)
    own, sib = take(3), take(3)
    take(1)
    ya, yb = take(n_src), take(n_src)
    wg_ref, wu_ref, wd_ref = take(3)
    e_refs, y_refs = take(n_src), take(n_src)
    sems, = take(1)
    step = pl.program_id(0)
    steps = 2 * slots_dev
    half, hidden = ha[0].shape
    toks = 2 * half
    blocks = hidden // 128
    pitch = 16
    unroll = 8

    def copies(srcs, i, b):
        return [pltpu.make_async_copy(src.at[i], dst.at[b], sems.at[n, b])
                for n, (src, dst) in enumerate(zip(srcs, (wg_ref, wu_ref, wd_ref)))]

    def fetch(i):
        @pl.when(i < slots_dev)
        def _():
            for c in copies(own, i, i % depth):
                c.start()

        @pl.when((i >= slots_dev) & (i < steps))
        def _():
            for c in copies(sib, i - slots_dev, i % depth):
                c.start()

    @pl.when(step == 0)
    def _():
        for i in range(depth - 1):
            fetch(jnp.int32(i))
        for y_ref in y_refs:
            y_ref[...] = jnp.zeros_like(y_ref)

    fetch(step + depth - 1)
    buf = step % depth
    for c in copies(own, 0, buf):
        c.wait()
    row_of = lax.broadcasted_iota(jnp.int32, (steps, toks), 0)
    count = [c[step] for c in counts]
    most = count[0] if n_src == 1 else jnp.maximum(count[0], count[1])
    pos = [jnp.sum(jnp.where(row_of == step, r[...], 0.0), axis=0, keepdims=True) for r in slot_refs]
    gate = [jnp.sum(jnp.where(row_of == step, r[...], 0.0), axis=0, keepdims=True) for r in gate_refs]
    low = 0
    for rows in classes:
        @pl.when((most > low) & (most <= rows))
        def _(rows=rows):
            xs, gcols = [], []
            for q in range(n_src):
                hit = lax.broadcasted_iota(jnp.int32, (rows, toks), 0).astype(F32) == pos[q]
                pick = jnp.where(hit, 1.0, 0.0).astype(BF16)
                gcols.append(jnp.sum(jnp.where(hit, gate[q], 0.0), axis=1, keepdims=True))
                xs.append((jnp.dot(pick[:, :half], ha[q][...], preferred_element_type=F32)
                           + jnp.dot(pick[:, half:], hb[q][...], preferred_element_type=F32)).astype(BF16))
            x = xs[0] if n_src == 1 else jnp.concatenate(xs, axis=0)
            gate_proj = jnp.dot(x, wg_ref[buf], preferred_element_type=F32)
            up_proj = jnp.dot(x, wu_ref[buf], preferred_element_type=F32)
            act = (jax.nn.silu(gate_proj) * up_proj).astype(BF16)
            out = jnp.dot(act, wd_ref[buf], preferred_element_type=F32).astype(BF16).astype(F32)
            for q in range(n_src):
                part = out[q * rows:(q + 1) * rows] * gcols[q]
                for j in range(blocks):
                    e_refs[q][pl.ds(j, rows, stride=pitch), :] = part[:, j * 128:(j + 1) * 128]

        low = rows

    for q in range(n_src):
        y_ref, e_ref, list_ref = y_refs[q], e_refs[q], lists[q]

        def scatter(i, carry):
            spots, sums = [], []
            for u in range(unroll):
                r = i * unroll + u
                spot = pl.ds(pl.multiple_of(list_ref[step, r] * pitch, pitch), pitch)
                row = pl.ds(pl.multiple_of(r * pitch, pitch), pitch)
                spots.append(spot)
                sums.append(y_ref[spot, :] + e_ref[row, :])
            for spot, v in zip(spots, sums):
                y_ref[spot, :] = v
            return carry

        lax.fori_loop(0, (count[q] + unroll - 1) // unroll, scatter, 0)

    @pl.when(step == steps - 1)
    def _():
        group = 64

        def unpack(i, carry):
            to = pl.ds(pl.multiple_of(i * group, group), group)
            for q in range(n_src):
                for ref, start in ((ya[q], 0), (yb[q], half)):
                    for j in range(blocks):
                        ref[to, j * 128:(j + 1) * 128] = y_refs[q][pl.ds((start + i * group) * pitch + j, group, stride=pitch), :]
            return carry

        lax.fori_loop(0, half // group, unpack, 0)


def expert_call(sources, own, sib, dep, local_max):
    n_src = len(sources)
    lists, counts, has, hbs, slots, gates = zip(*sources)
    half, hidden = has[0].shape
    slots_dev, _, ff = own[0].shape
    depth = 4 if n_src == 1 else 3
    classes = tuple(c for c in CLASSES if c < local_max) + (local_max,)
    whole = pl.BlockSpec((half, hidden), lambda s: (0, 0), pipeline_mode=pl.Buffered(1))
    table = pl.BlockSpec(slots[0].shape, lambda s: (0, 0), pipeline_mode=pl.Buffered(1))
    smem = pl.BlockSpec(memory_space=pltpu.SMEM)
    hbm = pl.BlockSpec(memory_space=pl.ANY)
    out = jax.ShapeDtypeStruct((half, hidden), F32)
    got = pl.pallas_call(
        functools.partial(expert_kernel, n_src, classes, slots_dev, depth),
        grid=(2 * slots_dev,),
        out_shape=(out,) * (2 * n_src),
        in_specs=[smem] * (2 * n_src) + [whole] * (2 * n_src) + [table] * (2 * n_src) + [hbm] * 7,
        out_specs=(whole,) * (2 * n_src),
        scratch_shapes=[pltpu.VMEM((depth, hidden, ff), BF16), pltpu.VMEM((depth, hidden, ff), BF16), pltpu.VMEM((depth, ff, hidden), BF16)]
        + [pltpu.VMEM((local_max * 16, 128), F32)] * n_src + [pltpu.VMEM(((2 * half + 8) * 16, 128), F32)] * n_src
        + [pltpu.SemaphoreType.DMA((3, depth))],
        compiler_params=pltpu.CompilerParams(dimension_semantics=("arbitrary",), vmem_limit_bytes=62 * 1024 * 1024),
        cost_estimate=pl.CostEstimate(flops=1_000_000, transcendentals=0,
                                      bytes_accessed=2 * slots_dev * 3 * hidden * ff * 2),
        name="experts",
    )(*lists, *counts, *has, *hbs, *slots, *gates, *own, *sib, dep)
    return got[:n_src], got[n_src:]


def solution(mesh):
    group_size = mesh.shape['ep']
    cores = 2
    right = [(i, (i + cores) % group_size) for i in range(group_size)]
    left = [(i, (i - cores) % group_size) for i in range(group_size)]
    far = [(i, (i + group_size // 2) % group_size) for i in range(group_size)]
    sibling = [(i, i ^ 1) for i in range(group_size)]

    def block(hidden_in, topk_idx, norm_gain, w_router, w_sgate, s_gate, s_up, s_down, w_gate, w_up, w_down):
        tok_dev, _ = hidden_in.shape
        top_k = topk_idx.shape[1]
        experts = w_router.shape[1]
        slots_dev = w_gate.shape[0]
        half = tok_dev // 2
        capacity = (5 * tok_dev * group_size * top_k + 4 * experts - 1) // (4 * experts)
        local_max = (2 * tok_dev * top_k + experts - 1) // experts
        me = lax.axis_index('ep')

        def go_right(v):
            return lax.ppermute(v, 'ep', right)

        def go_left(v):
            return lax.ppermute(v, 'ep', left)

        chip, core = me // cores, me % cores

        def after(v, *deps):
            return lax.optimization_barrier((v,) + deps)[0]

        ha, hb = norm_call(hidden_in, norm_gain)
        ha_r1, hb_l1 = go_right(ha), go_left(hb)

        logits = jnp.concatenate([jnp.dot(h, w_router, preferred_element_type=F32) for h in (ha, hb)], axis=0)
        router_probs = jax.nn.softmax(logits, axis=-1)
        chosen = topk_idx[:, :, None] == jnp.arange(experts)[None, None, :]
        gate_vals = jnp.sum(jnp.where(chosen, router_probs[:, None, :], 0.0), axis=-1)
        pad = (-2 * top_k) % 8
        table = jnp.concatenate([topk_idx.T.astype(F32), gate_vals.T, jnp.zeros((pad, tok_dev), F32)], axis=0)
        sib_table = lax.ppermute(table, 'ep', sibling)
        own_w = (w_gate, w_up, w_down)
        sib_w = tuple(lax.ppermute(after(w, sib_table), 'ep', sibling) for w in own_w)
        pair = jnp.stack([table, sib_table])
        t_r1, t_l1 = go_right(pair), go_left(pair)
        t_far = lax.ppermute(pair, 'ep', far)

        ha_r2, hb_l2 = go_right(ha_r1), go_left(hb_l1)
        hb_r1, ha_l1 = go_right(after(hb, ha_r1)), go_left(after(ha, hb_l1))

        steps = jnp.arange(group_size // cores)
        rel = cores * ((chip + steps) % (group_size // cores))
        ids = jnp.concatenate([jnp.stack([rel + core, rel + 1 - core], axis=1).reshape(-1), jnp.stack([chip, core])]).astype(jnp.int32)
        slot, gate, lists, kept = route_call(ids, table, sib_table, t_l1, t_far, t_r1, top_k, slots_dev, capacity, local_max)
        lists = lists[:, :, 0, :]
        kept = kept[:, :, 0].astype(jnp.int32)

        def source(j, part_a, part_b):
            return lists[j], kept[j], part_a, part_b, slot[j], gate[j]

        (y2a,), (y2b,) = expert_call([source(2, ha_r2, hb_l2)], own_w, sib_w, ha, local_max)
        p_ra, p_lb = go_right(y2a), go_left(y2b)
        (y1a, y3a), (y1b, y3b) = expert_call([source(1, ha_l1, hb_l1), source(3, ha_r1, hb_r1)], own_w, sib_w, y2a, local_max)
        d_b, d_a = go_right(y1b), go_left(y3a)
        (y0a,), (y0b,) = expert_call([source(0, ha, hb)], own_w, sib_w, y3a, local_max)
        p_ra, p_lb = after(p_ra, y0a), after(p_lb, y0b)
        z_a, z_b = go_right(y1a + p_ra), go_left(y3b + p_lb)
        base = []
        for i, (h, y0) in enumerate(((ha, y0a), (hb, y0b))):
            shared_val = shared_expert(after(h, y0a), w_sgate, s_gate, s_up, s_down)
            base.append(hidden_in[i * half:(i + 1) * half].astype(F32) + shared_val + y0)
        return final_call(base[0] + d_a, base[1] + d_b, z_a, z_b)

    row_spec = P(('dp', 'ep'), None)
    full_spec = P(None, None)
    slot_spec = P('ep', None, None)
    in_specs = (row_spec, row_spec, P(None), full_spec, full_spec, full_spec, full_spec, full_spec,
                slot_spec, slot_spec, slot_spec)
    return jax.shard_map(block, mesh=mesh, in_specs=in_specs, out_specs=row_spec, check_vma=False)
```

profile of v0, /device:TPU:88, one launch (start us, length us, event | category | flops | bytes accessed | tf_op | source)
XLA Modules:
  0.0 369.3 jit_solution(8900024855123127865)
XLA Ops:
  0.0 1.3 reshape.139.gain_ref
  1.3 4.6 %norm.1 = (bf16[512,1536]{1,0:T(8,128)(2,1)}, bf16[512,1536]{1,0:T(8,128)(2,1)}) custom-call(bf16[2,512,1536]{2,1,0:T(8,128)(2,1)} %bitcast.54, bf16[1,1536]{1,0:T(2,128)(2,1)} %reshape.139.gain_ref), custom_call_target="tpu_custom_call" | custom-call | flops 6291456 | bytes 6291456 | tf_op jit(solution)/shard_map/norm/pallas_call | solution.py:28
  6.0 2.1 fusion.13
  8.1 2.0 fusion.14
  10.3 0.2 select_reduce_fusion
  10.8 1.2 collective-permute-done.sib_ref
  12.0 0.2 collective-permute-start.4
  12.1 0.4 collective-permute-start.5
  12.5 0.2 collective-permute-start.6
  12.7 3.3 collective-permute-start.1
  16.0 0.5 collective-permute-start.2
  16.5 5.6 %collective-permute-done.1.next_ref = f32[2,16,1024]{2,1,0:T(8,128)S(1)} collective-permute-done((f32[2,16,1024]{2,1,0:T(8,128)S(1)}, f32[2,16,1024]{2,1,0:T(8,128)S(1)}, u32[]{:S(2)}, u32[]{:S(2)}) %collective-permute-start.1) | collective-permute-done | bytes 131104 | tf_op jit(solution)/shard_map/ppermute | solution.py:313
  22.1 0.9 collective-permute-done.2.far_ref
  23.0 1.1 collective-permute-start.9
  24.1 6.0 %collective-permute-done.3.prev_ref = f32[2,16,1024]{2,1,0:T(8,128)S(1)} collective-permute-done((f32[2,16,1024]{2,1,0:T(8,128)S(1)}, f32[2,16,1024]{2,1,0:T(8,128)S(1)}, u32[]{:S(2)}, u32[]{:S(2)}) %collective-permute-start.3) | collective-permute-done | bytes 131104 | tf_op jit(solution)/shard_map/ppermute | solution.py:310
  30.1 2.0 collective-permute-start.7
  32.2 30.6 %collective-permute-done.9.refs_5_ = bf16[512,1536]{1,0:T(8,128)(2,1)} collective-permute-done((bf16[512,1536]{1,0:T(8,128)(2,1)S(1)}, bf16[512,1536]{1,0:T(8,128)(2,1)}, u32[]{:S(2)}, u32[]{:S(2)}) %collective-permute-start.9) | collective-permute-done | bytes 1572896 | tf_op jit(solution)/shard_map/ppermute | solution.py:310
  62.8 1.5 collective-permute-done.7.refs_6_
  64.3 2.5 collective-permute-start.12
  66.9 0.6 pad_add_fusion.1.ids_ref
  67.5 11.2 %route.1 = (f32[4,16,1024]{2,1,0:T(8,128)}, f32[4,16,1024]{2,1,0:T(8,128)}, s32[4,16,8,192]{3,2,1,0:T(8,128)}, f32[4,16,128]{2,1,0:T(8,128)}) custom-call(s32[10]{0:T(128)} %pad_add_fusion.1.ids_ref, f32[16,1024]{1,0:T(8,128)} %copy-done.8, f32[16,1024]{1,0:T(8,128)} %copy-done.9, f32[2,16,1024]{2,1,0:T(8,128)} %copy-done.10, f32[2,16,1024]{2,1,0:T(8,128)} %copy-done.11, ...), custom_call_target="tpu_custom_call" | custom-call | flops 1000000 | bytes 2000000 | tf_op jit(solution)/shard_map/route/pallas_call | solution.py:140
  78.7 20.8 %collective-permute-done.11.refs_2_ = bf16[512,1536]{1,0:T(8,128)(2,1)} collective-permute-done((bf16[512,1536]{1,0:T(8,128)(2,1)}, bf16[512,1536]{1,0:T(8,128)(2,1)}, u32[]{:S(2)}, u32[]{:S(2)}) %collective-permute-start.11) | collective-permute-done | bytes 1572896 | tf_op jit(solution)/shard_map/ppermute | solution.py:310
  99.5 3.2 collective-permute-start.8
  102.7 0.8 slice_convert_fusion
  103.5 1.2 copy.24
  104.7 0.7 slice_reduce_fusion.3
  105.4 0.6 slice_bitcast_fusion.11
  106.1 1.7 slice_bitcast_fusion.6
  107.7 1.7 slice_bitcast_fusion.7
  109.4 42.3 %experts.3 = (f32[512,1536]{1,0:T(8,128)}, f32[512,1536]{1,0:T(8,128)}) custom-call(s32[16,192]{1,0:T(8,128)} %get-tuple-element.56.refs_0_, s32[16]{0:T(128)} %get-tuple-element.52.refs_1_, bf16[512,1536]{1,0:T(8,128)(2,1)} %collective-permute-done.11.refs_2_, bf16[512,1536]{1,0:T(8,128)(2,1)} %collective-permute-done.12.refs_3_, ...), custom_call_target="tpu_custom_call" | custom-call | flops 1000000 | bytes 75497472 | tf_op jit(solution)/shard_map/experts/pallas_call | solution.py:274
  151.7 4.6 %collective-permute-start.17 = (f32[512,1536]{1,0:T(8,128)}, f32[512,1536]{1,0:T(8,128)}, u32[]{:S(2)}, u32[]{:S(2)}) collective-permute-start(f32[512,1536]{1,0:T(8,128)} %get-tuple-element.49), channel_id=1, source_target_pairs={{0,6},{1,7},{2,0},{3,1},{4,2},{5,3},{6,4},{7,5},{8,14},{9,15},{10,... | collective-permute-start | bytes 9437192 | tf_op jit(solution)/shard_map/ppermute | solution.py:313
  156.3 63.6 %experts.4 = (f32[512,1536]{1,0:T(8,128)}, f32[512,1536]{1,0:T(8,128)}, f32[512,1536]{1,0:T(8,128)}, f32[512,1536]{1,0:T(8,128)}) custom-call(s32[16,192]{1,0:T(8,128)} %get-tuple-element.58.refs_0_, s32[16,192]{1,0:T(8,128)} %get-tuple-element.57.refs_1_, s32[16]{0:T(128)} %get-tuple-element.54.refs_2_, s32[16]{0:T(128)} %get-tuple-element.53.refs_3_, ...), custom_call_target="tpu_custom_call" | custom-call | flops 1000000 | bytes 75497472 | tf_op jit(solution)/shard_map/experts/pallas_call | solution.py:274
  219.8 4.7 %collective-permute-start.14 = (f32[512,1536]{1,0:T(8,128)}, f32[512,1536]{1,0:T(8,128)}, u32[]{:S(2)}, u32[]{:S(2)}) collective-permute-start(f32[512,1536]{1,0:T(8,128)} %get-tuple-element.45), channel_id=1, source_target_pairs={{0,2},{1,3},{2,4},{3,5},{4,6},{5,7},{6,0},{7,1},{8,10},{9,11},{10,... | collective-permute-start | bytes 9437192 | tf_op jit(solution)/shard_map/ppermute | solution.py:310
  224.5 6.9 %collective-permute-start.13 = (f32[512,1536]{1,0:T(8,128)}, f32[512,1536]{1,0:T(8,128)}, u32[]{:S(2)}, u32[]{:S(2)}) collective-permute-start(f32[512,1536]{1,0:T(8,128)} %get-tuple-element.40.refs_12_), channel_id=1, source_target_pairs={{0,6},{1,7},{2,0},{3,1},{4,2},{5,3},{6,4},{7,5},{8,14},{9,15},{10,... | collective-permute-start | bytes 9437192 | tf_op jit(solution)/shard_map/ppermute | solution.py:313
  231.5 43.2 %experts.5 = (f32[512,1536]{1,0:T(8,128)}, f32[512,1536]{1,0:T(8,128)}) custom-call(s32[16,192]{1,0:T(8,128)} %get-tuple-element.55.refs_0_, s32[16]{0:T(128)} %get-tuple-element.51.refs_1_, bf16[512,1536]{1,0:T(8,128)(2,1)} %get-tuple-element.42.refs_12_.refs_2_, bf16[512,1536]{1,0:T(8,128)(2,1)} %get-tuple-element.43.refs_3_, ...), custom_call_target="tpu_custom_call" | custom-call | flops 1000000 | bytes 75497472 | tf_op jit(solution)/shard_map/experts/pallas_call | solution.py:274
  274.7 2.0 fusion.17
  276.7 0.5 fusion.15
  277.3 5.2 %fusion.18 = f32[512,1024]{1,0:T(8,128)} fusion(bf16[512,1536]{1,0:T(8,128)(2,1)S(1)} %copy-done.5, bf16[1536,1024]{1,0:T(8,128)(2,1)} %param.16), kind=kOutput, calls=%fused_computation.55 | convolution fusion | flops 1610612736 | bytes 6815744 | tf_op jit(solution)/shard_map/dot_general | solution.py:63
  282.5 4.3 %add.119 = f32[512,1536]{1,0:T(8,128)} add(f32[512,1536]{1,0:T(8,128)S(1)} %copy-done.7, f32[512,1536]{1,0:T(8,128)} %collective-permute-done.17) | non-fusion elementwise | flops 786432 | bytes 9437184 | tf_op jit(solution)/shard_map/add | solution.py:355
  286.9 4.3 %add.118 = f32[512,1536]{1,0:T(8,128)} add(f32[512,1536]{1,0:T(8,128)S(1)} %copy-done.6, f32[512,1536]{1,0:T(8,128)} %collective-permute-done.15) | non-fusion elementwise | flops 786432 | bytes 9437184 | tf_op jit(solution)/shard_map/add | solution.py:355
  291.1 2.0 collective-permute-start.16
  293.2 3.2 fusion.16
  296.3 4.1 %collective-permute-done.14 = f32[512,1536]{1,0:T(8,128)} collective-permute-done((f32[512,1536]{1,0:T(8,128)}, f32[512,1536]{1,0:T(8,128)}, u32[]{:S(2)}, u32[]{:S(2)}) %collective-permute-start.14) | collective-permute-done | bytes 3145760 | tf_op jit(solution)/shard_map/ppermute | solution.py:310
  300.4 11.5 %fusion.3.base_b = f32[512,1536]{1,0:T(8,128)} fusion(f32[512,1536]{1,0:T(8,128)} %collective-permute-done.14, f32[512,1536]{1,0:T(8,128)} %get-tuple-element.44, bf16[1024,1536]{1,0:T(8,128)(2,1)} %param.18, f32[512]{0:T(512)S(1)} %add_divide_fusion, bf16[1024,1536]{1,0:T(8,128)(2,1)} %param.11, f32[512,1024]{1,0:T(8,128)} %fusion.18, ...), kind=kOutput, calls=%fused_computation.5 | convolution fusion | flops 3228303360 | bytes 20973568 | tf_op jit(solution)/shard_map/dot_general | solution.py:65
  312.0 10.9 %fusion.5.base_a = f32[512,1536]{1,0:T(8,128)} fusion(f32[512,1536]{1,0:T(8,128)} %collective-permute-done.13, f32[512,1536]{1,0:T(8,128)} %get-tuple-element.41, bf16[1024,1536]{1,0:T(8,128)(2,1)} %param.18, f32[512]{0:T(512)S(1)} %add_divide_fusion.1, bf16[1024,1536]{1,0:T(8,128)(2,1)} %param.11, f32[512,1024]{1,0:T(8,128)} %fusion.16, ...), kind=kOutput, calls=%fused_computation.7 | convolution fusion | flops 3228303360 | bytes 20973568 | tf_op jit(solution)/shard_map/dot_general | solution.py:65
  322.8 39.5 %collective-permute-done.18.zb_ref = f32[512,1536]{1,0:T(8,128)} collective-permute-done((f32[512,1536]{1,0:T(8,128)}, f32[512,1536]{1,0:T(8,128)}, u32[]{:S(2)}, u32[]{:S(2)}) %collective-permute-start.18) | collective-permute-done | bytes 3145760 | tf_op jit(solution)/shard_map/ppermute | solution.py:313
  362.3 0.4 collective-permute-done.16.za_ref
  362.8 6.5 %final.1 = bf16[2,512,1536]{2,1,0:T(8,128)(2,1)} custom-call(f32[512,1536]{1,0:T(8,128)} %fusion.5.base_a, f32[512,1536]{1,0:T(8,128)} %fusion.3.base_b, f32[512,1536]{1,0:T(8,128)} %collective-permute-done.16.za_ref, f32[512,1536]{1,0:T(8,128)} %collective-permute-done.18.zb_ref), custom_call_target="tpu_custom_call" | custom-call | flops 1572864 | bytes 15728640 | tf_op jit(solution)/shard_map/final/pallas_call | solution.py:49
  (61 shorter events, 0.8 us)
Async XLA Ops:
  0.0 6.0 %copy-start = (bf16[1536,64]{0,1:T(8,128)(2,1)S(1)}, bf16[1536,64]{0,1:T(8,128)(2,1)}, u32[]{:S(2)}) copy-start(bf16[1536,64]{0,1:T(8,128)(2,1)} %param.14) | copy-start | bytes 589828
  5.9 4.3 %copy-start.13 = (s32[1024,6]{0,1:T(8,128)S(1)}, s32[1024,6]{0,1:T(8,128)}, u32[]{:S(2)}) copy-start(s32[1024,6]{0,1:T(8,128)} %param.12) | copy-start | bytes 73732
  6.0 17.0 %copy-start.2 = (bf16[512,1536]{1,0:T(8,128)(2,1)S(1)}, bf16[512,1536]{1,0:T(8,128)(2,1)}, u32[]{:S(2)}) copy-start(bf16[512,1536]{1,0:T(8,128)(2,1)} %get-tuple-element.42.refs_12_.refs_2_) | copy-start | bytes 4718596
  6.0 24.2 %copy-start.4 = (bf16[512,1536]{1,0:T(8,128)(2,1)S(1)}, bf16[512,1536]{1,0:T(8,128)(2,1)}, u32[]{:S(2)}) copy-start(bf16[512,1536]{1,0:T(8,128)(2,1)} %get-tuple-element.43.refs_3_) | copy-start | bytes 4718596
  10.7 56.8 %copy-start.8 = (f32[16,1024]{1,0:T(8,128)}, f32[16,1024]{1,0:T(8,128)S(1)}, u32[]{:S(2)}) copy-start(f32[16,1024]{1,0:T(8,128)S(1)} %maximum_maximum_fusion.own_ref) | copy-start | bytes 196612
  10.7 1.3 collective-permute-start
  12.0 55.5 %copy-start.9 = (f32[16,1024]{1,0:T(8,128)}, f32[16,1024]{1,0:T(8,128)S(1)}, u32[]{:S(2)}) copy-start(f32[16,1024]{1,0:T(8,128)S(1)} %collective-permute-done.sib_ref) | copy-start | bytes 196612
  12.0 97.4 %collective-permute-start.4 = (bf16[8,1536,512]{2,1,0:T(8,128)(2,1)}, bf16[8,1536,512]{2,1,0:T(8,128)(2,1)}, u32[]{:S(2)}, u32[]{:S(2)}) collective-permute-start(bf16[8,1536,512]{2,1,0:T(8,128)(2,1)} %refs_6_.3), channel_id=1, source_target_pairs={{0,1},{1,0},{2,3},{3,2},{4,5},{5,4},{6,7},{7,6},{8,9},{9,8},{10,11... | collective-permute-start | bytes 37748744 | tf_op jit(solution)/shard_map/ppermute | solution.py:331
  12.1 97.3 %collective-permute-start.5 = (bf16[8,1536,512]{2,1,0:T(8,128)(2,1)}, bf16[8,1536,512]{2,1,0:T(8,128)(2,1)}, u32[]{:S(2)}, u32[]{:S(2)}) collective-permute-start(bf16[8,1536,512]{2,1,0:T(8,128)(2,1)} %refs_7_.3), channel_id=1, source_target_pairs={{0,1},{1,0},{2,3},{3,2},{4,5},{5,4},{6,7},{7,6},{8,9},{9,8},{10,11... | collective-permute-start | bytes 37748744 | tf_op jit(solution)/shard_map/ppermute | solution.py:331
  12.5 96.9 %collective-permute-start.6 = (bf16[8,512,1536]{2,1,0:T(8,128)(2,1)}, bf16[8,512,1536]{2,1,0:T(8,128)(2,1)}, u32[]{:S(2)}, u32[]{:S(2)}) collective-permute-start(bf16[8,512,1536]{2,1,0:T(8,128)(2,1)} %refs_8_.3), channel_id=1, source_target_pairs={{0,1},{1,0},{2,3},{3,2},{4,5},{5,4},{6,7},{7,6},{8,9},{9,8},{10,11... | collective-permute-start | bytes 37748744 | tf_op jit(solution)/shard_map/ppermute | solution.py:331
  12.7 9.3 %collective-permute-start.1 = (f32[2,16,1024]{2,1,0:T(8,128)S(1)}, f32[2,16,1024]{2,1,0:T(8,128)S(1)}, u32[]{:S(2)}, u32[]{:S(2)}) collective-permute-start(f32[2,16,1024]{2,1,0:T(8,128)S(1)} %pad_maximum_fusion.1), channel_id=1, source_target_pairs={{0,6},{1,7},{2,0},{3,1},{4,2},{5,3},{6,4},{7,5},{8,14},{9,15},{10,... | collective-permute-start | bytes 393224 | tf_op jit(solution)/shard_map/ppermute | solution.py:313
  16.0 7.0 %collective-permute-start.2 = (f32[2,16,1024]{2,1,0:T(8,128)S(1)}, f32[2,16,1024]{2,1,0:T(8,128)S(1)}, u32[]{:S(2)}, u32[]{:S(2)}) collective-permute-start(f32[2,16,1024]{2,1,0:T(8,128)S(1)} %pad_maximum_fusion.1), channel_id=1, source_target_pairs={{0,4},{1,5},{2,6},{3,7},{4,0},{5,1},{6,2},{7,3},{8,12},{9,13},{10,... | collective-permute-start | bytes 393224 | tf_op jit(solution)/shard_map/ppermute | solution.py:334
  22.1 45.4 %copy-start.10 = (f32[2,16,1024]{2,1,0:T(8,128)}, f32[2,16,1024]{2,1,0:T(8,128)S(1)}, u32[]{:S(2)}) copy-start(f32[2,16,1024]{2,1,0:T(8,128)S(1)} %collective-permute-done.1.next_ref) | copy-start | bytes 393220
  22.1 8.0 %collective-permute-start.3 = (f32[2,16,1024]{2,1,0:T(8,128)S(1)}, f32[2,16,1024]{2,1,0:T(8,128)S(1)}, u32[]{:S(2)}, u32[]{:S(2)}) collective-permute-start(f32[2,16,1024]{2,1,0:T(8,128)S(1)} %pad_maximum_fusion.1), channel_id=1, source_target_pairs={{0,2},{1,3},{2,4},{3,5},{4,6},{5,7},{6,0},{7,1},{8,10},{9,11},{10,... | collective-permute-start | bytes 393224 | tf_op jit(solution)/shard_map/ppermute | solution.py:310
  23.0 44.5 %copy-start.11 = (f32[2,16,1024]{2,1,0:T(8,128)}, f32[2,16,1024]{2,1,0:T(8,128)S(1)}, u32[]{:S(2)}) copy-start(f32[2,16,1024]{2,1,0:T(8,128)S(1)} %collective-permute-done.2.far_ref) | copy-start | bytes 393220
  23.0 39.8 %collective-permute-start.9 = (bf16[512,1536]{1,0:T(8,128)(2,1)S(1)}, bf16[512,1536]{1,0:T(8,128)(2,1)}, u32[]{:S(2)}, u32[]{:S(2)}) collective-permute-start(bf16[512,1536]{1,0:T(8,128)(2,1)S(1)} %copy-done.2), channel_id=1, source_target_pairs={{0,2},{1,3},{2,4},{3,5},{4,6},{5,7},{6,0},{7,1},{8,10},{9,11},{10,... | collective-permute-start | bytes 4718600 | tf_op jit(solution)/shard_map/ppermute | solution.py:310
  30.1 37.4 %copy-start.12 = (f32[2,16,1024]{2,1,0:T(8,128)}, f32[2,16,1024]{2,1,0:T(8,128)S(1)}, u32[]{:S(2)}) copy-start(f32[2,16,1024]{2,1,0:T(8,128)S(1)} %collective-permute-done.3.prev_ref) | copy-start | bytes 393220
  30.1 34.1 %collective-permute-start.7 = (bf16[512,1536]{1,0:T(8,128)(2,1)S(1)}, bf16[512,1536]{1,0:T(8,128)(2,1)}, u32[]{:S(2)}, u32[]{:S(2)}) collective-permute-start(bf16[512,1536]{1,0:T(8,128)(2,1)S(1)} %copy-done.4), channel_id=1, source_target_pairs={{0,6},{1,7},{2,0},{3,1},{4,2},{5,3},{6,4},{7,5},{8,14},{9,15},{10,... | collective-permute-start | bytes 4718600 | tf_op jit(solution)/shard_map/ppermute | solution.py:313
  62.7 36.7 %collective-permute-start.11 = (bf16[512,1536]{1,0:T(8,128)(2,1)}, bf16[512,1536]{1,0:T(8,128)(2,1)}, u32[]{:S(2)}, u32[]{:S(2)}) collective-permute-start(bf16[512,1536]{1,0:T(8,128)(2,1)} %collective-permute-done.9.refs_5_), channel_id=1, source_target_pairs={{0,2},{1,3},{2,4},{3,5},{4,6},{5,7},{6,0},{7,1},{8,10},{9,11},{10,... | collective-permute-start | bytes 4718600 | tf_op jit(solution)/shard_map/ppermute | solution.py:310
  64.3 35.2 %collective-permute-start.12 = (bf16[512,1536]{1,0:T(8,128)(2,1)}, bf16[512,1536]{1,0:T(8,128)(2,1)}, u32[]{:S(2)}, u32[]{:S(2)}) collective-permute-start(bf16[512,1536]{1,0:T(8,128)(2,1)} %collective-permute-done.7.refs_6_), channel_id=1, source_target_pairs={{0,6},{1,7},{2,0},{3,1},{4,2},{5,3},{6,4},{7,5},{8,14},{9,15},{10,... | collective-permute-start | bytes 4718600 | tf_op jit(solution)/shard_map/ppermute | solution.py:313
  99.5 56.8 %collective-permute-start.10 = (bf16[512,1536]{1,0:T(8,128)(2,1)}, bf16[512,1536]{1,0:T(8,128)(2,1)}, u32[]{:S(2)}, u32[]{:S(2)}) collective-permute-start(bf16[512,1536]{1,0:T(8,128)(2,1)} %get-tuple-element.43.refs_3_), channel_id=1, source_target_pairs={{0,2},{1,3},{2,4},{3,5},{4,6},{5,7},{6,0},{7,1},{8,10},{9,11},{10,... | collective-permute-start | bytes 4718600 | tf_op jit(solution)/shard_map/ppermute | solution.py:310
  99.5 56.8 %collective-permute-start.8 = (bf16[512,1536]{1,0:T(8,128)(2,1)S(1)}, bf16[512,1536]{1,0:T(8,128)(2,1)}, u32[]{:S(2)}, u32[]{:S(2)}) collective-permute-start(bf16[512,1536]{1,0:T(8,128)(2,1)S(1)} %copy-done.2), channel_id=1, source_target_pairs={{0,6},{1,7},{2,0},{3,1},{4,2},{5,3},{6,4},{7,5},{8,14},{9,15},{10,... | collective-permute-start | bytes 4718600 | tf_op jit(solution)/shard_map/ppermute | solution.py:313
  151.7 130.8 %collective-permute-start.17 = (f32[512,1536]{1,0:T(8,128)}, f32[512,1536]{1,0:T(8,128)}, u32[]{:S(2)}, u32[]{:S(2)}) collective-permute-start(f32[512,1536]{1,0:T(8,128)} %get-tuple-element.49), channel_id=1, source_target_pairs={{0,6},{1,7},{2,0},{3,1},{4,2},{5,3},{6,4},{7,5},{8,14},{9,15},{10,... | collective-permute-start | bytes 9437192 | tf_op jit(solution)/shard_map/ppermute | solution.py:313
  156.2 130.6 %collective-permute-start.15 = (f32[512,1536]{1,0:T(8,128)}, f32[512,1536]{1,0:T(8,128)}, u32[]{:S(2)}, u32[]{:S(2)}) collective-permute-start(f32[512,1536]{1,0:T(8,128)} %get-tuple-element.39.refs_18_), channel_id=1, source_target_pairs={{0,2},{1,3},{2,4},{3,5},{4,6},{5,7},{6,0},{7,1},{8,10},{9,11},{10,... | collective-permute-start | bytes 9437192 | tf_op jit(solution)/shard_map/ppermute | solution.py:310
  219.8 80.6 %collective-permute-start.14 = (f32[512,1536]{1,0:T(8,128)}, f32[512,1536]{1,0:T(8,128)}, u32[]{:S(2)}, u32[]{:S(2)}) collective-permute-start(f32[512,1536]{1,0:T(8,128)} %get-tuple-element.45), channel_id=1, source_target_pairs={{0,2},{1,3},{2,4},{3,5},{4,6},{5,7},{6,0},{7,1},{8,10},{9,11},{10,... | collective-permute-start | bytes 9437192 | tf_op jit(solution)/shard_map/ppermute | solution.py:310
  224.5 87.4 %collective-permute-start.13 = (f32[512,1536]{1,0:T(8,128)}, f32[512,1536]{1,0:T(8,128)}, u32[]{:S(2)}, u32[]{:S(2)}) collective-permute-start(f32[512,1536]{1,0:T(8,128)} %get-tuple-element.40.refs_12_), channel_id=1, source_target_pairs={{0,6},{1,7},{2,0},{3,1},{4,2},{5,3},{6,4},{7,5},{8,14},{9,15},{10,... | collective-permute-start | bytes 9437192 | tf_op jit(solution)/shard_map/ppermute | solution.py:313
  231.5 43.2 %copy-start.14 = (bf16[1536,1]{0,1:T(2,128)(2,1)S(1)}, bf16[1536,1]{0,1:T(2,128)(2,1)}, u32[]{:S(2)}) copy-start(bf16[1536,1]{0,1:T(2,128)(2,1)} %param.15) | copy-start | bytes 9220
  231.5 45.3 %copy-start.3 = (bf16[512,1536]{1,0:T(8,128)(2,1)S(1)}, bf16[512,1536]{1,0:T(8,128)(2,1)}, u32[]{:S(2)}) copy-start(bf16[512,1536]{1,0:T(8,128)(2,1)} %get-tuple-element.42.refs_12_.refs_2_) | copy-start | bytes 4718596
  274.7 2.6 copy-start.5
  277.3 5.3 %copy-start.7 = (f32[512,1536]{1,0:T(8,128)S(1)}, f32[512,1536]{1,0:T(8,128)}, u32[]{:S(2)}) copy-start(f32[512,1536]{1,0:T(8,128)} %get-tuple-element.48) | copy-start | bytes 9437188
  282.5 4.3 %copy-start.6 = (f32[512,1536]{1,0:T(8,128)S(1)}, f32[512,1536]{1,0:T(8,128)}, u32[]{:S(2)}) copy-start(f32[512,1536]{1,0:T(8,128)} %get-tuple-element.46) | copy-start | bytes 9437188
  286.8 75.5 %collective-permute-start.18 = (f32[512,1536]{1,0:T(8,128)}, f32[512,1536]{1,0:T(8,128)}, u32[]{:S(2)}, u32[]{:S(2)}) collective-permute-start(f32[512,1536]{1,0:T(8,128)} %add.119), channel_id=1, source_target_pairs={{0,6},{1,7},{2,0},{3,1},{4,2},{5,3},{6,4},{7,5},{8,14},{9,15},{10,... | collective-permute-start | bytes 9437192 | tf_op jit(solution)/shard_map/ppermute | solution.py:313
  286.8 6.3 %copy-start.15 = (bf16[1536,1024]{1,0:T(8,128)(2,1)S(1)}, bf16[1536,1024]{1,0:T(8,128)(2,1)}, u32[]{:S(2)}) copy-start(bf16[1536,1024]{1,0:T(8,128)(2,1)} %param.16) | copy-start | bytes 9437188
  291.1 71.6 %collective-permute-start.16 = (f32[512,1536]{1,0:T(8,128)}, f32[512,1536]{1,0:T(8,128)}, u32[]{:S(2)}, u32[]{:S(2)}) collective-permute-start(f32[512,1536]{1,0:T(8,128)} %add.118), channel_id=1, source_target_pairs={{0,2},{1,3},{2,4},{3,5},{4,6},{5,7},{6,0},{7,1},{8,10},{9,11},{10,... | collective-permute-start | bytes 9437192 | tf_op jit(solution)/shard_map/ppermute | solution.py:310
  362.8 6.5 %copy-start.1 = (bf16[1536,64]{0,1:T(8,128)(2,1)S(1)}, bf16[1536,64]{0,1:T(8,128)(2,1)}, u32[]{:S(2)}) copy-start(bf16[1536,64]{0,1:T(8,128)(2,1)} %param.14) | copy-start | bytes 589828
where the time goes:
time: 373 us; the launch traced here: 369 us
  Pallas kernels  171 us (46%)
  waiting for transfers between devices  111 us (30%)
  matrix products  37.5 us (10%)
  starting transfers between devices  31.5 us (8%)
  other arithmetic  10.6 us (3%)
  local copies, waits for them, and re-layouts  7.45 us (2%)
    pallas_call x3, Pallas kernels, expert_call(): pl.pallas_call(functools.partial(expert_kernel, n_src, classes, slots_dev...  149 us
    ppermute x7, waiting for transfers between devices, go_right(): return lax.ppermute(v, 'ep', right)  61.9 us
    ppermute x7, waiting for transfers between devices, go_left(): return lax.ppermute(v, 'ep', left)  46.6 us
    ppermute x7, starting transfers between devices, go_left(): return lax.ppermute(v, 'ep', left)  22.5 us
    dot_general x2, matrix products, shared_expert(): shared_val = jnp.dot(shared_act, s_down, preferred_element_type=F32)  22.4 us
    pallas_call x1, Pallas kernels, route_call(): pl.pallas_call(functools.partial(route_kernel, (top_k, slots_dev, capacit...  11.2 us
    add x2, other arithmetic, block(): z_a, z_b = (go_right(y1a + p_ra), go_left(y3b + p_lb))  8.59 us
    dot_general x2, matrix products, shared_expert(): jnp.dot(normed, s_gate, preferred_element_type=F32)  8.42 us
  transfers between devices with their start and end apart: 19, of which 10 were waited for; matrix products, arithmetic and copies ran while one was open for 13% of the time, Pallas kernels for 43%

commit v1 on v0

--- a/solution.py
+++ b/solution.py
@@ -66,34 +66,35 @@
     return jax.nn.sigmoid(jnp.dot(normed, w_sgate, preferred_element_type=F32)) * shared_val
 
 
-def route_kernel(geom, ids_ref, own_ref, sib_ref, next_ref, far_ref, prev_ref, slot_ref, gate_ref, list_ref, count_ref, hot_ref):
+def route_kernel(geom, ids_ref, own_ref, next_ref, far_ref, prev_ref, list_ref, glist_ref, count_ref, slot_ref, gate_ref):
     top_k, slots_dev, capacity, local_max = geom
     toks = own_ref.shape[1]
     slots = 2 * slots_dev
     chip, core = ids_ref[8], ids_ref[9]
-    order = lax.broadcasted_iota(jnp.int32, (slots, 1), 0)
-    slot_id = chip * slots + jnp.where(order < slots_dev, core * slots_dev + order, (1 - core) * slots_dev + order - slots_dev)
-    slot_id = slot_id.astype(F32)
-    tables = []
+
+    def slot_column(like):
+        order = lax.broadcasted_iota(jnp.int32, like, 0)
+        mine = core * slots_dev + order
+        other = (1 - core) * slots_dev + order - slots_dev
+        return (chip * slots + jnp.where(order < slots_dev, mine, other)).astype(F32)
+
+    slot_id = slot_column((slots, 1))
+    lane_id = lax.broadcasted_iota(jnp.int32, (slots, 128), 1).astype(F32)
+    hots, counts = [], []
     for j, ref in enumerate((own_ref, next_ref, far_ref, prev_ref)):
-        pair = (own_ref[...], sib_ref[...]) if j == 0 else (ref[0], ref[1])
-        tables.append(pair)
-    counts = []
-    for j in range(4):
+        table = ref[...]
+        hot = jnp.zeros((slots, toks), F32)
+        gate = jnp.zeros((slots, toks), F32)
+        for k in range(top_k):
+            hit = table[k:k + 1, :] == slot_id
+            hot = hot + jnp.where(hit, 1.0, 0.0)
+            gate = gate + jnp.where(hit, table[top_k + k:top_k + k + 1, :], 0.0)
         for i in range(2):
-            table = tables[j][i]
-            hot = jnp.zeros((slots, toks), F32)
-            gate = jnp.zeros((slots, toks), F32)
-            for k in range(top_k):
-                hit = table[k:k + 1, :] == slot_id
-                hot = hot + jnp.where(hit, 1.0, 0.0)
-                if i == 0:
-                    gate = gate + jnp.where(hit, table[top_k + k:top_k + k + 1, :], 0.0)
-            counts.append(jnp.sum(hot, axis=1, keepdims=True))
-            if i == 0:
-                hot_ref[pl.ds(j * slots, slots), :] = hot
-                gate_ref[j] = gate
-    hot_all = hot_ref[...]
+            row = table[2 * top_k + i:2 * top_k + i + 1, :128]
+            counts.append(jnp.sum(jnp.where(lane_id == slot_id, row, 0.0), axis=1, keepdims=True))
+        hots.append(hot)
+        gate_ref[j] = gate
+    hot_all = jnp.concatenate(hots, axis=0)
     hot_bf = hot_all.astype(BF16)
     tile = 256
     for c in range(toks // tile):
@@ -111,42 +112,47 @@
             if c == 0:
                 count_ref[j] = jnp.broadcast_to(jnp.clip(capacity - lower, 0.0, counts[2 * j]), (slots, 128))
     token = lax.broadcasted_iota(jnp.int32, (8, toks), 1)
-    high, low = token // 32, token % 32
     row8 = lax.broadcasted_iota(jnp.int32, (8, toks), 0)
-    digits = jnp.where(row8 == 0, high, low).astype(F32).astype(BF16)
+    digits = jnp.where(row8 == 0, token // 32, token % 32).astype(F32)
     row_of = lax.broadcasted_iota(jnp.int32, (slots, toks), 0)
     count_row = lax.broadcasted_iota(jnp.int32, (slots, 128), 0)
 
     def lists(e, carry):
         for j in range(4):
             pos = jnp.sum(jnp.where(row_of == e, slot_ref[j], 0.0), axis=0, keepdims=True)
+            gate = jnp.sum(jnp.where(row_of == e, gate_ref[j], 0.0), axis=0, keepdims=True)
+            g1 = gate.astype(BF16).astype(F32)
+            g2 = (gate - g1).astype(BF16).astype(F32)
+            g3 = gate - g1 - g2
+            left = jnp.where(row8 < 2, digits, jnp.where(row8 == 2, g1, jnp.where(row8 == 3, g2, g3))).astype(BF16)
             want = lax.broadcasted_iota(jnp.int32, (local_max, toks), 0).astype(F32)
             pick = jnp.where(want == pos, 1.0, 0.0).astype(BF16)
-            got = lax.dot_general(digits, pick, (((1,), (1,)), ((), ())), preferred_element_type=F32)
+            got = lax.dot_general(left, pick, (((1,), (1,)), ((), ())), preferred_element_type=F32)
             found = 32.0 * got[0:1] + got[1:2]
             held = jnp.sum(jnp.where(count_row == e, count_ref[j], 0.0), axis=0, keepdims=True)[:, 0:1]
             lane = lax.broadcasted_iota(jnp.int32, (1, local_max), 1).astype(F32)
             found = jnp.where(lane < held, found, float(toks)).astype(jnp.int32)
             list_ref[j, e] = jnp.broadcast_to(found, (8, local_max))
+            glist_ref[j, e] = jnp.broadcast_to((got[2:3] + got[3:4]) + got[4:5], (8, local_max))
         return carry
 
     lax.fori_loop(0, slots, lists, 0)
 
 
-def route_call(ids, own, sib, nxt, far, prv, top_k, slots_dev, capacity, local_max):
+def route_call(ids, own, nxt, far, prv, top_k, slots_dev, capacity, local_max):
     toks = own.shape[1]
     slots = 2 * slots_dev
     vmem = pl.BlockSpec(memory_space=pltpu.VMEM)
     return pl.pallas_call(
         functools.partial(route_kernel, (top_k, slots_dev, capacity, local_max)),
-        out_shape=(jax.ShapeDtypeStruct((4, slots, toks), F32), jax.ShapeDtypeStruct((4, slots, toks), F32),
-                   jax.ShapeDtypeStruct((4, slots, 8, local_max), jnp.int32), jax.ShapeDtypeStruct((4, slots, 128), F32)),
-        in_specs=[pl.BlockSpec(memory_space=pltpu.SMEM)] + [vmem] * 5,
-        out_specs=(vmem,) * 4,
-        scratch_shapes=[pltpu.VMEM((4 * slots, toks), F32)],
+        out_shape=(jax.ShapeDtypeStruct((4, slots, 8, local_max), jnp.int32), jax.ShapeDtypeStruct((4, slots, 8, local_max), F32),
+                   jax.ShapeDtypeStruct((4, slots, 128), F32)),
+        in_specs=[pl.BlockSpec(memory_space=pltpu.SMEM)] + [vmem] * 4,
+        out_specs=(vmem,) * 3,
+        scratch_shapes=[pltpu.VMEM((4, slots, toks), F32), pltpu.VMEM((4, slots, toks), F32)],
         cost_estimate=pl.CostEstimate(flops=1_000_000, transcendentals=0, bytes_accessed=2_000_000),
         name="route",
-    )(ids, own, sib, nxt, far, prv)
+    )(ids, own, nxt, far, prv)
 
 
 def expert_kernel(n_src, classes, slots_dev, depth, *refs):
@@ -157,21 +163,20 @@
         del refs[:n]
         return got
 
-    lists, counts = take(n_src), take(n_src)
-    ha, hb, slot_refs, gate_refs = take(n_src), take(n_src), take(n_src), take(n_src)
+    lists, glists, counts = take(n_src), take(n_src), take(n_src)
+    has, hbs = take(n_src), take(n_src)
     own, sib = take(3), take(3)
     take(1)
-    ya, yb = take(n_src), take(n_src)
+    yas, ybs = take(n_src), take(n_src)
     wg_ref, wu_ref, wd_ref = take(3)
-    e_refs, y_refs = take(n_src), take(n_src)
-    sems, = take(1)
+    row_refs, tok_refs, sum_refs = [take(2) for _ in range(n_src)], [take(2) for _ in range(n_src)], [take(2) for _ in range(n_src)]
+    stage_ref, sems, out_sems = take(3)
     step = pl.program_id(0)
     steps = 2 * slots_dev
-    half, hidden = ha[0].shape
-    toks = 2 * half
+    half, hidden = has[0].shape
     blocks = hidden // 128
-    pitch = 16
-    unroll = 8
+    pitch, unroll, group = 8, 8, 64
+    split = [(j // pitch, j % pitch) for j in range(blocks)]
 
     def copies(srcs, i, b):
         return [pltpu.make_async_copy(src.at[i], dst.at[b], sems.at[n, b])
@@ -192,99 +197,124 @@
     def _():
         for i in range(depth - 1):
             fetch(jnp.int32(i))
-        for y_ref in y_refs:
-            y_ref[...] = jnp.zeros_like(y_ref)
+        for q in range(n_src):
+            for ref in sum_refs[q]:
+                ref[...] = jnp.zeros_like(ref)
+            for ref in tok_refs[q]:
+                ref[pl.ds(2 * half * pitch, pitch), :] = jnp.zeros((pitch, 128), F32)
+
+            def spread(i, carry):
+                for src, start in ((has[q], 0), (hbs[q], half)):
+                    v = src[pl.ds(pl.multiple_of(i * group, group), group), :].astype(F32)
+                    for j, (w, k) in enumerate(split):
+                        tok_refs[q][w][pl.ds((start + i * group) * pitch + k, group, stride=pitch), :] = v[:, j * 128:(j + 1) * 128]
+                return carry
+
+            lax.fori_loop(0, half // group, spread, 0)
 
     fetch(step + depth - 1)
     buf = step % depth
     for c in copies(own, 0, buf):
         c.wait()
-    row_of = lax.broadcasted_iota(jnp.int32, (steps, toks), 0)
     count = [c[step] for c in counts]
     most = count[0] if n_src == 1 else jnp.maximum(count[0], count[1])
-    pos = [jnp.sum(jnp.where(row_of == step, r[...], 0.0), axis=0, keepdims=True) for r in slot_refs]
-    gate = [jnp.sum(jnp.where(row_of == step, r[...], 0.0), axis=0, keepdims=True) for r in gate_refs]
     low = 0
     for rows in classes:
         @pl.when((most > low) & (most <= rows))
         def _(rows=rows):
-            xs, gcols = [], []
+            xs = []
             for q in range(n_src):
-                hit = lax.broadcasted_iota(jnp.int32, (rows, toks), 0).astype(F32) == pos[q]
-                pick = jnp.where(hit, 1.0, 0.0).astype(BF16)
-                gcols.append(jnp.sum(jnp.where(hit, gate[q], 0.0), axis=1, keepdims=True))
-                xs.append((jnp.dot(pick[:, :half], ha[q][...], preferred_element_type=F32)
-                           + jnp.dot(pick[:, half:], hb[q][...], preferred_element_type=F32)).astype(BF16))
+                def pick(i, carry):
+                    for u in range(unroll):
+                        r = i * unroll + u
+                        spot = pl.ds(pl.multiple_of(lists[q][step, r] * pitch, pitch), pitch)
+                        row = pl.ds(pl.multiple_of(r * pitch, pitch), pitch)
+                        for w in range(2):
+                            row_refs[q][w][row, :] = tok_refs[q][w][spot, :]
+                    return carry
+
+                lax.fori_loop(0, rows // unroll, pick, 0)
+                xs.append(jnp.concatenate([row_refs[q][w][pl.ds(k, rows, stride=pitch), :].astype(BF16) for w, k in split], axis=1))
             x = xs[0] if n_src == 1 else jnp.concatenate(xs, axis=0)
             gate_proj = jnp.dot(x, wg_ref[buf], preferred_element_type=F32)
             up_proj = jnp.dot(x, wu_ref[buf], preferred_element_type=F32)
             act = (jax.nn.silu(gate_proj) * up_proj).astype(BF16)
             out = jnp.dot(act, wd_ref[buf], preferred_element_type=F32).astype(BF16).astype(F32)
             for q in range(n_src):
-                part = out[q * rows:(q + 1) * rows] * gcols[q]
-                for j in range(blocks):
-                    e_refs[q][pl.ds(j, rows, stride=pitch), :] = part[:, j * 128:(j + 1) * 128]
+                for j, (w, k) in enumerate(split):
+                    row_refs[q][w][pl.ds(k, rows, stride=pitch), :] = out[q * rows:(q + 1) * rows, j * 128:(j + 1) * 128]
 
         low = rows
 
     for q in range(n_src):
-        y_ref, e_ref, list_ref = y_refs[q], e_refs[q], lists[q]
-
         def scatter(i, carry):
             spots, sums = [], []
             for u in range(unroll):
                 r = i * unroll + u
-                spot = pl.ds(pl.multiple_of(list_ref[step, r] * pitch, pitch), pitch)
+                spot = pl.ds(pl.multiple_of(lists[q][step, r] * pitch, pitch), pitch)
                 row = pl.ds(pl.multiple_of(r * pitch, pitch), pitch)
-                spots.append(spot)
-                sums.append(y_ref[spot, :] + e_ref[row, :])
-            for spot, v in zip(spots, sums):
-                y_ref[spot, :] = v
+                g = glists[q][step, r]
+                for w in range(2):
+                    spots.append((w, spot))
+                    sums.append(sum_refs[q][w][spot, :] + row_refs[q][w][row, :] * g)
+            for (w, spot), v in zip(spots, sums):
+                sum_refs[q][w][spot, :] = v
             return carry
 
         lax.fori_loop(0, (count[q] + unroll - 1) // unroll, scatter, 0)
 
     @pl.when(step == steps - 1)
     def _():
-        group = 64
+        outs = [(q, ref, start) for q in range(n_src) for ref, start in ((yas[q], 0), (ybs[q], half))]
+
+        def put(n, ref, i):
+            rows = pl.ds(pl.multiple_of(i * group, group), group)
+            return pltpu.make_async_copy(stage_ref.at[i % 2, n], ref.at[rows], out_sems.at[i % 2, n])
 
         def unpack(i, carry):
-            to = pl.ds(pl.multiple_of(i * group, group), group)
-            for q in range(n_src):
-                for ref, start in ((ya[q], 0), (yb[q], half)):
-                    for j in range(blocks):
-                        ref[to, j * 128:(j + 1) * 128] = y_refs[q][pl.ds((start + i * group) * pitch + j, group, stride=pitch), :]
+            for n, (q, ref, start) in enumerate(outs):
+                @pl.when(i >= 2)
+                def _():
+                    put(n, ref, i).wait()
+
+                for j, (w, k) in enumerate(split):
+                    stage_ref[i % 2, n, :, j * 128:(j + 1) * 128] = (
+                        sum_refs[q][w][pl.ds((start + i * group) * pitch + k, group, stride=pitch), :])
+                put(n, ref, i).start()
             return carry
 
         lax.fori_loop(0, half // group, unpack, 0)
+        for i in range(2):
+            for n, (q, ref, start) in enumerate(outs):
+                put(n, ref, i).wait()
 
 
 def expert_call(sources, own, sib, dep, local_max):
     n_src = len(sources)
-    lists, counts, has, hbs, slots, gates = zip(*sources)
+    lists, glists, counts, has, hbs = zip(*sources)
     half, hidden = has[0].shape
     slots_dev, _, ff = own[0].shape
-    depth = 4 if n_src == 1 else 3
+    depth = 4 if n_src == 1 else 2
     classes = tuple(c for c in CLASSES if c < local_max) + (local_max,)
     whole = pl.BlockSpec((half, hidden), lambda s: (0, 0), pipeline_mode=pl.Buffered(1))
-    table = pl.BlockSpec(slots[0].shape, lambda s: (0, 0), pipeline_mode=pl.Buffered(1))
     smem = pl.BlockSpec(memory_space=pltpu.SMEM)
     hbm = pl.BlockSpec(memory_space=pl.ANY)
     out = jax.ShapeDtypeStruct((half, hidden), F32)
+    toks = (2 * half + 8) * 8
     got = pl.pallas_call(
         functools.partial(expert_kernel, n_src, classes, slots_dev, depth),
         grid=(2 * slots_dev,),
         out_shape=(out,) * (2 * n_src),
-        in_specs=[smem] * (2 * n_src) + [whole] * (2 * n_src) + [table] * (2 * n_src) + [hbm] * 7,
-        out_specs=(whole,) * (2 * n_src),
+        in_specs=[smem] * (3 * n_src) + [whole] * (2 * n_src) + [hbm] * 7,
+        out_specs=(hbm,) * (2 * n_src),
         scratch_shapes=[pltpu.VMEM((depth, hidden, ff), BF16), pltpu.VMEM((depth, hidden, ff), BF16), pltpu.VMEM((depth, ff, hidden), BF16)]
-        + [pltpu.VMEM((local_max * 16, 128), F32)] * n_src + [pltpu.VMEM(((2 * half + 8) * 16, 128), F32)] * n_src
-        + [pltpu.SemaphoreType.DMA((3, depth))],
-        compiler_params=pltpu.CompilerParams(dimension_semantics=("arbitrary",), vmem_limit_bytes=62 * 1024 * 1024),
+        + [pltpu.VMEM((local_max * 8, 128), F32)] * (2 * n_src) + [pltpu.VMEM((toks, 128), F32)] * (4 * n_src)
+        + [pltpu.VMEM((2, 2 * n_src, 64, hidden), F32), pltpu.SemaphoreType.DMA((3, depth)), pltpu.SemaphoreType.DMA((2, 2 * n_src))],
+        compiler_params=pltpu.CompilerParams(dimension_semantics=("arbitrary",), vmem_limit_bytes=63 * 1024 * 1024),
         cost_estimate=pl.CostEstimate(flops=1_000_000, transcendentals=0,
                                       bytes_accessed=2 * slots_dev * 3 * hidden * ff * 2),
         name="experts",
-    )(*lists, *counts, *has, *hbs, *slots, *gates, *own, *sib, dep)
+    )(*lists, *glists, *counts, *has, *hbs, *own, *sib, dep)
     return got[:n_src], got[n_src:]
 
 
@@ -324,14 +354,14 @@
         router_probs = jax.nn.softmax(logits, axis=-1)
         chosen = topk_idx[:, :, None] == jnp.arange(experts)[None, None, :]
         gate_vals = jnp.sum(jnp.where(chosen, router_probs[:, None, :], 0.0), axis=-1)
-        pad = (-2 * top_k) % 8
-        table = jnp.concatenate([topk_idx.T.astype(F32), gate_vals.T, jnp.zeros((pad, tok_dev), F32)], axis=0)
-        sib_table = lax.ppermute(table, 'ep', sibling)
+        own_counts = jnp.sum(chosen.astype(F32), axis=(0, 1)).reshape(1, experts)
+        sib_counts = lax.ppermute(own_counts, 'ep', sibling)
+        count_rows = jnp.pad(jnp.concatenate([own_counts, sib_counts], axis=0), ((0, (-2 * top_k - 2) % 8), (0, tok_dev - experts)))
+        table = jnp.concatenate([topk_idx.T.astype(F32), gate_vals.T, count_rows], axis=0)
         own_w = (w_gate, w_up, w_down)
-        sib_w = tuple(lax.ppermute(after(w, sib_table), 'ep', sibling) for w in own_w)
-        pair = jnp.stack([table, sib_table])
-        t_r1, t_l1 = go_right(pair), go_left(pair)
-        t_far = lax.ppermute(pair, 'ep', far)
+        sib_w = tuple(lax.ppermute(after(w, sib_counts), 'ep', sibling) for w in own_w)
+        t_r1, t_l1 = go_right(table), go_left(table)
+        t_far = lax.ppermute(table, 'ep', far)
 
         ha_r2, hb_l2 = go_right(ha_r1), go_left(hb_l1)
         hb_r1, ha_l1 = go_right(after(hb, ha_r1)), go_left(after(ha, hb_l1))
@@ -339,12 +369,12 @@
         steps = jnp.arange(group_size // cores)
         rel = cores * ((chip + steps) % (group_size // cores))
         ids = jnp.concatenate([jnp.stack([rel + core, rel + 1 - core], axis=1).reshape(-1), jnp.stack([chip, core])]).astype(jnp.int32)
-        slot, gate, lists, kept = route_call(ids, table, sib_table, t_l1, t_far, t_r1, top_k, slots_dev, capacity, local_max)
-        lists = lists[:, :, 0, :]
+        lists, glists, kept = route_call(ids, table, t_l1, t_far, t_r1, top_k, slots_dev, capacity, local_max)
+        lists, glists = lists[:, :, 0, :], glists[:, :, 0, :]
         kept = kept[:, :, 0].astype(jnp.int32)
 
         def source(j, part_a, part_b):
-            return lists[j], kept[j], part_a, part_b, slot[j], gate[j]
+            return lists[j], glists[j], kept[j], part_a, part_b
 
         (y2a,), (y2b,) = expert_call([source(2, ha_r2, hb_l2)], own_w, sib_w, ha, local_max)
         p_ra, p_lb = go_right(y2a), go_left(y2b)

time: 373 us -> 369 us (0.989)
  Pallas kernels: 171 us -> 153 us
  waiting for transfers between devices: 111 us -> 123 us
    pallas_call x3, Pallas kernels: 149 us -> 130 us  [expert_call(): pl.pallas_call(functools.partial(expert_kernel, n_src, classes, slots_dev...]
    ppermute x7, waiting for transfers between devices: 61.9 us -> 77.8 us  [go_right(): return lax.ppermute(v, 'ep', right)]
    ppermute x7, waiting for transfers between devices: 46.6 us -> 41.8 us  [go_left(): return lax.ppermute(v, 'ep', left)]
    ppermute x7, starting transfers between devices: 22.5 us -> 26.3 us  [go_left(): return lax.ppermute(v, 'ep', left)]
  transfers between devices with their start and end apart: 19 -> 19, of which waited for: 10 -> 9; matrix products, arithmetic and copies ran while one was open for 13% -> 14% of each run, Pallas kernels for 43% -> 38%
where the time goes in v1:
time: 369 us; the launch traced here: 368 us
  Pallas kernels  153 us (41%)
  waiting for transfers between devices  123 us (33%)
  matrix products  39.3 us (11%)
  starting transfers between devices  35.2 us (10%)
  other arithmetic  10.5 us (3%)
  local copies, waits for them, and re-layouts  6.97 us (2%)
    pallas_call x3, Pallas kernels, expert_call(): pl.pallas_call(functools.partial(expert_kernel, n_src, classes, slots_dev...  130 us
    ppermute x7, waiting for transfers between devices, go_right(): return lax.ppermute(v, 'ep', right)  77.8 us
    ppermute x7, waiting for transfers between devices, go_left(): return lax.ppermute(v, 'ep', left)  41.8 us
    ppermute x7, starting transfers between devices, go_left(): return lax.ppermute(v, 'ep', left)  26.3 us
    dot_general x2, matrix products, shared_expert(): shared_val = jnp.dot(shared_act, s_down, preferred_element_type=F32)  21.9 us
    pallas_call x1, Pallas kernels, route_call(): pl.pallas_call(functools.partial(route_kernel, (top_k, slots_dev, capacit...  11.1 us
    dot_general x2, matrix products, shared_expert(): jnp.dot(normed, s_gate, preferred_element_type=F32)  9.41 us
    add x2, other arithmetic, block(): z_a, z_b = (go_right(y1a + p_ra), go_left(y3b + p_lb))  8.46 us
  transfers between devices with their start and end apart: 19, of which 9 were waited for; matrix products, arithmetic and copies ran while one was open for 14% of the time, Pallas kernels for 38%

profile of v1, /device:TPU:88, one launch (start us, length us, event | category | flops | bytes accessed | tf_op | source)
XLA Modules:
  0.0 368.0 jit_solution(5097710396696989390)
XLA Ops:
  0.0 1.3 reshape.150.gain_ref
  1.3 4.6 %norm.1 = (bf16[512,1536]{1,0:T(8,128)(2,1)}, bf16[512,1536]{1,0:T(8,128)(2,1)}) custom-call(bf16[2,512,1536]{2,1,0:T(8,128)(2,1)} %bitcast.44, bf16[1,1536]{1,0:T(2,128)(2,1)} %reshape.150.gain_ref), custom_call_target="tpu_custom_call" | custom-call | flops 6291456 | bytes 6291456 | tf_op jit(solution)/shard_map/norm/pallas_call | solution.py:28
  5.9 2.0 fusion.13
  7.9 2.0 fusion.14
  10.1 0.4 select_reduce_fusion
  10.5 0.1 collective-permute-start
  10.6 1.1 collective-permute-done
  11.7 0.2 collective-permute-start.4
  11.9 0.3 collective-permute-start.5
  12.2 0.2 collective-permute-start.6
  12.5 3.3 collective-permute-start.1
  15.7 0.5 collective-permute-start.2
  16.2 2.8 collective-permute-done.1.next_ref
  19.0 2.5 collective-permute-done.2.far_ref
  21.5 3.9 %collective-permute-done.3.prev_ref = f32[16,1024]{1,0:T(8,128)S(1)} collective-permute-done((f32[16,1024]{1,0:T(8,128)S(1)}, f32[16,1024]{1,0:T(8,128)S(1)}, u32[]{:S(2)}, u32[]{:S(2)}) %collective-permute-start.3) | collective-permute-done | bytes 65568 | tf_op jit(solution)/shard_map/ppermute | solution.py:340
  25.4 2.2 collective-permute-start.7
  27.6 31.0 %collective-permute-done.9.refs_7_ = bf16[512,1536]{1,0:T(8,128)(2,1)S(1)} collective-permute-done((bf16[512,1536]{1,0:T(8,128)(2,1)}, bf16[512,1536]{1,0:T(8,128)(2,1)S(1)}, u32[]{:S(2)}, u32[]{:S(2)}) %collective-permute-start.9) | collective-permute-done | bytes 1572896 | tf_op jit(solution)/shard_map/ppermute | solution.py:340
  58.6 1.1 copy-done.5
  59.8 3.2 collective-permute-start.12
  63.2 32.8 %collective-permute-done.11.refs_3_ = bf16[512,1536]{1,0:T(8,128)(2,1)} collective-permute-done((bf16[512,1536]{1,0:T(8,128)(2,1)S(1)}, bf16[512,1536]{1,0:T(8,128)(2,1)}, u32[]{:S(2)}, u32[]{:S(2)}) %collective-permute-start.11) | collective-permute-done | bytes 1572896 | tf_op jit(solution)/shard_map/ppermute | solution.py:340
  95.9 3.2 collective-permute-start.8
  99.2 0.6 pad_add_fusion.1.ids_ref
  99.8 11.1 %route.1 = (s32[4,16,8,192]{3,2,1,0:T(8,128)}, f32[4,16,8,192]{3,2,1,0:T(8,128)}, f32[4,16,128]{2,1,0:T(8,128)}) custom-call(s32[10]{0:T(128)} %pad_add_fusion.1.ids_ref, f32[16,1024]{1,0:T(8,128)} %copy-done.7, f32[16,1024]{1,0:T(8,128)} %copy-done.9, f32[16,1024]{1,0:T(8,128)} %copy-done.10, f32[16,1024]{1,0:T(8,128)} %copy-done.11), custom_call_target="tpu_custom_call" | custom-call | flops 1000000 | bytes 2000000 | tf_op jit(solution)/shard_map/route/pallas_call | solution.py:146
  110.9 1.2 copy.33
  112.1 1.2 copy.32
  113.3 0.8 slice_convert_fusion
  114.1 0.7 slice_reduce_fusion.3
  114.8 0.6 slice_bitcast_fusion.6
  115.5 0.6 slice_bitcast_fusion.7
  116.1 36.7 %experts.3 = (f32[512,1536]{1,0:T(8,128)}, f32[512,1536]{1,0:T(8,128)}) custom-call(s32[16,192]{1,0:T(8,128)} %get-tuple-element.60.refs_0_, f32[16,192]{1,0:T(8,128)} %get-tuple-element.56.refs_1_, s32[16]{0:T(128)} %get-tuple-element.50.refs_2_, bf16[512,1536]{1,0:T(8,128)(2,1)} %collective-permute-done.11.refs_3_, ...), custom_call_target="tpu_custom_call" | custom-call | flops 1000000 | bytes 75497472 | tf_op jit(solution)/shard_map/experts/pallas_call | solution.py:304
  152.8 6.5 %collective-permute-start.17 = (f32[512,1536]{1,0:T(8,128)}, f32[512,1536]{1,0:T(8,128)}, u32[]{:S(2)}, u32[]{:S(2)}) collective-permute-start(f32[512,1536]{1,0:T(8,128)} %get-tuple-element.47), channel_id=1, source_target_pairs={{0,6},{1,7},{2,0},{3,1},{4,2},{5,3},{6,4},{7,5},{8,14},{9,15},{10,... | collective-permute-start | bytes 9437192 | tf_op jit(solution)/shard_map/ppermute | solution.py:343
  159.3 55.8 %experts.4 = (f32[512,1536]{1,0:T(8,128)}, f32[512,1536]{1,0:T(8,128)}, f32[512,1536]{1,0:T(8,128)}, f32[512,1536]{1,0:T(8,128)}) custom-call(s32[16,192]{1,0:T(8,128)} %get-tuple-element.62.refs_0_, s32[16,192]{1,0:T(8,128)} %get-tuple-element.61.refs_1_, f32[16,192]{1,0:T(8,128)} %get-tuple-element.58.refs_2_, f32[16,192]{1,0:T(8,128)} %get-tuple-element.57.refs_3_, ...), custom_call_target="tpu_custom_call" | custom-call | flops 1000000 | bytes 75497472 | tf_op jit(solution)/shard_map/experts/pallas_call | solution.py:304
  215.1 5.5 %collective-permute-start.14 = (f32[512,1536]{1,0:T(8,128)}, f32[512,1536]{1,0:T(8,128)}, u32[]{:S(2)}, u32[]{:S(2)}) collective-permute-start(f32[512,1536]{1,0:T(8,128)} %get-tuple-element.43), channel_id=1, source_target_pairs={{0,2},{1,3},{2,4},{3,5},{4,6},{5,7},{6,0},{7,1},{8,10},{9,11},{10,... | collective-permute-start | bytes 9437192 | tf_op jit(solution)/shard_map/ppermute | solution.py:340
  220.7 7.9 %collective-permute-start.13 = (f32[512,1536]{1,0:T(8,128)}, f32[512,1536]{1,0:T(8,128)}, u32[]{:S(2)}, u32[]{:S(2)}) collective-permute-start(f32[512,1536]{1,0:T(8,128)} %get-tuple-element.38.refs_11_), channel_id=1, source_target_pairs={{0,6},{1,7},{2,0},{3,1},{4,2},{5,3},{6,4},{7,5},{8,14},{9,15},{10,... | collective-permute-start | bytes 9437192 | tf_op jit(solution)/shard_map/ppermute | solution.py:343
  228.5 38.0 %experts.5 = (f32[512,1536]{1,0:T(8,128)}, f32[512,1536]{1,0:T(8,128)}) custom-call(s32[16,192]{1,0:T(8,128)} %get-tuple-element.59.refs_0_, f32[16,192]{1,0:T(8,128)} %get-tuple-element.55.refs_1_, s32[16]{0:T(128)} %get-tuple-element.49.refs_2_, bf16[512,1536]{1,0:T(8,128)(2,1)} %get-tuple-element.40.refs_11_.refs_3_, ...), custom_call_target="tpu_custom_call" | custom-call | flops 1000000 | bytes 75497472 | tf_op jit(solution)/shard_map/experts/pallas_call | solution.py:304
  266.5 2.1 fusion.17
  268.6 1.9 fusion.15
  270.6 4.7 %fusion.18 = f32[512,1024]{1,0:T(8,128)} fusion(bf16[512,1536]{1,0:T(8,128)(2,1)} %get-tuple-element.41.refs_4_, bf16[1536,1024]{1,0:T(8,128)(2,1)S(1)} %copy-done.13), kind=kOutput, calls=%fused_computation.54 | convolution fusion | flops 1610612736 | bytes 6815744 | tf_op jit(solution)/shard_map/dot_general | solution.py:63
  275.3 4.3 %add.121 = f32[512,1536]{1,0:T(8,128)} add(f32[512,1536]{1,0:T(8,128)S(1)} %copy-done.4, f32[512,1536]{1,0:T(8,128)} %collective-permute-done.17) | non-fusion elementwise | flops 786432 | bytes 9437184 | tf_op jit(solution)/shard_map/add | solution.py:385
  279.6 4.1 %add.120 = f32[512,1536]{1,0:T(8,128)} add(f32[512,1536]{1,0:T(8,128)S(1)} %copy-done.3, f32[512,1536]{1,0:T(8,128)} %collective-permute-done.15) | non-fusion elementwise | flops 786432 | bytes 9437184 | tf_op jit(solution)/shard_map/add | solution.py:385
  283.7 2.0 collective-permute-start.16
  285.8 4.7 %fusion.16 = f32[512,1024]{1,0:T(8,128)} fusion(bf16[512,1536]{1,0:T(8,128)(2,1)} %get-tuple-element.40.refs_11_.refs_3_, bf16[1536,1024]{1,0:T(8,128)(2,1)S(1)} %copy-done.13), kind=kOutput, calls=%fused_computation.52 | convolution fusion | flops 1610612736 | bytes 6815744 | tf_op jit(solution)/shard_map/dot_general | solution.py:63
  290.5 7.2 %collective-permute-done.14 = f32[512,1536]{1,0:T(8,128)} collective-permute-done((f32[512,1536]{1,0:T(8,128)}, f32[512,1536]{1,0:T(8,128)}, u32[]{:S(2)}, u32[]{:S(2)}) %collective-permute-start.14) | collective-permute-done | bytes 3145760 | tf_op jit(solution)/shard_map/ppermute | solution.py:340
  297.7 11.0 %fusion.3.base_b = f32[512,1536]{1,0:T(8,128)} fusion(f32[512,1536]{1,0:T(8,128)} %collective-permute-done.14, f32[512,1536]{1,0:T(8,128)} %get-tuple-element.42, bf16[1024,1536]{1,0:T(8,128)(2,1)} %param.18, f32[512]{0:T(512)S(1)} %add_divide_fusion, bf16[1024,1536]{1,0:T(8,128)(2,1)S(1)} %copy-done.2, f32[512,1024]{1,0:T(8,128)} %fusion.18, ...), kind=kOutput, calls=%fused_computation.5 | convolution fusion | flops 3228303360 | bytes 20973568 | tf_op jit(solution)/shard_map/dot_general | solution.py:65
  308.7 10.9 %fusion.5.base_a = f32[512,1536]{1,0:T(8,128)} fusion(f32[512,1536]{1,0:T(8,128)} %collective-permute-done.13, f32[512,1536]{1,0:T(8,128)} %get-tuple-element.39, bf16[1024,1536]{1,0:T(8,128)(2,1)} %param.18, f32[512]{0:T(512)S(1)} %add_divide_fusion.1, bf16[1024,1536]{1,0:T(8,128)(2,1)S(1)} %copy-done.2, f32[512,1024]{1,0:T(8,128)} %fusion.16, ...), kind=kOutput, calls=%fused_computation.7 | convolution fusion | flops 3228303360 | bytes 20973568 | tf_op jit(solution)/shard_map/dot_general | solution.py:65
  319.6 39.0 %collective-permute-done.18.zb_ref = f32[512,1536]{1,0:T(8,128)} collective-permute-done((f32[512,1536]{1,0:T(8,128)}, f32[512,1536]{1,0:T(8,128)}, u32[]{:S(2)}, u32[]{:S(2)}) %collective-permute-start.18) | collective-permute-done | bytes 3145760 | tf_op jit(solution)/shard_map/ppermute | solution.py:343
  358.6 2.9 collective-permute-done.16.za_ref
  361.5 6.5 %final.1 = bf16[2,512,1536]{2,1,0:T(8,128)(2,1)} custom-call(f32[512,1536]{1,0:T(8,128)} %fusion.5.base_a, f32[512,1536]{1,0:T(8,128)} %fusion.3.base_b, f32[512,1536]{1,0:T(8,128)} %collective-permute-done.16.za_ref, f32[512,1536]{1,0:T(8,128)} %collective-permute-done.18.zb_ref), custom_call_target="tpu_custom_call" | custom-call | flops 1572864 | bytes 15728640 | tf_op jit(solution)/shard_map/final/pallas_call | solution.py:49
  (54 shorter events, 0.5 us)
Async XLA Ops:
  0.0 5.9 %copy-start = (bf16[1536,64]{0,1:T(8,128)(2,1)S(1)}, bf16[1536,64]{0,1:T(8,128)(2,1)}, u32[]{:S(2)}) copy-start(bf16[1536,64]{0,1:T(8,128)(2,1)} %param.14) | copy-start | bytes 589828
  5.9 4.2 %copy-start.8 = (s32[1024,6]{0,1:T(8,128)S(1)}, s32[1024,6]{0,1:T(8,128)}, u32[]{:S(2)}) copy-start(s32[1024,6]{0,1:T(8,128)} %param.12) | copy-start | bytes 73732
  10.5 1.3 collective-permute-start
  11.7 104.4 %collective-permute-start.4 = (bf16[8,1536,512]{2,1,0:T(8,128)(2,1)}, bf16[8,1536,512]{2,1,0:T(8,128)(2,1)}, u32[]{:S(2)}, u32[]{:S(2)}) collective-permute-start(bf16[8,1536,512]{2,1,0:T(8,128)(2,1)} %refs_5_.3), channel_id=1, source_target_pairs={{0,1},{1,0},{2,3},{3,2},{4,5},{5,4},{6,7},{7,6},{8,9},{9,8},{10,11... | collective-permute-start | bytes 37748744 | tf_op jit(solution)/shard_map/ppermute | solution.py:362
  11.9 104.2 %collective-permute-start.5 = (bf16[8,1536,512]{2,1,0:T(8,128)(2,1)}, bf16[8,1536,512]{2,1,0:T(8,128)(2,1)}, u32[]{:S(2)}, u32[]{:S(2)}) collective-permute-start(bf16[8,1536,512]{2,1,0:T(8,128)(2,1)} %refs_6_.3), channel_id=1, source_target_pairs={{0,1},{1,0},{2,3},{3,2},{4,5},{5,4},{6,7},{7,6},{8,9},{9,8},{10,11... | collective-permute-start | bytes 37748744 | tf_op jit(solution)/shard_map/ppermute | solution.py:362
  12.2 103.9 %collective-permute-start.6 = (bf16[8,512,1536]{2,1,0:T(8,128)(2,1)}, bf16[8,512,1536]{2,1,0:T(8,128)(2,1)}, u32[]{:S(2)}, u32[]{:S(2)}) collective-permute-start(bf16[8,512,1536]{2,1,0:T(8,128)(2,1)} %refs_7_.3), channel_id=1, source_target_pairs={{0,1},{1,0},{2,3},{3,2},{4,5},{5,4},{6,7},{7,6},{8,9},{9,8},{10,11... | collective-permute-start | bytes 37748744 | tf_op jit(solution)/shard_map/ppermute | solution.py:362
  12.4 87.3 %copy-start.7 = (f32[16,1024]{1,0:T(8,128)}, f32[16,1024]{1,0:T(8,128)S(1)}, u32[]{:S(2)}) copy-start(f32[16,1024]{1,0:T(8,128)S(1)} %pad_maximum_fusion.1.own_ref) | copy-start | bytes 196612
  12.5 6.6 %collective-permute-start.1 = (f32[16,1024]{1,0:T(8,128)S(1)}, f32[16,1024]{1,0:T(8,128)S(1)}, u32[]{:S(2)}, u32[]{:S(2)}) collective-permute-start(f32[16,1024]{1,0:T(8,128)S(1)} %pad_maximum_fusion.1.own_ref), channel_id=1, source_target_pairs={{0,6},{1,7},{2,0},{3,1},{4,2},{5,3},{6,4},{7,5},{8,14},{9,15},{10,... | collective-permute-start | bytes 196616 | tf_op jit(solution)/shard_map/ppermute | solution.py:343
  15.7 5.8 %collective-permute-start.2 = (f32[16,1024]{1,0:T(8,128)S(1)}, f32[16,1024]{1,0:T(8,128)S(1)}, u32[]{:S(2)}, u32[]{:S(2)}) collective-permute-start(f32[16,1024]{1,0:T(8,128)S(1)} %pad_maximum_fusion.1.own_ref), channel_id=1, source_target_pairs={{0,4},{1,5},{2,6},{3,7},{4,0},{5,1},{6,2},{7,3},{8,12},{9,13},{10,... | collective-permute-start | bytes 196616 | tf_op jit(solution)/shard_map/ppermute | solution.py:364
  19.0 80.8 %copy-start.9 = (f32[16,1024]{1,0:T(8,128)}, f32[16,1024]{1,0:T(8,128)S(1)}, u32[]{:S(2)}) copy-start(f32[16,1024]{1,0:T(8,128)S(1)} %collective-permute-done.1.next_ref) | copy-start | bytes 196612
  19.0 6.4 %collective-permute-start.3 = (f32[16,1024]{1,0:T(8,128)S(1)}, f32[16,1024]{1,0:T(8,128)S(1)}, u32[]{:S(2)}, u32[]{:S(2)}) collective-permute-start(f32[16,1024]{1,0:T(8,128)S(1)} %pad_maximum_fusion.1.own_ref), channel_id=1, source_target_pairs={{0,2},{1,3},{2,4},{3,5},{4,6},{5,7},{6,0},{7,1},{8,10},{9,11},{10,... | collective-permute-start | bytes 196616 | tf_op jit(solution)/shard_map/ppermute | solution.py:340
  21.5 78.3 %copy-start.10 = (f32[16,1024]{1,0:T(8,128)}, f32[16,1024]{1,0:T(8,128)S(1)}, u32[]{:S(2)}) copy-start(f32[16,1024]{1,0:T(8,128)S(1)} %collective-permute-done.2.far_ref) | copy-start | bytes 196612
  21.5 37.1 %collective-permute-start.9 = (bf16[512,1536]{1,0:T(8,128)(2,1)}, bf16[512,1536]{1,0:T(8,128)(2,1)S(1)}, u32[]{:S(2)}, u32[]{:S(2)}) collective-permute-start(bf16[512,1536]{1,0:T(8,128)(2,1)} %get-tuple-element.40.refs_11_.refs_3_), channel_id=1, source_target_pairs={{0,2},{1,3},{2,4},{3,5},{4,6},{5,7},{6,0},{7,1},{8,10},{9,11},{10,... | collective-permute-start | bytes 4718600 | tf_op jit(solution)/shard_map/ppermute | solution.py:340
  25.4 74.4 %copy-start.11 = (f32[16,1024]{1,0:T(8,128)}, f32[16,1024]{1,0:T(8,128)S(1)}, u32[]{:S(2)}) copy-start(f32[16,1024]{1,0:T(8,128)S(1)} %collective-permute-done.3.prev_ref) | copy-start | bytes 196612
  25.4 34.3 %collective-permute-start.7 = (bf16[512,1536]{1,0:T(8,128)(2,1)}, bf16[512,1536]{1,0:T(8,128)(2,1)S(1)}, u32[]{:S(2)}, u32[]{:S(2)}) collective-permute-start(bf16[512,1536]{1,0:T(8,128)(2,1)} %get-tuple-element.41.refs_4_), channel_id=1, source_target_pairs={{0,6},{1,7},{2,0},{3,1},{4,2},{5,3},{6,4},{7,5},{8,14},{9,15},{10,... | collective-permute-start | bytes 4718600 | tf_op jit(solution)/shard_map/ppermute | solution.py:343
  58.6 1.1 copy-start.5
  59.7 36.2 %collective-permute-start.11 = (bf16[512,1536]{1,0:T(8,128)(2,1)S(1)}, bf16[512,1536]{1,0:T(8,128)(2,1)}, u32[]{:S(2)}, u32[]{:S(2)}) collective-permute-start(bf16[512,1536]{1,0:T(8,128)(2,1)S(1)} %collective-permute-done.9.refs_7_), channel_id=1, source_target_pairs={{0,2},{1,3},{2,4},{3,5},{4,6},{5,7},{6,0},{7,1},{8,10},{9,11},{10,... | collective-permute-start | bytes 4718600 | tf_op jit(solution)/shard_map/ppermute | solution.py:340
  59.8 36.2 %copy-start.6 = (bf16[512,1536]{1,0:T(8,128)(2,1)}, bf16[512,1536]{1,0:T(8,128)(2,1)S(1)}, u32[]{:S(2)}) copy-start(bf16[512,1536]{1,0:T(8,128)(2,1)S(1)} %collective-permute-done.7.refs_8_) | copy-start | bytes 4718596
  59.8 36.2 %collective-permute-start.12 = (bf16[512,1536]{1,0:T(8,128)(2,1)S(1)}, bf16[512,1536]{1,0:T(8,128)(2,1)}, u32[]{:S(2)}, u32[]{:S(2)}) collective-permute-start(bf16[512,1536]{1,0:T(8,128)(2,1)S(1)} %collective-permute-done.7.refs_8_), channel_id=1, source_target_pairs={{0,6},{1,7},{2,0},{3,1},{4,2},{5,3},{6,4},{7,5},{8,14},{9,15},{10,... | collective-permute-start | bytes 4718600 | tf_op jit(solution)/shard_map/ppermute | solution.py:343
  95.9 63.4 %collective-permute-start.10 = (bf16[512,1536]{1,0:T(8,128)(2,1)}, bf16[512,1536]{1,0:T(8,128)(2,1)}, u32[]{:S(2)}, u32[]{:S(2)}) collective-permute-start(bf16[512,1536]{1,0:T(8,128)(2,1)} %get-tuple-element.41.refs_4_), channel_id=1, source_target_pairs={{0,2},{1,3},{2,4},{3,5},{4,6},{5,7},{6,0},{7,1},{8,10},{9,11},{10,... | collective-permute-start | bytes 4718600 | tf_op jit(solution)/shard_map/ppermute | solution.py:340
  95.9 63.4 %collective-permute-start.8 = (bf16[512,1536]{1,0:T(8,128)(2,1)}, bf16[512,1536]{1,0:T(8,128)(2,1)}, u32[]{:S(2)}, u32[]{:S(2)}) collective-permute-start(bf16[512,1536]{1,0:T(8,128)(2,1)} %get-tuple-element.40.refs_11_.refs_3_), channel_id=1, source_target_pairs={{0,6},{1,7},{2,0},{3,1},{4,2},{5,3},{6,4},{7,5},{8,14},{9,15},{10,... | collective-permute-start | bytes 4718600 | tf_op jit(solution)/shard_map/ppermute | solution.py:343
  152.8 122.5 %collective-permute-start.17 = (f32[512,1536]{1,0:T(8,128)}, f32[512,1536]{1,0:T(8,128)}, u32[]{:S(2)}, u32[]{:S(2)}) collective-permute-start(f32[512,1536]{1,0:T(8,128)} %get-tuple-element.47), channel_id=1, source_target_pairs={{0,6},{1,7},{2,0},{3,1},{4,2},{5,3},{6,4},{7,5},{8,14},{9,15},{10,... | collective-permute-start | bytes 9437192 | tf_op jit(solution)/shard_map/ppermute | solution.py:343
  159.3 120.3 %collective-permute-start.15 = (f32[512,1536]{1,0:T(8,128)}, f32[512,1536]{1,0:T(8,128)}, u32[]{:S(2)}, u32[]{:S(2)}) collective-permute-start(f32[512,1536]{1,0:T(8,128)} %get-tuple-element.37.refs_16_), channel_id=1, source_target_pairs={{0,2},{1,3},{2,4},{3,5},{4,6},{5,7},{6,0},{7,1},{8,10},{9,11},{10,... | collective-permute-start | bytes 9437192 | tf_op jit(solution)/shard_map/ppermute | solution.py:340
  215.1 82.5 %collective-permute-start.14 = (f32[512,1536]{1,0:T(8,128)}, f32[512,1536]{1,0:T(8,128)}, u32[]{:S(2)}, u32[]{:S(2)}) collective-permute-start(f32[512,1536]{1,0:T(8,128)} %get-tuple-element.43), channel_id=1, source_target_pairs={{0,2},{1,3},{2,4},{3,5},{4,6},{5,7},{6,0},{7,1},{8,10},{9,11},{10,... | collective-permute-start | bytes 9437192 | tf_op jit(solution)/shard_map/ppermute | solution.py:340
  220.7 88.0 %collective-permute-start.13 = (f32[512,1536]{1,0:T(8,128)}, f32[512,1536]{1,0:T(8,128)}, u32[]{:S(2)}, u32[]{:S(2)}) collective-permute-start(f32[512,1536]{1,0:T(8,128)} %get-tuple-element.38.refs_11_), channel_id=1, source_target_pairs={{0,6},{1,7},{2,0},{3,1},{4,2},{5,3},{6,4},{7,5},{8,14},{9,15},{10,... | collective-permute-start | bytes 9437192 | tf_op jit(solution)/shard_map/ppermute | solution.py:343
  228.5 38.0 %copy-start.12 = (bf16[1536,1]{0,1:T(2,128)(2,1)S(1)}, bf16[1536,1]{0,1:T(2,128)(2,1)}, u32[]{:S(2)}) copy-start(bf16[1536,1]{0,1:T(2,128)(2,1)} %param.15) | copy-start | bytes 9220
  266.5 4.0 %copy-start.13 = (bf16[1536,1024]{1,0:T(8,128)(2,1)S(1)}, bf16[1536,1024]{1,0:T(8,128)(2,1)}, u32[]{:S(2)}) copy-start(bf16[1536,1024]{1,0:T(8,128)(2,1)} %param.16) | copy-start | bytes 9437188
  270.5 4.7 %copy-start.4 = (f32[512,1536]{1,0:T(8,128)S(1)}, f32[512,1536]{1,0:T(8,128)}, u32[]{:S(2)}) copy-start(f32[512,1536]{1,0:T(8,128)} %get-tuple-element.46) | copy-start | bytes 9437188
  275.3 4.3 %copy-start.3 = (f32[512,1536]{1,0:T(8,128)S(1)}, f32[512,1536]{1,0:T(8,128)}, u32[]{:S(2)}) copy-start(f32[512,1536]{1,0:T(8,128)} %get-tuple-element.44) | copy-start | bytes 9437188
  279.6 79.0 %collective-permute-start.18 = (f32[512,1536]{1,0:T(8,128)}, f32[512,1536]{1,0:T(8,128)}, u32[]{:S(2)}, u32[]{:S(2)}) collective-permute-start(f32[512,1536]{1,0:T(8,128)} %add.121), channel_id=1, source_target_pairs={{0,6},{1,7},{2,0},{3,1},{4,2},{5,3},{6,4},{7,5},{8,14},{9,15},{10,... | collective-permute-start | bytes 9437192 | tf_op jit(solution)/shard_map/ppermute | solution.py:343
  283.7 77.8 %collective-permute-start.16 = (f32[512,1536]{1,0:T(8,128)}, f32[512,1536]{1,0:T(8,128)}, u32[]{:S(2)}, u32[]{:S(2)}) collective-permute-start(f32[512,1536]{1,0:T(8,128)} %add.120), channel_id=1, source_target_pairs={{0,2},{1,3},{2,4},{3,5},{4,6},{5,7},{6,0},{7,1},{8,10},{9,11},{10,... | collective-permute-start | bytes 9437192 | tf_op jit(solution)/shard_map/ppermute | solution.py:340
  285.8 11.9 %copy-start.2 = (bf16[1024,1536]{1,0:T(8,128)(2,1)S(1)}, bf16[1024,1536]{1,0:T(8,128)(2,1)}, u32[]{:S(2)}) copy-start(bf16[1024,1536]{1,0:T(8,128)(2,1)} %param.11) | copy-start | bytes 9437188
  361.5 6.5 %copy-start.1 = (bf16[1536,64]{0,1:T(8,128)(2,1)S(1)}, bf16[1536,64]{0,1:T(8,128)(2,1)}, u32[]{:S(2)}) copy-start(bf16[1536,64]{0,1:T(8,128)(2,1)} %param.14) | copy-start | bytes 589828

commit v2 on v1

--- a/solution.py
+++ b/solution.py
@@ -10,6 +10,7 @@
 
 F32, BF16 = jnp.float32, jnp.bfloat16
 CLASSES = (64, 128, 192)
+PAIRS = ((0, 0), (3, 1), (2, 2), (1, 3))
 
 
 def norm_kernel(x_ref, gain_ref, ha_ref, hb_ref):
@@ -96,21 +97,38 @@
         gate_ref[j] = gate
     hot_all = jnp.concatenate(hots, axis=0)
     hot_bf = hot_all.astype(BF16)
-    tile = 256
-    for c in range(toks // tile):
+    tile, half = 256, toks // 2
+
+    def before(c):
         rows = lax.broadcasted_iota(jnp.int32, (toks, tile), 0)
         cols = lax.broadcasted_iota(jnp.int32, (toks, tile), 1) + c * tile
-        before = jnp.where(rows < cols, 1.0, 0.0).astype(BF16)
-        pos = jnp.dot(hot_bf, before, preferred_element_type=F32)
+        return jnp.where(rows < cols, 1.0, 0.0).astype(BF16)
+
+    lowers = []
+    for j in range(4):
+        lower = jnp.zeros((slots, 1), F32)
+        for q in range(8):
+            lower = lower + counts[q] * (ids_ref[q] < ids_ref[2 * j]).astype(F32)
+        lowers.append(lower)
+    for c in range(toks // tile):
+        pos = jnp.dot(hot_bf, before(c), preferred_element_type=F32)
         for j in range(4):
-            lower = jnp.zeros((slots, 1), F32)
-            for q in range(8):
-                lower = lower + counts[q] * (ids_ref[q] < ids_ref[2 * j]).astype(F32)
             part = pos[j * slots:(j + 1) * slots]
-            kept = (hot_all[j * slots:(j + 1) * slots, c * tile:(c + 1) * tile] > 0.0) & (part + lower < capacity)
-            slot_ref[j, :, c * tile:(c + 1) * tile] = jnp.where(kept, part, -1.0)
-            if c == 0:
-                count_ref[j] = jnp.broadcast_to(jnp.clip(capacity - lower, 0.0, counts[2 * j]), (slots, 128))
+            kept = (hot_all[j * slots:(j + 1) * slots, c * tile:(c + 1) * tile] > 0.0) & (part + lowers[j] < capacity)
+            slot_ref[j, :, c * tile:(c + 1) * tile] = jnp.where(kept, 1.0, 0.0)
+    joined = []
+    gates = [gate_ref[j] for j in range(4)]
+    for v, (ja, jb) in enumerate(PAIRS):
+        joined.append(jnp.concatenate([slot_ref[ja][:, :half], slot_ref[jb][:, half:]], axis=1))
+        gate_ref[v] = jnp.concatenate([gates[ja][:, :half], gates[jb][:, half:]], axis=1)
+        count_ref[v] = jnp.broadcast_to(jnp.sum(joined[v], axis=1, keepdims=True), (slots, 128))
+    kept_all = jnp.concatenate(joined, axis=0)
+    kept_bf = kept_all.astype(BF16)
+    for c in range(toks // tile):
+        pos = jnp.dot(kept_bf, before(c), preferred_element_type=F32)
+        for v in range(4):
+            kept = kept_all[v * slots:(v + 1) * slots, c * tile:(c + 1) * tile] > 0.0
+            slot_ref[v, :, c * tile:(c + 1) * tile] = jnp.where(kept, pos[v * slots:(v + 1) * slots], -1.0)
     token = lax.broadcasted_iota(jnp.int32, (8, toks), 1)
     row8 = lax.broadcasted_iota(jnp.int32, (8, toks), 0)
     digits = jnp.where(row8 == 0, token // 32, token % 32).astype(F32)
@@ -125,15 +143,16 @@
             g2 = (gate - g1).astype(BF16).astype(F32)
             g3 = gate - g1 - g2
             left = jnp.where(row8 < 2, digits, jnp.where(row8 == 2, g1, jnp.where(row8 == 3, g2, g3))).astype(BF16)
-            want = lax.broadcasted_iota(jnp.int32, (local_max, toks), 0).astype(F32)
+            width = local_max if PAIRS[j][0] == PAIRS[j][1] else 2 * local_max
+            want = lax.broadcasted_iota(jnp.int32, (width, toks), 0).astype(F32)
             pick = jnp.where(want == pos, 1.0, 0.0).astype(BF16)
             got = lax.dot_general(left, pick, (((1,), (1,)), ((), ())), preferred_element_type=F32)
             found = 32.0 * got[0:1] + got[1:2]
             held = jnp.sum(jnp.where(count_row == e, count_ref[j], 0.0), axis=0, keepdims=True)[:, 0:1]
-            lane = lax.broadcasted_iota(jnp.int32, (1, local_max), 1).astype(F32)
+            lane = lax.broadcasted_iota(jnp.int32, (1, width), 1).astype(F32)
             found = jnp.where(lane < held, found, float(toks)).astype(jnp.int32)
-            list_ref[j, e] = jnp.broadcast_to(found, (8, local_max))
-            glist_ref[j, e] = jnp.broadcast_to((got[2:3] + got[3:4]) + got[4:5], (8, local_max))
+            list_ref[j, e, :, :width] = jnp.broadcast_to(found, (8, width))
+            glist_ref[j, e, :, :width] = jnp.broadcast_to((got[2:3] + got[3:4]) + got[4:5], (8, width))
         return carry
 
     lax.fori_loop(0, slots, lists, 0)
@@ -145,7 +164,7 @@
     vmem = pl.BlockSpec(memory_space=pltpu.VMEM)
     return pl.pallas_call(
         functools.partial(route_kernel, (top_k, slots_dev, capacity, local_max)),
-        out_shape=(jax.ShapeDtypeStruct((4, slots, 8, local_max), jnp.int32), jax.ShapeDtypeStruct((4, slots, 8, local_max), F32),
+        out_shape=(jax.ShapeDtypeStruct((4, slots, 8, 2 * local_max), jnp.int32), jax.ShapeDtypeStruct((4, slots, 8, 2 * local_max), F32),
                    jax.ShapeDtypeStruct((4, slots, 128), F32)),
         in_specs=[pl.BlockSpec(memory_space=pltpu.SMEM)] + [vmem] * 4,
         out_specs=(vmem,) * 3,
@@ -155,8 +174,9 @@
     )(ids, own, nxt, far, prv)
 
 
-def expert_kernel(n_src, classes, slots_dev, depth, *refs):
+def expert_kernel(pieces, classes, slots_dev, depth, *refs):
     refs = list(refs)
+    n_src = 1
 
     def take(n):
         got = refs[:n]
@@ -167,7 +187,7 @@
     has, hbs = take(n_src), take(n_src)
     own, sib = take(3), take(3)
     take(1)
-    yas, ybs = take(n_src), take(n_src)
+    ys = take(pieces)
     wg_ref, wu_ref, wd_ref = take(3)
     row_refs, tok_refs, sum_refs = [take(2) for _ in range(n_src)], [take(2) for _ in range(n_src)], [take(2) for _ in range(n_src)]
     stage_ref, sems, out_sems = take(3)
@@ -265,7 +285,8 @@
 
     @pl.when(step == steps - 1)
     def _():
-        outs = [(q, ref, start) for q in range(n_src) for ref, start in ((yas[q], 0), (ybs[q], half))]
+        size = 2 * half // pieces
+        outs = [(0, ref, n * size) for n, ref in enumerate(ys)]
 
         def put(n, ref, i):
             rows = pl.ds(pl.multiple_of(i * group, group), group)
@@ -283,39 +304,36 @@
                 put(n, ref, i).start()
             return carry
 
-        lax.fori_loop(0, half // group, unpack, 0)
+        lax.fori_loop(0, size // group, unpack, 0)
         for i in range(2):
             for n, (q, ref, start) in enumerate(outs):
                 put(n, ref, i).wait()
 
 
-def expert_call(sources, own, sib, dep, local_max):
-    n_src = len(sources)
-    lists, glists, counts, has, hbs = zip(*sources)
-    half, hidden = has[0].shape
+def expert_call(routes, ha, hb, own, sib, dep, row_max, pieces):
+    half, hidden = ha.shape
     slots_dev, _, ff = own[0].shape
-    depth = 4 if n_src == 1 else 2
-    classes = tuple(c for c in CLASSES if c < local_max) + (local_max,)
+    depth = 4
+    classes = tuple(c for c in CLASSES if c < row_max) + (row_max,)
     whole = pl.BlockSpec((half, hidden), lambda s: (0, 0), pipeline_mode=pl.Buffered(1))
     smem = pl.BlockSpec(memory_space=pltpu.SMEM)
     hbm = pl.BlockSpec(memory_space=pl.ANY)
-    out = jax.ShapeDtypeStruct((half, hidden), F32)
+    out = jax.ShapeDtypeStruct((2 * half // pieces, hidden), F32)
     toks = (2 * half + 8) * 8
-    got = pl.pallas_call(
-        functools.partial(expert_kernel, n_src, classes, slots_dev, depth),
+    return pl.pallas_call(
+        functools.partial(expert_kernel, pieces, classes, slots_dev, depth),
         grid=(2 * slots_dev,),
-        out_shape=(out,) * (2 * n_src),
-        in_specs=[smem] * (3 * n_src) + [whole] * (2 * n_src) + [hbm] * 7,
-        out_specs=(hbm,) * (2 * n_src),
+        out_shape=(out,) * pieces,
+        in_specs=[smem] * 3 + [whole] * 2 + [hbm] * 7,
+        out_specs=(hbm,) * pieces,
         scratch_shapes=[pltpu.VMEM((depth, hidden, ff), BF16), pltpu.VMEM((depth, hidden, ff), BF16), pltpu.VMEM((depth, ff, hidden), BF16)]
-        + [pltpu.VMEM((local_max * 8, 128), F32)] * (2 * n_src) + [pltpu.VMEM((toks, 128), F32)] * (4 * n_src)
-        + [pltpu.VMEM((2, 2 * n_src, 64, hidden), F32), pltpu.SemaphoreType.DMA((3, depth)), pltpu.SemaphoreType.DMA((2, 2 * n_src))],
-        compiler_params=pltpu.CompilerParams(dimension_semantics=("arbitrary",), vmem_limit_bytes=63 * 1024 * 1024),
+        + [pltpu.VMEM((row_max * 8, 128), F32)] * 2 + [pltpu.VMEM((toks, 128), F32)] * 4
+        + [pltpu.VMEM((2, pieces, 64, hidden), F32), pltpu.SemaphoreType.DMA((3, depth)), pltpu.SemaphoreType.DMA((2, pieces))],
+        compiler_params=pltpu.CompilerParams(dimension_semantics=("arbitrary",), vmem_limit_bytes=62 * 1024 * 1024),
         cost_estimate=pl.CostEstimate(flops=1_000_000, transcendentals=0,
                                       bytes_accessed=2 * slots_dev * 3 * hidden * ff * 2),
         name="experts",
-    )(*lists, *glists, *counts, *has, *hbs, *own, *sib, dep)
-    return got[:n_src], got[n_src:]
+    )(*routes, ha, hb, *own, *sib, dep)
 
 
 def solution(mesh):
@@ -373,20 +391,23 @@
         lists, glists = lists[:, :, 0, :], glists[:, :, 0, :]
         kept = kept[:, :, 0].astype(jnp.int32)
 
-        def source(j, part_a, part_b):
-            return lists[j], glists[j], kept[j], part_a, part_b
-
-        (y2a,), (y2b,) = expert_call([source(2, ha_r2, hb_l2)], own_w, sib_w, ha, local_max)
+        def routes(v, row_max):
+            return lists[v, :, :row_max], glists[v, :, :row_max], kept[v]
+
+        d_a0, d_a1, d_b0, d_b1 = expert_call(routes(1, 2 * local_max), ha_r1, hb_l1, own_w, sib_w, ha, 2 * local_max, 4)
+        d_a0, d_b0 = go_left(d_a0), go_right(d_b0)
+        y2a, y2b = expert_call(routes(2, local_max), ha_r2, hb_l2, own_w, sib_w, d_a1, local_max, 2)
         p_ra, p_lb = go_right(y2a), go_left(y2b)
-        (y1a, y3a), (y1b, y3b) = expert_call([source(1, ha_l1, hb_l1), source(3, ha_r1, hb_r1)], own_w, sib_w, y2a, local_max)
-        d_b, d_a = go_right(y1b), go_left(y3a)
-        (y0a,), (y0b,) = expert_call([source(0, ha, hb)], own_w, sib_w, y3a, local_max)
+        d_a1, d_b1 = go_left(d_a1), go_right(d_b1)
+        y1a, y3b = expert_call(routes(3, 2 * local_max), ha_l1, hb_r1, own_w, sib_w, y2a, 2 * local_max, 2)
+        y0a, y0b = expert_call(routes(0, local_max), ha, hb, own_w, sib_w, y3b, local_max, 2)
         p_ra, p_lb = after(p_ra, y0a), after(p_lb, y0b)
         z_a, z_b = go_right(y1a + p_ra), go_left(y3b + p_lb)
         base = []
         for i, (h, y0) in enumerate(((ha, y0a), (hb, y0b))):
             shared_val = shared_expert(after(h, y0a), w_sgate, s_gate, s_up, s_down)
             base.append(hidden_in[i * half:(i + 1) * half].astype(F32) + shared_val + y0)
+        d_a, d_b = jnp.concatenate([d_a0, d_a1], axis=0), jnp.concatenate([d_b0, d_b1], axis=0)
         return final_call(base[0] + d_a, base[1] + d_b, z_a, z_b)
 
     row_spec = P(('dp', 'ep'), None)

time: 369 us -> 478 us (1.30)
  waiting for transfers between devices: 123 us -> 204 us
  Pallas kernels: 153 us -> 174 us
  starting transfers between devices: 35.2 us -> 42.9 us
    ppermute x7 -> x8, waiting for transfers between devices: 41.8 us -> 115 us  [go_left(): return lax.ppermute(v, 'ep', left)]
    pallas_call x3 -> x4, Pallas kernels: 130 us -> 148 us  [expert_call(): pl.pallas_call(functools.partial(expert_kernel, pieces, classes, slots_de...]
    ppermute x7 -> x8, waiting for transfers between devices: 77.8 us -> 85.2 us  [go_right(): return lax.ppermute(v, 'ep', right)]
    ppermute x7 -> x8, starting transfers between devices: 26.3 us -> 32.1 us  [go_left(): return lax.ppermute(v, 'ep', left)]
  transfers between devices with their start and end apart: 19 -> 21, of which waited for: 9 -> 8; matrix products, arithmetic and copies ran while one was open for 14% -> 10% of each run, Pallas kernels for 38% -> 26%
where the time goes in v2:
time: 478 us; the launch traced here: 476 us
  waiting for transfers between devices  204 us (43%)
  Pallas kernels  174 us (36%)
  starting transfers between devices  42.9 us (9%)
  matrix products  37.4 us (8%)
  other arithmetic  10.4 us (2%)
  local copies, waits for them, and re-layouts  7.63 us (2%)
    pallas_call x4, Pallas kernels, expert_call(): pl.pallas_call(functools.partial(expert_kernel, pieces, classes, slots_de...  148 us
    ppermute x8, waiting for transfers between devices, go_left(): return lax.ppermute(v, 'ep', left)  115 us
    ppermute x8, waiting for transfers between devices, go_right(): return lax.ppermute(v, 'ep', right)  85.2 us
    ppermute x8, starting transfers between devices, go_left(): return lax.ppermute(v, 'ep', left)  32.1 us
    dot_general x2, matrix products, shared_expert(): shared_val = jnp.dot(shared_act, s_down, preferred_element_type=F32)  22.3 us
    pallas_call x1, Pallas kernels, route_call(): pl.pallas_call(functools.partial(route_kernel, (top_k, slots_dev, capacit...  15 us
    dot_general x2, matrix products, shared_expert(): jnp.dot(normed, s_gate, preferred_element_type=F32)  9.97 us
  transfers between devices with their start and end apart: 21, of which 8 were waited for; matrix products, arithmetic and copies ran while one was open for 10% of the time, Pallas kernels for 26%

profile of v2, /device:TPU:88, one launch (start us, length us, event | category | flops | bytes accessed | tf_op | source)
XLA Modules:
  0.0 476.5 jit_solution(13217473615221024153)
XLA Ops:
  0.0 1.3 reshape.142.gain_ref
  1.3 4.6 norm.1
  5.9 2.1 fusion.14
  8.1 0.6 fusion.13
  8.8 0.4 select_reduce_fusion
  9.3 1.1 collective-permute-done
  10.6 0.3 collective-permute-start.5
  11.2 1.7 collective-permute-start.3
  12.9 3.0 collective-permute-start.2
  15.9 1.1 collective-permute-done.3.prev_ref
  17.0 2.4 collective-permute-start.1
  19.6 0.8 collective-permute-start.7
  20.4 1.5 collective-permute-done.1.next_ref
  22.1 0.6 pad_add_fusion.1.ids_ref
  22.7 15.0 %route.1 = (s32[4,16,8,384]{3,2,1,0:T(8,128)}, f32[4,16,8,384]{3,2,1,0:T(8,128)}, f32[4,16,128]{2,1,0:T(8,128)}) custom-call(s32[10]{0:T(128)} %pad_add_fusion.1.ids_ref, f32[16,1024]{1,0:T(8,128)} %copy-done.11, f32[16,1024]{1,0:T(8,128)} %copy-done.15, f32[16,1024]{1,0:T(8,128)} %copy-done.14, f32[16,1024]{1,0:T(8,128)} %copy-done.13), custom_call_target="tpu_custom_call" | custom-call | flops 1000000 | bytes 2000000 | tf_op jit(solution)/shard_map/route/pallas_call | solution.py:165
  37.6 17.9 %collective-permute-done.7.refs_4_ = bf16[512,1536]{1,0:T(8,128)(2,1)S(1)} collective-permute-done((bf16[512,1536]{1,0:T(8,128)(2,1)}, bf16[512,1536]{1,0:T(8,128)(2,1)S(1)}, u32[]{:S(2)}, u32[]{:S(2)}) %collective-permute-start.7) | collective-permute-done | bytes 1572896 | tf_op jit(solution)/shard_map/ppermute | solution.py:361
  55.6 2.7 collective-permute-start.12
  58.3 0.8 slice_convert_fusion
  59.1 1.3 copy.30
  60.9 0.7 slice_reduce_fusion
  61.6 0.6 slice_bitcast_fusion.7
  62.2 0.6 slice_bitcast_fusion.6
  62.8 0.6 slice_bitcast_fusion.3
  63.5 0.6 slice_bitcast_fusion.2
  64.1 1.8 collective-permute-done.6.refs_10_
  65.9 36.6 %experts.4 = (f32[256,1536]{1,0:T(8,128)}, f32[256,1536]{1,0:T(8,128)}, f32[256,1536]{1,0:T(8,128)}, f32[256,1536]{1,0:T(8,128)}) custom-call(s32[16,384]{1,0:T(8,128)} %get-tuple-element.61.refs_0_, f32[16,384]{1,0:T(8,128)} %get-tuple-element.59.refs_1_, s32[16]{0:T(128)} %get-tuple-element.53.refs_2_, bf16[512,1536]{1,0:T(8,128)(2,1)} %collective-permute-done.9.refs_3_, ...), custom_call_target="tpu_custom_call" | custom-call | flops 1000000 | bytes 75497472 | tf_op jit(solution)/shard_map/experts/pallas_call | solution.py:323
  102.6 36.9 %experts.5 = (f32[512,1536]{1,0:T(8,128)}, f32[512,1536]{1,0:T(8,128)}) custom-call(s32[16,192]{1,0:T(8,128)} %get-tuple-element.65.refs_0_, f32[16,192]{1,0:T(8,128)} %get-tuple-element.63.refs_1_, s32[16]{0:T(128)} %get-tuple-element.54.refs_2_, bf16[512,1536]{1,0:T(8,128)(2,1)} %collective-permute-done.11.refs_3_, ...), custom_call_target="tpu_custom_call" | custom-call | flops 1000000 | bytes 75497472 | tf_op jit(solution)/shard_map/experts/pallas_call | solution.py:323
  139.4 13.1 %collective-permute-start.19 = (f32[512,1536]{1,0:T(8,128)}, f32[512,1536]{1,0:T(8,128)}, u32[]{:S(2)}, u32[]{:S(2)}) collective-permute-start(f32[512,1536]{1,0:T(8,128)} %get-tuple-element.51), channel_id=1, source_target_pairs={{0,6},{1,7},{2,0},{3,1},{4,2},{5,3},{6,4},{7,5},{8,14},{9,15},{10,... | collective-permute-start | bytes 9437192 | tf_op jit(solution)/shard_map/ppermute | solution.py:361
  152.6 3.2 collective-permute-start.8
  155.8 3.2 collective-permute-start.13
  159.0 95.9 %collective-permute-done.8.refs_3_ = bf16[512,1536]{1,0:T(8,128)(2,1)S(1)} collective-permute-done((bf16[512,1536]{1,0:T(8,128)(2,1)S(1)}, bf16[512,1536]{1,0:T(8,128)(2,1)S(1)}, u32[]{:S(2)}, u32[]{:S(2)}) %collective-permute-start.8) | collective-permute-done | bytes 1572896 | tf_op jit(solution)/shard_map/ppermute | solution.py:361
  255.0 1.2 copy-done.10
  256.2 3.7 collective-permute-start.14
  259.9 36.3 %experts.6 = (f32[512,1536]{1,0:T(8,128)}, f32[512,1536]{1,0:T(8,128)}) custom-call(s32[16,384]{1,0:T(8,128)} %get-tuple-element.62.refs_0_, f32[16,384]{1,0:T(8,128)} %get-tuple-element.60.refs_1_, s32[16]{0:T(128)} %get-tuple-element.55.refs_2_, bf16[512,1536]{1,0:T(8,128)(2,1)} %copy-done.10, bf16[512,1536]{1,0:T(8,128)(2,1)} %collective-permute-done.10.refs_4_, ...), custom_call_target="tpu_custom_call" | custom-call | flops 1000000 | bytes 75497472 | tf_op jit(solution)/shard_map/experts/pallas_call | solution.py:323
  296.2 38.2 %experts.7 = (f32[512,1536]{1,0:T(8,128)}, f32[512,1536]{1,0:T(8,128)}) custom-call(s32[16,192]{1,0:T(8,128)} %get-tuple-element.66.refs_0_, f32[16,192]{1,0:T(8,128)} %get-tuple-element.64.refs_1_, s32[16]{0:T(128)} %get-tuple-element.56.refs_2_, bf16[512,1536]{1,0:T(8,128)(2,1)} %get-tuple-element.43.refs_11_.refs_3_, ...), custom_call_target="tpu_custom_call" | custom-call | flops 1000000 | bytes 75497472 | tf_op jit(solution)/shard_map/experts/pallas_call | solution.py:323
  334.5 5.2 %fusion.16 = f32[512,1024]{1,0:T(8,128)} fusion(bf16[512,1536]{1,0:T(8,128)(2,1)S(1)} %copy-done.4, bf16[1536,1024]{1,0:T(8,128)(2,1)} %param.16), kind=kOutput, calls=%fused_computation.54 | convolution fusion | flops 1610612736 | bytes 6815744 | tf_op jit(solution)/shard_map/dot_general | solution.py:64
  339.7 0.5 fusion.15
  340.2 4.7 fusion.18
  345.0 4.3 add.121
  349.2 3.0 collective-permute-start.20
  352.2 4.1 add.120
  356.4 3.2 collective-permute-start.18
  359.6 1.9 fusion.17
  361.5 2.0 collective-permute-start.16
  363.6 10.9 %fusion.5.base_a = f32[512,1536]{1,0:T(8,128)} fusion(f32[512,1536]{1,0:T(8,128)} %get-tuple-element.42, bf16[1024,1536]{1,0:T(8,128)(2,1)} %param.18, f32[256,1536]{1,0:T(8,128)} %collective-permute-done.14, f32[256,1536]{1,0:T(8,128)} %collective-permute-done.13, f32[512]{0:T(512)S(1)} %add_divide_fusion.1, bf16[1024,1536]{1,0:T(8,128)(2,1)} %param.11, ...), kind=kOutput, calls=%fused_computation.7 | convolution fusion | flops 3229089792 | bytes 20973568 | tf_op jit(solution)/shard_map/dot_general | solution.py:66
  374.5 84.0 %collective-permute-done.16 = f32[256,1536]{1,0:T(8,128)} collective-permute-done((f32[256,1536]{1,0:T(8,128)}, f32[256,1536]{1,0:T(8,128)}, u32[]{:S(2)}, u32[]{:S(2)}) %collective-permute-start.16) | collective-permute-done | bytes 1572896 | tf_op jit(solution)/shard_map/ppermute | solution.py:358
  458.5 11.5 %fusion.3.base_b = f32[512,1536]{1,0:T(8,128)} fusion(f32[512,1536]{1,0:T(8,128)} %get-tuple-element.46, bf16[1024,1536]{1,0:T(8,128)(2,1)} %param.18, f32[256,1536]{1,0:T(8,128)} %collective-permute-done.16, f32[256,1536]{1,0:T(8,128)} %collective-permute-done.15, f32[512]{0:T(512)S(1)} %add_divide_fusion, bf16[1024,1536]{1,0:T(8,128)(2,1)} %param.11, ...), kind=kOutput, calls=%fused_computation.5 | convolution fusion | flops 3229089792 | bytes 20973568 | tf_op jit(solution)/shard_map/dot_general | solution.py:66
  470.0 6.5 %final.1 = bf16[2,512,1536]{2,1,0:T(8,128)(2,1)} custom-call(f32[512,1536]{1,0:T(8,128)} %fusion.5.base_a, f32[512,1536]{1,0:T(8,128)} %fusion.3.base_b, f32[512,1536]{1,0:T(8,128)} %collective-permute-done.18.za_ref, f32[512,1536]{1,0:T(8,128)} %collective-permute-done.20.zb_ref), custom_call_target="tpu_custom_call" | custom-call | flops 1572864 | bytes 15728640 | tf_op jit(solution)/shard_map/final/pallas_call | solution.py:50
  (73 shorter events, 1.6 us)
Async XLA Ops:
  0.0 5.9 %copy-start = (bf16[1536,64]{0,1:T(8,128)(2,1)S(1)}, bf16[1536,64]{0,1:T(8,128)(2,1)}, u32[]{:S(2)}) copy-start(bf16[1536,64]{0,1:T(8,128)(2,1)} %param.14) | copy-start | bytes 589828
  5.9 2.1 copy-start.2
  5.9 2.9 copy-start.12
  9.2 1.3 collective-permute-start
  10.4 53.7 %collective-permute-start.4 = (bf16[8,1536,512]{2,1,0:T(8,128)(2,1)}, bf16[8,1536,512]{2,1,0:T(8,128)(2,1)}, u32[]{:S(2)}, u32[]{:S(2)}) collective-permute-start(bf16[8,1536,512]{2,1,0:T(8,128)(2,1)} %refs_5_.7), channel_id=1, source_target_pairs={{0,1},{1,0},{2,3},{3,2},{4,5},{5,4},{6,7},{7,6},{8,9},{9,8},{10,11... | collective-permute-start | bytes 37748744 | tf_op jit(solution)/shard_map/ppermute | solution.py:380
  10.6 53.5 %collective-permute-start.5 = (bf16[8,1536,512]{2,1,0:T(8,128)(2,1)}, bf16[8,1536,512]{2,1,0:T(8,128)(2,1)}, u32[]{:S(2)}, u32[]{:S(2)}) collective-permute-start(bf16[8,1536,512]{2,1,0:T(8,128)(2,1)} %refs_6_.7), channel_id=1, source_target_pairs={{0,1},{1,0},{2,3},{3,2},{4,5},{5,4},{6,7},{7,6},{8,9},{9,8},{10,11... | collective-permute-start | bytes 37748744 | tf_op jit(solution)/shard_map/ppermute | solution.py:380
  10.9 55.0 %collective-permute-start.6 = (bf16[8,512,1536]{2,1,0:T(8,128)(2,1)}, bf16[8,512,1536]{2,1,0:T(8,128)(2,1)}, u32[]{:S(2)}, u32[]{:S(2)}) collective-permute-start(bf16[8,512,1536]{2,1,0:T(8,128)(2,1)} %refs_7_.7), channel_id=1, source_target_pairs={{0,1},{1,0},{2,3},{3,2},{4,5},{5,4},{6,7},{7,6},{8,9},{9,8},{10,11... | collective-permute-start | bytes 37748744 | tf_op jit(solution)/shard_map/ppermute | solution.py:380
  11.1 11.5 %copy-start.11 = (f32[16,1024]{1,0:T(8,128)}, f32[16,1024]{1,0:T(8,128)S(1)}, u32[]{:S(2)}) copy-start(f32[16,1024]{1,0:T(8,128)S(1)} %pad_maximum_fusion.1.own_ref) | copy-start | bytes 196612
  11.2 5.9 %collective-permute-start.3 = (f32[16,1024]{1,0:T(8,128)S(1)}, f32[16,1024]{1,0:T(8,128)S(1)}, u32[]{:S(2)}, u32[]{:S(2)}) collective-permute-start(f32[16,1024]{1,0:T(8,128)S(1)} %pad_maximum_fusion.1.own_ref), channel_id=1, source_target_pairs={{0,2},{1,3},{2,4},{3,5},{4,6},{5,7},{6,0},{7,1},{8,10},{9,11},{10,... | collective-permute-start | bytes 196616 | tf_op jit(solution)/shard_map/ppermute | solution.py:358
  12.9 6.7 %collective-permute-start.2 = (f32[16,1024]{1,0:T(8,128)S(1)}, f32[16,1024]{1,0:T(8,128)S(1)}, u32[]{:S(2)}, u32[]{:S(2)}) collective-permute-start(f32[16,1024]{1,0:T(8,128)S(1)} %pad_maximum_fusion.1.own_ref), channel_id=1, source_target_pairs={{0,4},{1,5},{2,6},{3,7},{4,0},{5,1},{6,2},{7,3},{8,12},{9,13},{10,... | collective-permute-start | bytes 196616 | tf_op jit(solution)/shard_map/ppermute | solution.py:382
  17.0 5.6 %copy-start.13 = (f32[16,1024]{1,0:T(8,128)}, f32[16,1024]{1,0:T(8,128)S(1)}, u32[]{:S(2)}) copy-start(f32[16,1024]{1,0:T(8,128)S(1)} %collective-permute-done.3.prev_ref) | copy-start | bytes 196612
  17.0 4.8 %collective-permute-start.1 = (f32[16,1024]{1,0:T(8,128)S(1)}, f32[16,1024]{1,0:T(8,128)S(1)}, u32[]{:S(2)}, u32[]{:S(2)}) collective-permute-start(f32[16,1024]{1,0:T(8,128)S(1)} %pad_maximum_fusion.1.own_ref), channel_id=1, source_target_pairs={{0,6},{1,7},{2,0},{3,1},{4,2},{5,3},{6,4},{7,5},{8,14},{9,15},{10,... | collective-permute-start | bytes 196616 | tf_op jit(solution)/shard_map/ppermute | solution.py:361
  19.6 3.1 copy-start.14
  19.6 36.0 %collective-permute-start.7 = (bf16[512,1536]{1,0:T(8,128)(2,1)}, bf16[512,1536]{1,0:T(8,128)(2,1)S(1)}, u32[]{:S(2)}, u32[]{:S(2)}) collective-permute-start(bf16[512,1536]{1,0:T(8,128)(2,1)} %get-tuple-element.45.refs_4_), channel_id=1, source_target_pairs={{0,6},{1,7},{2,0},{3,1},{4,2},{5,3},{6,4},{7,5},{8,14},{9,15},{10,... | collective-permute-start | bytes 4718600 | tf_op jit(solution)/shard_map/ppermute | solution.py:361
  21.9 0.8 copy-start.15
  21.9 36.4 %collective-permute-start.9 = (bf16[512,1536]{1,0:T(8,128)(2,1)S(1)}, bf16[512,1536]{1,0:T(8,128)(2,1)}, u32[]{:S(2)}, u32[]{:S(2)}) collective-permute-start(bf16[512,1536]{1,0:T(8,128)(2,1)S(1)} %copy-done.2), channel_id=1, source_target_pairs={{0,2},{1,3},{2,4},{3,5},{4,6},{5,7},{6,0},{7,1},{8,10},{9,11},{10,... | collective-permute-start | bytes 4718600 | tf_op jit(solution)/shard_map/ppermute | solution.py:358
  37.6 22.7 %copy-start.7 = (s32[4,16,8,384]{3,2,1,0:T(8,128)S(1)}, s32[4,16,8,384]{3,2,1,0:T(8,128)}, u32[]{:S(2)}) copy-start(s32[4,16,8,384]{3,2,1,0:T(8,128)} %get-tuple-element.31) | copy-start | bytes 2359300
  37.6 22.9 %copy-start.6 = (f32[4,16,8,384]{3,2,1,0:T(8,128)S(1)}, f32[4,16,8,384]{3,2,1,0:T(8,128)}, u32[]{:S(2)}) copy-start(f32[4,16,8,384]{3,2,1,0:T(8,128)} %get-tuple-element.32) | copy-start | bytes 2359300
  55.6 5.1 %copy-start.9 = (bf16[512,1536]{1,0:T(8,128)(2,1)}, bf16[512,1536]{1,0:T(8,128)(2,1)S(1)}, u32[]{:S(2)}) copy-start(bf16[512,1536]{1,0:T(8,128)(2,1)S(1)} %collective-permute-done.7.refs_4_) | copy-start | bytes 4718596
  55.6 46.9 %collective-permute-start.12 = (bf16[512,1536]{1,0:T(8,128)(2,1)S(1)}, bf16[512,1536]{1,0:T(8,128)(2,1)}, u32[]{:S(2)}, u32[]{:S(2)}) collective-permute-start(bf16[512,1536]{1,0:T(8,128)(2,1)S(1)} %collective-permute-done.7.refs_4_), channel_id=1, source_target_pairs={{0,6},{1,7},{2,0},{3,1},{4,2},{5,3},{6,4},{7,5},{8,14},{9,15},{10,... | collective-permute-start | bytes 4718600 | tf_op jit(solution)/shard_map/ppermute | solution.py:361
  58.3 44.2 %collective-permute-start.11 = (bf16[512,1536]{1,0:T(8,128)(2,1)}, bf16[512,1536]{1,0:T(8,128)(2,1)}, u32[]{:S(2)}, u32[]{:S(2)}) collective-permute-start(bf16[512,1536]{1,0:T(8,128)(2,1)} %collective-permute-done.9.refs_3_), channel_id=1, source_target_pairs={{0,2},{1,3},{2,4},{3,5},{4,6},{5,7},{6,0},{7,1},{8,10},{9,11},{10,... | collective-permute-start | bytes 4718600 | tf_op jit(solution)/shard_map/ppermute | solution.py:358
  102.6 50.0 %copy-start.3 = (bf16[512,1536]{1,0:T(8,128)(2,1)S(1)}, bf16[512,1536]{1,0:T(8,128)(2,1)}, u32[]{:S(2)}) copy-start(bf16[512,1536]{1,0:T(8,128)(2,1)} %get-tuple-element.43.refs_11_.refs_3_) | copy-start | bytes 4718596
  139.4 205.5 %collective-permute-start.19 = (f32[512,1536]{1,0:T(8,128)}, f32[512,1536]{1,0:T(8,128)}, u32[]{:S(2)}, u32[]{:S(2)}) collective-permute-start(f32[512,1536]{1,0:T(8,128)} %get-tuple-element.51), channel_id=1, source_target_pairs={{0,6},{1,7},{2,0},{3,1},{4,2},{5,3},{6,4},{7,5},{8,14},{9,15},{10,... | collective-permute-start | bytes 9437192 | tf_op jit(solution)/shard_map/ppermute | solution.py:361
  152.6 199.7 %collective-permute-start.17 = (f32[512,1536]{1,0:T(8,128)}, f32[512,1536]{1,0:T(8,128)}, u32[]{:S(2)}, u32[]{:S(2)}) collective-permute-start(f32[512,1536]{1,0:T(8,128)} %get-tuple-element.40.refs_11_), channel_id=1, source_target_pairs={{0,2},{1,3},{2,4},{3,5},{4,6},{5,7},{6,0},{7,1},{8,10},{9,11},{10,... | collective-permute-start | bytes 9437192 | tf_op jit(solution)/shard_map/ppermute | solution.py:358
  152.6 102.4 %collective-permute-start.8 = (bf16[512,1536]{1,0:T(8,128)(2,1)S(1)}, bf16[512,1536]{1,0:T(8,128)(2,1)S(1)}, u32[]{:S(2)}, u32[]{:S(2)}) collective-permute-start(bf16[512,1536]{1,0:T(8,128)(2,1)S(1)} %copy-done.3), channel_id=1, source_target_pairs={{0,6},{1,7},{2,0},{3,1},{4,2},{5,3},{6,4},{7,5},{8,14},{9,15},{10,... | collective-permute-start | bytes 4718600 | tf_op jit(solution)/shard_map/ppermute | solution.py:361
  155.8 104.1 %collective-permute-start.10 = (bf16[512,1536]{1,0:T(8,128)(2,1)}, bf16[512,1536]{1,0:T(8,128)(2,1)}, u32[]{:S(2)}, u32[]{:S(2)}) collective-permute-start(bf16[512,1536]{1,0:T(8,128)(2,1)} %get-tuple-element.45.refs_4_), channel_id=1, source_target_pairs={{0,2},{1,3},{2,4},{3,5},{4,6},{5,7},{6,0},{7,1},{8,10},{9,11},{10,... | collective-permute-start | bytes 4718600 | tf_op jit(solution)/shard_map/ppermute | solution.py:358
  155.8 205.7 %collective-permute-start.13 = (f32[256,1536]{1,0:T(8,128)}, f32[256,1536]{1,0:T(8,128)}, u32[]{:S(2)}, u32[]{:S(2)}) collective-permute-start(f32[256,1536]{1,0:T(8,128)} %get-tuple-element.44), channel_id=1, source_target_pairs={{0,6},{1,7},{2,0},{3,1},{4,2},{5,3},{6,4},{7,5},{8,14},{9,15},{10,... | collective-permute-start | bytes 4718600 | tf_op jit(solution)/shard_map/ppermute | solution.py:361
  255.0 1.2 copy-start.10
  256.2 107.4 %collective-permute-start.14 = (f32[256,1536]{1,0:T(8,128)}, f32[256,1536]{1,0:T(8,128)}, u32[]{:S(2)}, u32[]{:S(2)}) collective-permute-start(f32[256,1536]{1,0:T(8,128)} %get-tuple-element.39.refs_11_), channel_id=1, source_target_pairs={{0,6},{1,7},{2,0},{3,1},{4,2},{5,3},{6,4},{7,5},{8,14},{9,15},{10,... | collective-permute-start | bytes 4718600 | tf_op jit(solution)/shard_map/ppermute | solution.py:361
  259.9 114.6 %collective-permute-start.15 = (f32[256,1536]{1,0:T(8,128)}, f32[256,1536]{1,0:T(8,128)}, u32[]{:S(2)}, u32[]{:S(2)}) collective-permute-start(f32[256,1536]{1,0:T(8,128)} %get-tuple-element.47), channel_id=1, source_target_pairs={{0,2},{1,3},{2,4},{3,5},{4,6},{5,7},{6,0},{7,1},{8,10},{9,11},{10,... | collective-permute-start | bytes 4718600 | tf_op jit(solution)/shard_map/ppermute | solution.py:358
  296.2 38.3 %copy-start.4 = (bf16[512,1536]{1,0:T(8,128)(2,1)S(1)}, bf16[512,1536]{1,0:T(8,128)(2,1)}, u32[]{:S(2)}) copy-start(bf16[512,1536]{1,0:T(8,128)(2,1)} %get-tuple-element.43.refs_11_.refs_3_) | copy-start | bytes 4718596
  334.5 5.3 %copy-start.16 = (bf16[1536,1]{0,1:T(2,128)(2,1)S(1)}, bf16[1536,1]{0,1:T(2,128)(2,1)}, u32[]{:S(2)}) copy-start(bf16[1536,1]{0,1:T(2,128)(2,1)} %param.15) | copy-start | bytes 9220
  334.5 5.8 %copy-start.17 = (bf16[1536,1024]{1,0:T(8,128)(2,1)S(1)}, bf16[1536,1024]{1,0:T(8,128)(2,1)}, u32[]{:S(2)}) copy-start(bf16[1536,1024]{1,0:T(8,128)(2,1)} %param.16) | copy-start | bytes 9437188
  340.2 4.7 copy-start.5
  345.0 7.3 %copy-start.8 = (f32[512,1536]{1,0:T(8,128)S(1)}, f32[512,1536]{1,0:T(8,128)}, u32[]{:S(2)}) copy-start(f32[512,1536]{1,0:T(8,128)} %get-tuple-element.49) | copy-start | bytes 9437188
  349.2 120.7 %collective-permute-start.20 = (f32[512,1536]{1,0:T(8,128)}, f32[512,1536]{1,0:T(8,128)}, u32[]{:S(2)}, u32[]{:S(2)}) collective-permute-start(f32[512,1536]{1,0:T(8,128)} %add.121), channel_id=1, source_target_pairs={{0,6},{1,7},{2,0},{3,1},{4,2},{5,3},{6,4},{7,5},{8,14},{9,15},{10,... | collective-permute-start | bytes 9437192 | tf_op jit(solution)/shard_map/ppermute | solution.py:361
  356.4 113.6 %collective-permute-start.18 = (f32[512,1536]{1,0:T(8,128)}, f32[512,1536]{1,0:T(8,128)}, u32[]{:S(2)}, u32[]{:S(2)}) collective-permute-start(f32[512,1536]{1,0:T(8,128)} %add.120), channel_id=1, source_target_pairs={{0,2},{1,3},{2,4},{3,5},{4,6},{5,7},{6,0},{7,1},{8,10},{9,11},{10,... | collective-permute-start | bytes 9437192 | tf_op jit(solution)/shard_map/ppermute | solution.py:358
  361.5 96.9 %collective-permute-start.16 = (f32[256,1536]{1,0:T(8,128)}, f32[256,1536]{1,0:T(8,128)}, u32[]{:S(2)}, u32[]{:S(2)}) collective-permute-start(f32[256,1536]{1,0:T(8,128)} %get-tuple-element.48), channel_id=1, source_target_pairs={{0,2},{1,3},{2,4},{3,5},{4,6},{5,7},{6,0},{7,1},{8,10},{9,11},{10,... | collective-permute-start | bytes 4718600 | tf_op jit(solution)/shard_map/ppermute | solution.py:358
  470.0 6.5 %copy-start.1 = (bf16[1536,64]{0,1:T(8,128)(2,1)S(1)}, bf16[1536,64]{0,1:T(8,128)(2,1)}, u32[]{:S(2)}) copy-start(bf16[1536,64]{0,1:T(8,128)(2,1)} %param.14) | copy-start | bytes 589828

commit v3 on v2

--- a/solution.py
+++ b/solution.py
@@ -14,7 +14,7 @@
 
 
 def norm_kernel(x_ref, gain_ref, ha_ref, hb_ref):
-    gain = gain_ref[...].astype(F32)
+    gain = gain_ref[...].astype(F32)[None, :]
     for i, out_ref in enumerate((ha_ref, hb_ref)):
         x = x_ref[i].astype(F32)
         inv_rms = lax.rsqrt(jnp.mean(x * x, axis=-1, keepdims=True) + 1e-6)
@@ -30,34 +30,38 @@
         norm_kernel,
         grid=(half // rows,),
         out_shape=(out, out),
-        in_specs=[pl.BlockSpec((2, rows, hidden), lambda i: (0, i, 0)), pl.BlockSpec((1, hidden), lambda i: (0, 0))],
+        in_specs=[pl.BlockSpec((2, rows, hidden), lambda i: (0, i, 0)), pl.BlockSpec((hidden,), lambda i: (0,))],
         out_specs=(block, block),
         compiler_params=pltpu.CompilerParams(dimension_semantics=("arbitrary",)),
         cost_estimate=pl.CostEstimate(flops=4 * toks * hidden, transcendentals=toks, bytes_accessed=4 * toks * hidden),
         name="norm",
-    )(hidden_in.reshape(2, half, hidden), norm_gain.reshape(1, hidden))
-
-
-def final_kernel(base_a, base_b, za_ref, zb_ref, out_ref):
+    )(hidden_in.reshape(2, half, hidden), norm_gain)
+
+
+def final_kernel(base_a, base_b, za_ref, zb_ref, *rest):
+    out_ref = rest[-1]
     out_ref[0] = (base_a[...] + za_ref[...]).astype(BF16)
     out_ref[1] = (base_b[...] + zb_ref[...]).astype(BF16)
 
 
-def final_call(base_a, base_b, za, zb):
-    half, hidden = za.shape
-    rows = 128
+def final_call(part, base_a, base_b, za, zb, so_far):
+    size, hidden = za.shape
+    rows = 64
+    first = part * (size // rows)
     block = pl.BlockSpec((rows, hidden), lambda i: (i, 0))
-    out = pl.pallas_call(
+    base = pl.BlockSpec((rows, hidden), lambda i: (i + first, 0))
+    more = [] if so_far is None else [so_far]
+    return pl.pallas_call(
         final_kernel,
-        grid=(half // rows,),
-        out_shape=jax.ShapeDtypeStruct((2, half, hidden), BF16),
-        in_specs=[block] * 4,
-        out_specs=pl.BlockSpec((2, rows, hidden), lambda i: (0, i, 0)),
+        grid=(size // rows,),
+        out_shape=jax.ShapeDtypeStruct((2, 2 * size, hidden), BF16),
+        in_specs=[base] * 2 + [block] * 2 + [pl.BlockSpec(memory_space=pl.ANY)] * len(more),
+        out_specs=pl.BlockSpec((2, rows, hidden), lambda i: (0, i + first, 0)),
+        input_output_aliases={4: 0} if more else {},
         compiler_params=pltpu.CompilerParams(dimension_semantics=("arbitrary",)),
-        cost_estimate=pl.CostEstimate(flops=2 * half * hidden, transcendentals=0, bytes_accessed=20 * half * hidden),
+        cost_estimate=pl.CostEstimate(flops=4 * size * hidden, transcendentals=0, bytes_accessed=20 * size * hidden),
         name="final",
-    )(base_a, base_b, za, zb)
-    return out.reshape(2 * half, hidden)
+    )(base_a, base_b, za, zb, *more)
 
 
 def shared_expert(normed, w_sgate, s_gate, s_up, s_down):
@@ -345,7 +349,7 @@
     sibling = [(i, i ^ 1) for i in range(group_size)]
 
     def block(hidden_in, topk_idx, norm_gain, w_router, w_sgate, s_gate, s_up, s_down, w_gate, w_up, w_down):
-        tok_dev, _ = hidden_in.shape
+        tok_dev, hidden = hidden_in.shape
         top_k = topk_idx.shape[1]
         experts = w_router.shape[1]
         slots_dev = w_gate.shape[0]
@@ -381,8 +385,8 @@
         t_r1, t_l1 = go_right(table), go_left(table)
         t_far = lax.ppermute(table, 'ep', far)
 
+        hb_r1, ha_l1 = go_right(hb), go_left(ha)
         ha_r2, hb_l2 = go_right(ha_r1), go_left(hb_l1)
-        hb_r1, ha_l1 = go_right(after(hb, ha_r1)), go_left(after(ha, hb_l1))
 
         steps = jnp.arange(group_size // cores)
         rel = cores * ((chip + steps) % (group_size // cores))
@@ -394,21 +398,25 @@
         def routes(v, row_max):
             return lists[v, :, :row_max], glists[v, :, :row_max], kept[v]
 
-        d_a0, d_a1, d_b0, d_b1 = expert_call(routes(1, 2 * local_max), ha_r1, hb_l1, own_w, sib_w, ha, 2 * local_max, 4)
-        d_a0, d_b0 = go_left(d_a0), go_right(d_b0)
-        y2a, y2b = expert_call(routes(2, local_max), ha_r2, hb_l2, own_w, sib_w, d_a1, local_max, 2)
-        p_ra, p_lb = go_right(y2a), go_left(y2b)
-        d_a1, d_b1 = go_left(d_a1), go_right(d_b1)
-        y1a, y3b = expert_call(routes(3, 2 * local_max), ha_l1, hb_r1, own_w, sib_w, y2a, 2 * local_max, 2)
-        y0a, y0b = expert_call(routes(0, local_max), ha, hb, own_w, sib_w, y3b, local_max, 2)
-        p_ra, p_lb = after(p_ra, y0a), after(p_lb, y0b)
-        z_a, z_b = go_right(y1a + p_ra), go_left(y3b + p_lb)
+        d_a, d_b = expert_call(routes(1, 2 * local_max), ha_r1, hb_l1, own_w, sib_w, ha, 2 * local_max, 2)
+        d_dep, d_a, d_b = d_a, go_left(d_a), go_right(d_b)
+        y2 = expert_call(routes(2, local_max), ha_r2, hb_l2, own_w, sib_w, d_dep, local_max, 4)
+        p = [go_right(y2[0]), go_left(y2[2])]
+        p += [go_right(y2[1]), go_left(y2[3])]
+        y1 = expert_call(routes(3, 2 * local_max), ha_l1, hb_r1, own_w, sib_w, y2[0], 2 * local_max, 4)
+        y0 = expert_call(routes(0, local_max), ha, hb, own_w, sib_w, y1[0], local_max, 2)
+        z, last = [], (y0[0],)
+        for i in range(2):
+            add_a, add_b = y1[i] + after(p[2 * i], *last), y1[2 + i] + after(p[2 * i + 1], *last)
+            last = (add_a, add_b)
+            z.append((go_right(add_a), go_left(add_b)))
         base = []
-        for i, (h, y0) in enumerate(((ha, y0a), (hb, y0b))):
-            shared_val = shared_expert(after(h, y0a), w_sgate, s_gate, s_up, s_down)
-            base.append(hidden_in[i * half:(i + 1) * half].astype(F32) + shared_val + y0)
-        d_a, d_b = jnp.concatenate([d_a0, d_a1], axis=0), jnp.concatenate([d_b0, d_b1], axis=0)
-        return final_call(base[0] + d_a, base[1] + d_b, z_a, z_b)
+        for i, (h, y, d) in enumerate(((ha, y0[0], d_a), (hb, y0[1], d_b))):
+            shared_val = shared_expert(after(h, y), w_sgate, s_gate, s_up, s_down)
+            base.append(hidden_in[i * half:(i + 1) * half].astype(F32) + shared_val + y + d)
+        out = final_call(0, base[0], base[1], *z[0], None)
+        out = final_call(1, base[0], base[1], *z[1], out)
+        return out.reshape(tok_dev, hidden)
 
     row_spec = P(('dp', 'ep'), None)
     full_spec = P(None, None)

time: 478 us -> 372 us (0.78)
  waiting for transfers between devices: 204 us -> 102 us
    ppermute x8 -> x9, waiting for transfers between devices: 115 us -> 22.9 us  [go_left(): return lax.ppermute(v, 'ep', left)]
    ppermute x8 -> x9, waiting for transfers between devices: 85.2 us -> 77.6 us  [go_right(): return lax.ppermute(v, 'ep', right)]
    ppermute x8 -> x9, starting transfers between devices: 7.02 us -> 2.06 us  [go_right(): return lax.ppermute(v, 'ep', right)]
    ppermute x8 -> x9, starting transfers between devices: 32.1 us -> 35.1 us  [go_left(): return lax.ppermute(v, 'ep', left)]
    add x2 -> x4, other arithmetic: 8.39 us -> 10 us  [the longest x2 5.71 us: block(): y1[i] + after(p[2 * i], *last)]
  transfers between devices with their start and end apart: 21 -> 23, of which waited for: 8 -> 11; matrix products, arithmetic and copies ran while one was open for 10% -> 13% of each run, Pallas kernels for 26% -> 45%
where the time goes in v3:
time: 372 us; the launch traced here: 371 us
  Pallas kernels  175 us (47%)
  waiting for transfers between devices  102 us (27%)
  starting transfers between devices  40.9 us (11%)
  matrix products  35.3 us (9%)
  other arithmetic  11.3 us (3%)
  local copies, waits for them, and re-layouts  5.24 us (1%)
    pallas_call x4, Pallas kernels, expert_call(): pl.pallas_call(functools.partial(expert_kernel, pieces, classes, slots_de...  147 us
    ppermute x9, waiting for transfers between devices, go_right(): return lax.ppermute(v, 'ep', right)  77.6 us
    ppermute x9, starting transfers between devices, go_left(): return lax.ppermute(v, 'ep', left)  35.1 us
    ppermute x9, waiting for transfers between devices, go_left(): return lax.ppermute(v, 'ep', left)  22.9 us
    dot_general x2, matrix products, shared_expert(): shared_val = jnp.dot(shared_act, s_down, preferred_element_type=F32)  22.2 us
    pallas_call x1, Pallas kernels, route_call(): pl.pallas_call(functools.partial(route_kernel, (top_k, slots_dev, capacit...  14.9 us
    pallas_call x2, Pallas kernels, final_call(): pl.pallas_call(final_kernel, grid=(size // rows,), out_shape=jax.ShapeDty...  8.94 us
    dot_general x2, matrix products, shared_expert(): jnp.dot(normed, s_gate, preferred_element_type=F32)  7.93 us
  transfers between devices with their start and end apart: 23, of which 11 were waited for; matrix products, arithmetic and copies ran while one was open for 13% of the time, Pallas kernels for 45%

profile of v3, /device:TPU:88, one launch (start us, length us, event | category | flops | bytes accessed | tf_op | source)
XLA Modules:
  0.0 370.6 jit_solution(6240847758239393662)
XLA Ops:
  0.0 4.7 %norm.1 = (bf16[512,1536]{1,0:T(8,128)(2,1)}, bf16[512,1536]{1,0:T(8,128)(2,1)}) custom-call(bf16[2,512,1536]{2,1,0:T(8,128)(2,1)} %bitcast.48, bf16[1536]{0:T(1024)(128)(2,1)} %gain_ref.1), custom_call_target="tpu_custom_call" | custom-call | flops 6291456 | bytes 6291456 | tf_op jit(solution)/shard_map/norm/pallas_call | solution.py:29
  4.7 2.1 fusion.14
  6.8 0.6 fusion.13
  7.6 0.4 select_reduce_fusion
  8.1 1.1 collective-permute-done
  9.9 1.7 collective-permute-start.3
  11.6 3.0 collective-permute-start.2
  14.6 1.1 collective-permute-done.3.prev_ref
  15.8 2.4 collective-permute-start.1
  18.4 0.8 collective-permute-start.11
  19.1 1.5 collective-permute-done.1.next_ref
  20.8 0.6 pad_add_fusion.1.ids_ref
  21.4 14.9 %route.1 = (s32[4,16,8,384]{3,2,1,0:T(8,128)}, f32[4,16,8,384]{3,2,1,0:T(8,128)}, f32[4,16,128]{2,1,0:T(8,128)}) custom-call(s32[10]{0:T(128)} %pad_add_fusion.1.ids_ref, f32[16,1024]{1,0:T(8,128)} %copy-done.10, f32[16,1024]{1,0:T(8,128)} %copy-done.14, f32[16,1024]{1,0:T(8,128)} %copy-done.13, f32[16,1024]{1,0:T(8,128)} %copy-done.12), custom_call_target="tpu_custom_call" | custom-call | flops 1000000 | bytes 2000000 | tf_op jit(solution)/shard_map/route/pallas_call | solution.py:169
  36.3 1.4 copy.29
  37.8 16.7 %collective-permute-done.11.refs_4_ = bf16[512,1536]{1,0:T(8,128)(2,1)} collective-permute-done((bf16[512,1536]{1,0:T(8,128)(2,1)}, bf16[512,1536]{1,0:T(8,128)(2,1)}, u32[]{:S(2)}, u32[]{:S(2)}) %collective-permute-start.11) | collective-permute-done | bytes 1572896 | tf_op jit(solution)/shard_map/ppermute | solution.py:365
  54.5 2.7 collective-permute-start.12
  57.5 0.6 slice_bitcast_fusion.7
  58.1 0.6 slice_bitcast_fusion.6
  58.7 0.6 slice_bitcast_fusion.5
  59.4 3.5 collective-permute-start.7
  62.9 0.7 slice_reduce_fusion.1
  63.8 0.6 slice_bitcast_fusion.4
  64.7 37.6 %experts.4 = (f32[512,1536]{1,0:T(8,128)}, f32[512,1536]{1,0:T(8,128)}) custom-call(s32[16,384]{1,0:T(8,128)} %get-tuple-element.66.refs_0_, f32[16,384]{1,0:T(8,128)} %get-tuple-element.64.refs_1_, s32[16]{0:T(128)} %get-tuple-element.58.refs_2_, bf16[512,1536]{1,0:T(8,128)(2,1)} %collective-permute-done.9.refs_3_, ...), custom_call_target="tpu_custom_call" | custom-call | flops 1000000 | bytes 75497472 | tf_op jit(solution)/shard_map/experts/pallas_call | solution.py:327
  102.3 35.7 %experts.5 = (f32[256,1536]{1,0:T(8,128)}, f32[256,1536]{1,0:T(8,128)}, f32[256,1536]{1,0:T(8,128)}, f32[256,1536]{1,0:T(8,128)}) custom-call(s32[16,192]{1,0:T(8,128)} %get-tuple-element.69.refs_0_, f32[16,192]{1,0:T(8,128)} %get-tuple-element.67.refs_1_, s32[16]{0:T(128)} %get-tuple-element.57.refs_2_, bf16[512,1536]{1,0:T(8,128)(2,1)} %collective-permute-done.10.refs_3_, ...), custom_call_target="tpu_custom_call" | custom-call | flops 1000000 | bytes 75497472 | tf_op jit(solution)/shard_map/experts/pallas_call | solution.py:327
  138.0 13.1 %collective-permute-start.17 = (f32[256,1536]{1,0:T(8,128)}, f32[256,1536]{1,0:T(8,128)}, u32[]{:S(2)}, u32[]{:S(2)}) collective-permute-start(f32[256,1536]{1,0:T(8,128)} %get-tuple-element.51), channel_id=1, source_target_pairs={{0,6},{1,7},{2,0},{3,1},{4,2},{5,3},{6,4},{7,5},{8,14},{9,15},{10,... | collective-permute-start | bytes 4718600 | tf_op jit(solution)/shard_map/ppermute | solution.py:365
  151.2 3.2 collective-permute-start.13
  154.7 35.4 %experts.6 = (f32[256,1536]{1,0:T(8,128)}, f32[256,1536]{1,0:T(8,128)}, f32[256,1536]{1,0:T(8,128)}, f32[256,1536]{1,0:T(8,128)}) custom-call(s32[16,384]{1,0:T(8,128)} %get-tuple-element.65.refs_0_, f32[16,384]{1,0:T(8,128)} %get-tuple-element.63.refs_1_, s32[16]{0:T(128)} %get-tuple-element.59.refs_2_, bf16[512,1536]{1,0:T(8,128)(2,1)} %collective-permute-done.7.refs_3_, ...), custom_call_target="tpu_custom_call" | custom-call | flops 1000000 | bytes 75497472 | tf_op jit(solution)/shard_map/experts/pallas_call | solution.py:327
  190.2 38.2 %experts.7 = (f32[512,1536]{1,0:T(8,128)}, f32[512,1536]{1,0:T(8,128)}) custom-call(s32[16,192]{1,0:T(8,128)} %get-tuple-element.70.refs_0_, f32[16,192]{1,0:T(8,128)} %get-tuple-element.68.refs_1_, s32[16]{0:T(128)} %get-tuple-element.60.refs_2_, bf16[512,1536]{1,0:T(8,128)(2,1)} %get-tuple-element.43.refs_11_.refs_3_, ...), custom_call_target="tpu_custom_call" | custom-call | flops 1000000 | bytes 75497472 | tf_op jit(solution)/shard_map/experts/pallas_call | solution.py:327
  228.4 0.5 fusion.15
  228.9 3.0 collective-permute-start.19
  231.9 1.9 fusion.17
  233.8 3.2 fusion.16
  237.1 4.7 %fusion.18 = f32[512,1024]{1,0:T(8,128)} fusion(bf16[512,1536]{1,0:T(8,128)(2,1)} %get-tuple-element.45.refs_4_, bf16[1536,1024]{1,0:T(8,128)(2,1)S(1)} %copy-done.17), kind=kOutput, calls=%fused_computation.56 | convolution fusion | flops 1610612736 | bytes 6815744 | tf_op jit(solution)/shard_map/dot_general | solution.py:68
  241.8 48.5 %collective-permute-done.16 = f32[256,1536]{1,0:T(8,128)} collective-permute-done((f32[256,1536]{1,0:T(8,128)}, f32[256,1536]{1,0:T(8,128)}, u32[]{:S(2)}, u32[]{:S(2)}) %collective-permute-start.16) | collective-permute-done | bytes 1572896 | tf_op jit(solution)/shard_map/ppermute | solution.py:362
  290.3 2.8 add.126
  293.1 2.9 add.127
  296.0 3.2 collective-permute-start.22
  299.2 2.9 add.128
  302.2 1.4 add.129
  303.6 3.2 collective-permute-start.20
  306.8 11.3 %fusion.3.base_b = f32[512,1536]{1,0:T(8,128)} fusion(f32[512,1536]{1,0:T(8,128)} %collective-permute-done.14, f32[512,1536]{1,0:T(8,128)} %get-tuple-element.44, bf16[1024,1536]{1,0:T(8,128)(2,1)} %param.18, f32[512]{0:T(512)S(1)} %add_divide_fusion, bf16[1024,1536]{1,0:T(8,128)(2,1)} %param.11, f32[512,1024]{1,0:T(8,128)} %fusion.18, ...), kind=kOutput, calls=%fused_computation.5 | convolution fusion | flops 3228303360 | bytes 20973568 | tf_op jit(solution)/shard_map/dot_general | solution.py:70
  318.1 11.0 %fusion.5.base_a = f32[512,1536]{1,0:T(8,128)} fusion(f32[512,1536]{1,0:T(8,128)} %collective-permute-done.13, f32[512,1536]{1,0:T(8,128)} %get-tuple-element.42, bf16[1024,1536]{1,0:T(8,128)(2,1)} %param.18, f32[512]{0:T(512)S(1)} %add_divide_fusion.1, bf16[1024,1536]{1,0:T(8,128)(2,1)} %param.11, f32[512,1024]{1,0:T(8,128)} %fusion.16, ...), kind=kOutput, calls=%fused_computation.7 | convolution fusion | flops 3228303360 | bytes 20973568 | tf_op jit(solution)/shard_map/dot_general | solution.py:70
  329.0 2.8 collective-permute-done.21.za_ref
  331.8 2.5 collective-permute-done.22.zb_ref
  334.3 4.5 %final.2.rest_0_ = bf16[2,512,1536]{2,1,0:T(8,128)(2,1)} custom-call(f32[512,1536]{1,0:T(8,128)} %fusion.5.base_a, f32[512,1536]{1,0:T(8,128)} %fusion.3.base_b, f32[256,1536]{1,0:T(8,128)} %collective-permute-done.21.za_ref, f32[256,1536]{1,0:T(8,128)} %collective-permute-done.22.zb_ref), custom_call_target="tpu_custom_call" | custom-call | flops 1572864 | bytes 7864320 | tf_op jit(solution)/shard_map/final/pallas_call | solution.py:54
  338.8 25.1 %collective-permute-done.18.za_ref = f32[256,1536]{1,0:T(8,128)} collective-permute-done((f32[256,1536]{1,0:T(8,128)}, f32[256,1536]{1,0:T(8,128)}, u32[]{:S(2)}, u32[]{:S(2)}) %collective-permute-start.18) | collective-permute-done | bytes 1572896 | tf_op jit(solution)/shard_map/ppermute | solution.py:362
  363.9 2.2 collective-permute-done.20.zb_ref
  366.1 4.5 %final.3 = bf16[2,512,1536]{2,1,0:T(8,128)(2,1)} custom-call(f32[512,1536]{1,0:T(8,128)} %fusion.5.base_a, f32[512,1536]{1,0:T(8,128)} %fusion.3.base_b, f32[256,1536]{1,0:T(8,128)} %collective-permute-done.18.za_ref, f32[256,1536]{1,0:T(8,128)} %collective-permute-done.20.zb_ref, bf16[2,512,1536]{2,1,0:T(8,128)(2,1)} %final.2.rest_0_), custom_call_target="tpu_custom_call", output_to_operand_aliasing={{}: (4, {})} | custom-call | flops 1572864 | bytes 7864320 | tf_op jit(solution)/shard_map/final/pallas_call | solution.py:54
  (79 shorter events, 2.6 us)
Async XLA Ops:
  0.0 4.7 %copy-start = (bf16[1536,64]{0,1:T(8,128)(2,1)S(1)}, bf16[1536,64]{0,1:T(8,128)(2,1)}, u32[]{:S(2)}) copy-start(bf16[1536,64]{0,1:T(8,128)(2,1)} %param.14) | copy-start | bytes 589828
  4.7 2.1 copy-start.2
  4.7 2.9 copy-start.11
  7.9 1.3 collective-permute-start
  9.2 50.2 %collective-permute-start.4 = (bf16[8,1536,512]{2,1,0:T(8,128)(2,1)}, bf16[8,1536,512]{2,1,0:T(8,128)(2,1)}, u32[]{:S(2)}, u32[]{:S(2)}) collective-permute-start(bf16[8,1536,512]{2,1,0:T(8,128)(2,1)} %refs_5_.7), channel_id=1, source_target_pairs={{0,1},{1,0},{2,3},{3,2},{4,5},{5,4},{6,7},{7,6},{8,9},{9,8},{10,11... | collective-permute-start | bytes 37748744 | tf_op jit(solution)/shard_map/ppermute | solution.py:384
  9.4 50.0 %collective-permute-start.5 = (bf16[8,1536,512]{2,1,0:T(8,128)(2,1)}, bf16[8,1536,512]{2,1,0:T(8,128)(2,1)}, u32[]{:S(2)}, u32[]{:S(2)}) collective-permute-start(bf16[8,1536,512]{2,1,0:T(8,128)(2,1)} %refs_6_.7), channel_id=1, source_target_pairs={{0,1},{1,0},{2,3},{3,2},{4,5},{5,4},{6,7},{7,6},{8,9},{9,8},{10,11... | collective-permute-start | bytes 37748744 | tf_op jit(solution)/shard_map/ppermute | solution.py:384
  9.7 55.0 %collective-permute-start.6 = (bf16[8,512,1536]{2,1,0:T(8,128)(2,1)}, bf16[8,512,1536]{2,1,0:T(8,128)(2,1)}, u32[]{:S(2)}, u32[]{:S(2)}) collective-permute-start(bf16[8,512,1536]{2,1,0:T(8,128)(2,1)} %refs_7_.7), channel_id=1, source_target_pairs={{0,1},{1,0},{2,3},{3,2},{4,5},{5,4},{6,7},{7,6},{8,9},{9,8},{10,11... | collective-permute-start | bytes 37748744 | tf_op jit(solution)/shard_map/ppermute | solution.py:384
  9.9 11.5 %copy-start.10 = (f32[16,1024]{1,0:T(8,128)}, f32[16,1024]{1,0:T(8,128)S(1)}, u32[]{:S(2)}) copy-start(f32[16,1024]{1,0:T(8,128)S(1)} %pad_maximum_fusion.1.own_ref) | copy-start | bytes 196612
  9.9 5.9 %collective-permute-start.3 = (f32[16,1024]{1,0:T(8,128)S(1)}, f32[16,1024]{1,0:T(8,128)S(1)}, u32[]{:S(2)}, u32[]{:S(2)}) collective-permute-start(f32[16,1024]{1,0:T(8,128)S(1)} %pad_maximum_fusion.1.own_ref), channel_id=1, source_target_pairs={{0,2},{1,3},{2,4},{3,5},{4,6},{5,7},{6,0},{7,1},{8,10},{9,11},{10,... | collective-permute-start | bytes 196616 | tf_op jit(solution)/shard_map/ppermute | solution.py:362
  11.6 6.7 %collective-permute-start.2 = (f32[16,1024]{1,0:T(8,128)S(1)}, f32[16,1024]{1,0:T(8,128)S(1)}, u32[]{:S(2)}, u32[]{:S(2)}) collective-permute-start(f32[16,1024]{1,0:T(8,128)S(1)} %pad_maximum_fusion.1.own_ref), channel_id=1, source_target_pairs={{0,4},{1,5},{2,6},{3,7},{4,0},{5,1},{6,2},{7,3},{8,12},{9,13},{10,... | collective-permute-start | bytes 196616 | tf_op jit(solution)/shard_map/ppermute | solution.py:386
  15.8 5.6 %copy-start.12 = (f32[16,1024]{1,0:T(8,128)}, f32[16,1024]{1,0:T(8,128)S(1)}, u32[]{:S(2)}) copy-start(f32[16,1024]{1,0:T(8,128)S(1)} %collective-permute-done.3.prev_ref) | copy-start | bytes 196612
  15.8 4.8 %collective-permute-start.1 = (f32[16,1024]{1,0:T(8,128)S(1)}, f32[16,1024]{1,0:T(8,128)S(1)}, u32[]{:S(2)}, u32[]{:S(2)}) collective-permute-start(f32[16,1024]{1,0:T(8,128)S(1)} %pad_maximum_fusion.1.own_ref), channel_id=1, source_target_pairs={{0,6},{1,7},{2,0},{3,1},{4,2},{5,3},{6,4},{7,5},{8,14},{9,15},{10,... | collective-permute-start | bytes 196616 | tf_op jit(solution)/shard_map/ppermute | solution.py:365
  18.4 3.1 copy-start.13
  18.4 36.1 %collective-permute-start.11 = (bf16[512,1536]{1,0:T(8,128)(2,1)}, bf16[512,1536]{1,0:T(8,128)(2,1)}, u32[]{:S(2)}, u32[]{:S(2)}) collective-permute-start(bf16[512,1536]{1,0:T(8,128)(2,1)} %get-tuple-element.45.refs_4_), channel_id=1, source_target_pairs={{0,6},{1,7},{2,0},{3,1},{4,2},{5,3},{6,4},{7,5},{8,14},{9,15},{10,... | collective-permute-start | bytes 4718600 | tf_op jit(solution)/shard_map/ppermute | solution.py:365
  20.6 0.8 copy-start.14
  20.6 36.5 %collective-permute-start.9 = (bf16[512,1536]{1,0:T(8,128)(2,1)S(1)}, bf16[512,1536]{1,0:T(8,128)(2,1)}, u32[]{:S(2)}, u32[]{:S(2)}) collective-permute-start(bf16[512,1536]{1,0:T(8,128)(2,1)S(1)} %copy-done.2), channel_id=1, source_target_pairs={{0,2},{1,3},{2,4},{3,5},{4,6},{5,7},{6,0},{7,1},{8,10},{9,11},{10,... | collective-permute-start | bytes 4718600 | tf_op jit(solution)/shard_map/ppermute | solution.py:362
  36.3 20.8 %copy-start.6 = (s32[4,16,8,384]{3,2,1,0:T(8,128)S(1)}, s32[4,16,8,384]{3,2,1,0:T(8,128)}, u32[]{:S(2)}) copy-start(s32[4,16,8,384]{3,2,1,0:T(8,128)} %get-tuple-element.33) | copy-start | bytes 2359300
  36.3 21.0 %copy-start.5 = (f32[4,16,8,384]{3,2,1,0:T(8,128)S(1)}, f32[4,16,8,384]{3,2,1,0:T(8,128)}, u32[]{:S(2)}) copy-start(f32[4,16,8,384]{3,2,1,0:T(8,128)} %get-tuple-element.34) | copy-start | bytes 2359300
  37.8 21.0 %copy-start.15 = (f32[4,16,128]{2,1,0:T(8,128)S(1)}, f32[4,16,128]{2,1,0:T(8,128)}, u32[]{:S(2)}) copy-start(f32[4,16,128]{2,1,0:T(8,128)} %get-tuple-element.35) | copy-start | bytes 98308
  54.5 47.8 %collective-permute-start.12 = (bf16[512,1536]{1,0:T(8,128)(2,1)}, bf16[512,1536]{1,0:T(8,128)(2,1)}, u32[]{:S(2)}, u32[]{:S(2)}) collective-permute-start(bf16[512,1536]{1,0:T(8,128)(2,1)} %collective-permute-done.11.refs_4_), channel_id=1, source_target_pairs={{0,6},{1,7},{2,0},{3,1},{4,2},{5,3},{6,4},{7,5},{8,14},{9,15},{10,... | collective-permute-start | bytes 4718600 | tf_op jit(solution)/shard_map/ppermute | solution.py:365
  57.2 45.1 %collective-permute-start.10 = (bf16[512,1536]{1,0:T(8,128)(2,1)}, bf16[512,1536]{1,0:T(8,128)(2,1)}, u32[]{:S(2)}, u32[]{:S(2)}) collective-permute-start(bf16[512,1536]{1,0:T(8,128)(2,1)} %collective-permute-done.9.refs_3_), channel_id=1, source_target_pairs={{0,2},{1,3},{2,4},{3,5},{4,6},{5,7},{6,0},{7,1},{8,10},{9,11},{10,... | collective-permute-start | bytes 4718600 | tf_op jit(solution)/shard_map/ppermute | solution.py:362
  59.4 95.0 %collective-permute-start.8 = (bf16[512,1536]{1,0:T(8,128)(2,1)}, bf16[512,1536]{1,0:T(8,128)(2,1)}, u32[]{:S(2)}, u32[]{:S(2)}) collective-permute-start(bf16[512,1536]{1,0:T(8,128)(2,1)} %get-tuple-element.45.refs_4_), channel_id=1, source_target_pairs={{0,2},{1,3},{2,4},{3,5},{4,6},{5,7},{6,0},{7,1},{8,10},{9,11},{10,... | collective-permute-start | bytes 4718600 | tf_op jit(solution)/shard_map/ppermute | solution.py:362
  59.4 95.0 %collective-permute-start.7 = (bf16[512,1536]{1,0:T(8,128)(2,1)S(1)}, bf16[512,1536]{1,0:T(8,128)(2,1)}, u32[]{:S(2)}, u32[]{:S(2)}) collective-permute-start(bf16[512,1536]{1,0:T(8,128)(2,1)S(1)} %copy-done.2), channel_id=1, source_target_pairs={{0,6},{1,7},{2,0},{3,1},{4,2},{5,3},{6,4},{7,5},{8,14},{9,15},{10,... | collective-permute-start | bytes 4718600 | tf_op jit(solution)/shard_map/ppermute | solution.py:365
  138.0 90.9 %collective-permute-start.17 = (f32[256,1536]{1,0:T(8,128)}, f32[256,1536]{1,0:T(8,128)}, u32[]{:S(2)}, u32[]{:S(2)}) collective-permute-start(f32[256,1536]{1,0:T(8,128)} %get-tuple-element.51), channel_id=1, source_target_pairs={{0,6},{1,7},{2,0},{3,1},{4,2},{5,3},{6,4},{7,5},{8,14},{9,15},{10,... | collective-permute-start | bytes 4718600 | tf_op jit(solution)/shard_map/ppermute | solution.py:365
  151.2 152.4 %collective-permute-start.14 = (f32[512,1536]{1,0:T(8,128)}, f32[512,1536]{1,0:T(8,128)}, u32[]{:S(2)}, u32[]{:S(2)}) collective-permute-start(f32[512,1536]{1,0:T(8,128)} %get-tuple-element.46), channel_id=1, source_target_pairs={{0,2},{1,3},{2,4},{3,5},{4,6},{5,7},{6,0},{7,1},{8,10},{9,11},{10,... | collective-permute-start | bytes 9437192 | tf_op jit(solution)/shard_map/ppermute | solution.py:362
  151.2 166.9 %collective-permute-start.13 = (f32[512,1536]{1,0:T(8,128)}, f32[512,1536]{1,0:T(8,128)}, u32[]{:S(2)}, u32[]{:S(2)}) collective-permute-start(f32[512,1536]{1,0:T(8,128)} %get-tuple-element.39.refs_11_), channel_id=1, source_target_pairs={{0,6},{1,7},{2,0},{3,1},{4,2},{5,3},{6,4},{7,5},{8,14},{9,15},{10,... | collective-permute-start | bytes 9437192 | tf_op jit(solution)/shard_map/ppermute | solution.py:365
  154.4 144.9 %collective-permute-start.15 = (f32[256,1536]{1,0:T(8,128)}, f32[256,1536]{1,0:T(8,128)}, u32[]{:S(2)}, u32[]{:S(2)}) collective-permute-start(f32[256,1536]{1,0:T(8,128)} %get-tuple-element.48), channel_id=1, source_target_pairs={{0,2},{1,3},{2,4},{3,5},{4,6},{5,7},{6,0},{7,1},{8,10},{9,11},{10,... | collective-permute-start | bytes 4718600 | tf_op jit(solution)/shard_map/ppermute | solution.py:362
  154.4 135.9 %collective-permute-start.16 = (f32[256,1536]{1,0:T(8,128)}, f32[256,1536]{1,0:T(8,128)}, u32[]{:S(2)}, u32[]{:S(2)}) collective-permute-start(f32[256,1536]{1,0:T(8,128)} %get-tuple-element.40.refs_11_), channel_id=1, source_target_pairs={{0,2},{1,3},{2,4},{3,5},{4,6},{5,7},{6,0},{7,1},{8,10},{9,11},{10,... | collective-permute-start | bytes 4718600 | tf_op jit(solution)/shard_map/ppermute | solution.py:362
  190.1 38.3 %copy-start.3 = (bf16[512,1536]{1,0:T(8,128)(2,1)S(1)}, bf16[512,1536]{1,0:T(8,128)(2,1)}, u32[]{:S(2)}) copy-start(bf16[512,1536]{1,0:T(8,128)(2,1)} %get-tuple-element.43.refs_11_.refs_3_) | copy-start | bytes 4718596
  190.2 38.3 %copy-start.16 = (bf16[1536,1]{0,1:T(2,128)(2,1)S(1)}, bf16[1536,1]{0,1:T(2,128)(2,1)}, u32[]{:S(2)}) copy-start(bf16[1536,1]{0,1:T(2,128)(2,1)} %param.15) | copy-start | bytes 9220
  228.4 5.4 %copy-start.17 = (bf16[1536,1024]{1,0:T(8,128)(2,1)S(1)}, bf16[1536,1024]{1,0:T(8,128)(2,1)}, u32[]{:S(2)}) copy-start(bf16[1536,1024]{1,0:T(8,128)(2,1)} %param.16) | copy-start | bytes 9437188
  228.9 67.1 %collective-permute-start.19 = (f32[256,1536]{1,0:T(8,128)}, f32[256,1536]{1,0:T(8,128)S(1)}, u32[]{:S(2)}, u32[]{:S(2)}) collective-permute-start(f32[256,1536]{1,0:T(8,128)} %get-tuple-element.55), channel_id=1, source_target_pairs={{0,6},{1,7},{2,0},{3,1},{4,2},{5,3},{6,4},{7,5},{8,14},{9,15},{10,... | collective-permute-start | bytes 4718600 | tf_op jit(solution)/shard_map/ppermute | solution.py:365
  237.1 53.2 %copy-start.4 = (f32[256,1536]{1,0:T(8,128)S(1)}, f32[256,1536]{1,0:T(8,128)}, u32[]{:S(2)}) copy-start(f32[256,1536]{1,0:T(8,128)} %get-tuple-element.41.refs_11_) | copy-start | bytes 4718596
  241.8 51.3 %copy-start.9 = (f32[256,1536]{1,0:T(8,128)S(1)}, f32[256,1536]{1,0:T(8,128)}, u32[]{:S(2)}) copy-start(f32[256,1536]{1,0:T(8,128)} %get-tuple-element.50) | copy-start | bytes 4718596
  293.1 38.8 %collective-permute-start.21 = (f32[256,1536]{1,0:T(8,128)}, f32[256,1536]{1,0:T(8,128)}, u32[]{:S(2)}, u32[]{:S(2)}) collective-permute-start(f32[256,1536]{1,0:T(8,128)} %add.126), channel_id=1, source_target_pairs={{0,2},{1,3},{2,4},{3,5},{4,6},{5,7},{6,0},{7,1},{8,10},{9,11},{10,... | collective-permute-start | bytes 4718600 | tf_op jit(solution)/shard_map/ppermute | solution.py:362
  293.1 6.2 %copy-start.8 = (f32[256,1536]{1,0:T(8,128)S(1)}, f32[256,1536]{1,0:T(8,128)}, u32[]{:S(2)}) copy-start(f32[256,1536]{1,0:T(8,128)} %get-tuple-element.47) | copy-start | bytes 4718596
  296.0 38.3 %collective-permute-start.22 = (f32[256,1536]{1,0:T(8,128)}, f32[256,1536]{1,0:T(8,128)}, u32[]{:S(2)}, u32[]{:S(2)}) collective-permute-start(f32[256,1536]{1,0:T(8,128)} %add.127), channel_id=1, source_target_pairs={{0,6},{1,7},{2,0},{3,1},{4,2},{5,3},{6,4},{7,5},{8,14},{9,15},{10,... | collective-permute-start | bytes 4718600 | tf_op jit(solution)/shard_map/ppermute | solution.py:365
  299.2 2.9 copy-start.7
  302.2 61.7 %collective-permute-start.18 = (f32[256,1536]{1,0:T(8,128)}, f32[256,1536]{1,0:T(8,128)}, u32[]{:S(2)}, u32[]{:S(2)}) collective-permute-start(f32[256,1536]{1,0:T(8,128)} %add.128), channel_id=1, source_target_pairs={{0,2},{1,3},{2,4},{3,5},{4,6},{5,7},{6,0},{7,1},{8,10},{9,11},{10,... | collective-permute-start | bytes 4718600 | tf_op jit(solution)/shard_map/ppermute | solution.py:362
  303.6 62.5 %collective-permute-start.20 = (f32[256,1536]{1,0:T(8,128)}, f32[256,1536]{1,0:T(8,128)}, u32[]{:S(2)}, u32[]{:S(2)}) collective-permute-start(f32[256,1536]{1,0:T(8,128)} %add.129), channel_id=1, source_target_pairs={{0,6},{1,7},{2,0},{3,1},{4,2},{5,3},{6,4},{7,5},{8,14},{9,15},{10,... | collective-permute-start | bytes 4718600 | tf_op jit(solution)/shard_map/ppermute | solution.py:365
  366.1 4.5 %copy-start.1 = (bf16[1536,64]{0,1:T(8,128)(2,1)S(1)}, bf16[1536,64]{0,1:T(8,128)(2,1)}, u32[]{:S(2)}) copy-start(bf16[1536,64]{0,1:T(8,128)(2,1)} %param.14) | copy-start | bytes 589828

commit v4 on v3

--- a/solution.py
+++ b/solution.py
@@ -249,12 +249,14 @@
             xs = []
             for q in range(n_src):
                 def pick(i, carry):
+                    found = []
                     for u in range(unroll):
-                        r = i * unroll + u
-                        spot = pl.ds(pl.multiple_of(lists[q][step, r] * pitch, pitch), pitch)
-                        row = pl.ds(pl.multiple_of(r * pitch, pitch), pitch)
+                        spot = pl.ds(pl.multiple_of(lists[q][step, i * unroll + u] * pitch, pitch), pitch)
+                        found += [tok_refs[q][w][spot, :] for w in range(2)]
+                    for u in range(unroll):
+                        row = pl.ds(pl.multiple_of((i * unroll + u) * pitch, pitch), pitch)
                         for w in range(2):
-                            row_refs[q][w][row, :] = tok_refs[q][w][spot, :]
+                            row_refs[q][w][row, :] = found[2 * u + w]
                     return carry
 
                 lax.fori_loop(0, rows // unroll, pick, 0)
@@ -404,18 +406,19 @@
         p = [go_right(y2[0]), go_left(y2[2])]
         p += [go_right(y2[1]), go_left(y2[3])]
         y1 = expert_call(routes(3, 2 * local_max), ha_l1, hb_r1, own_w, sib_w, y2[0], 2 * local_max, 4)
-        y0 = expert_call(routes(0, local_max), ha, hb, own_w, sib_w, y1[0], local_max, 2)
-        z, last = [], (y0[0],)
-        for i in range(2):
-            add_a, add_b = y1[i] + after(p[2 * i], *last), y1[2 + i] + after(p[2 * i + 1], *last)
-            last = (add_a, add_b)
-            z.append((go_right(add_a), go_left(add_b)))
-        base = []
-        for i, (h, y, d) in enumerate(((ha, y0[0], d_a), (hb, y0[1], d_b))):
-            shared_val = shared_expert(after(h, y), w_sgate, s_gate, s_up, s_down)
-            base.append(hidden_in[i * half:(i + 1) * half].astype(F32) + shared_val + y + d)
-        out = final_call(0, base[0], base[1], *z[0], None)
-        out = final_call(1, base[0], base[1], *z[1], out)
+        half_sums = [shared_expert(after(h, y1[0]), w_sgate, s_gate, s_up, s_down) for h in (ha, hb)]
+
+        def relay(i, *deps):
+            return y1[i] + after(p[2 * i], *deps), y1[2 + i] + after(p[2 * i + 1], *deps)
+
+        add_a, add_b = relay(0, *half_sums)
+        z0 = go_right(add_a), go_left(add_b)
+        y0 = expert_call(routes(0, local_max), ha, hb, own_w, sib_w, add_b, local_max, 2)
+        add_a, add_b = relay(1, y0[0])
+        z1 = go_right(add_a), go_left(add_b)
+        base = [hidden_in[i * half:(i + 1) * half].astype(F32) + half_sums[i] + y0[i] + d for i, d in enumerate((d_a, d_b))]
+        out = final_call(0, base[0], base[1], *z0, None)
+        out = final_call(1, base[0], base[1], *z1, out)
         return out.reshape(tok_dev, hidden)
 
     row_spec = P(('dp', 'ep'), None)

time: 372 us -> 377 us (1.013)
  other arithmetic: 11.3 us -> 25.1 us
  waiting for transfers between devices: 102 us -> 94.7 us
    ppermute x9, waiting for transfers between devices: 77.6 us -> 56.1 us  [go_right(): return lax.ppermute(v, 'ep', right)]
    ppermute x9, waiting for transfers between devices: 22.9 us -> 37.3 us  [go_left(): return lax.ppermute(v, 'ep', left)]
    ppermute x9, starting transfers between devices: 2.06 us -> 16.1 us  [go_right(): return lax.ppermute(v, 'ep', right)]
    add x4 -> x5, other arithmetic: 10 us -> 23 us  [the longest x1 11.5 us: block(): hidden_in[i * half:(i + 1) * half].astype(F32) + half_sums[i] + y0[i] + d]
    ppermute x9, starting transfers between devices: 35.1 us -> 22.9 us  [go_left(): return lax.ppermute(v, 'ep', left)]
    dot_general x2, matrix products: 22.2 us -> 17.8 us  [shared_expert(): shared_val = jnp.dot(shared_act, s_down, preferred_element_type=F32)]
  transfers between devices with their start and end apart: 23 -> 23, of which waited for: 11 -> 10; matrix products, arithmetic and copies ran while one was open for 13% -> 16% of each run, Pallas kernels for 45% -> 44%
where the time goes in v4:
time: 377 us
  Pallas kernels  176 us (47%)
  waiting for transfers between devices  94.7 us (25%)
  starting transfers between devices  42.8 us (11%)
  matrix products  33.3 us (9%)
  other arithmetic  25.1 us (7%)
  local copies, waits for them, and re-layouts  5.12 us (1%)
    pallas_call x4, Pallas kernels, expert_call(): pl.pallas_call(functools.partial(expert_kernel, pieces, classes, slots_de...  147 us
    ppermute x9, waiting for transfers between devices, go_right(): return lax.ppermute(v, 'ep', right)  56.1 us
    ppermute x9, waiting for transfers between devices, go_left(): return lax.ppermute(v, 'ep', left)  37.3 us
    ppermute x9, starting transfers between devices, go_left(): return lax.ppermute(v, 'ep', left)  22.9 us
    dot_general x2, matrix products, shared_expert(): shared_val = jnp.dot(shared_act, s_down, preferred_element_type=F32)  17.8 us
    ppermute x9, starting transfers between devices, go_right(): return lax.ppermute(v, 'ep', right)  16.1 us
    pallas_call x1, Pallas kernels, route_call(): pl.pallas_call(functools.partial(route_kernel, (top_k, slots_dev, capacit...  14.9 us
    add x1, other arithmetic, block(): hidden_in[i * half:(i + 1) * half].astype(F32) + half_sums[i] + y0[i] + d  11.5 us
  transfers between devices with their start and end apart: 23, of which 10 were waited for; matrix products, arithmetic and copies ran while one was open for 16% of the time, Pallas kernels for 44%

profile of v4, /device:TPU:88, one launch (start us, length us, event | category | flops | bytes accessed | tf_op | source)
XLA Modules:
  0.0 376.8 jit_solution(10636733502612926173)
XLA Ops:
  0.0 4.7 %norm.1 = (bf16[512,1536]{1,0:T(8,128)(2,1)}, bf16[512,1536]{1,0:T(8,128)(2,1)}) custom-call(bf16[2,512,1536]{2,1,0:T(8,128)(2,1)} %bitcast.48, bf16[1536]{0:T(1024)(128)(2,1)} %gain_ref.1), custom_call_target="tpu_custom_call" | custom-call | flops 6291456 | bytes 6291456 | tf_op jit(solution)/shard_map/norm/pallas_call | solution.py:29
  4.7 2.1 fusion.8
  8.0 1.1 collective-permute-done
  9.9 1.7 collective-permute-start.3
  11.6 3.0 collective-permute-start.2
  14.6 1.1 collective-permute-done.3.prev_ref
  15.8 2.4 collective-permute-start.1
  18.3 0.8 collective-permute-start.11
  19.1 1.5 collective-permute-done.1.next_ref
  20.8 0.7 pad_add_fusion.1.ids_ref
  21.5 14.9 %route.1 = (s32[4,16,8,384]{3,2,1,0:T(8,128)}, f32[4,16,8,384]{3,2,1,0:T(8,128)}, f32[4,16,128]{2,1,0:T(8,128)}) custom-call(s32[10]{0:T(128)} %pad_add_fusion.1.ids_ref, f32[16,1024]{1,0:T(8,128)} %copy-done.11, f32[16,1024]{1,0:T(8,128)} %copy-done.15, f32[16,1024]{1,0:T(8,128)} %copy-done.14, f32[16,1024]{1,0:T(8,128)} %copy-done.13), custom_call_target="tpu_custom_call" | custom-call | flops 1000000 | bytes 2000000 | tf_op jit(solution)/shard_map/route/pallas_call | solution.py:169
  36.4 18.0 %collective-permute-done.11.refs_4_ = bf16[512,1536]{1,0:T(8,128)(2,1)} collective-permute-done((bf16[512,1536]{1,0:T(8,128)(2,1)}, bf16[512,1536]{1,0:T(8,128)(2,1)}, u32[]{:S(2)}, u32[]{:S(2)}) %collective-permute-start.11) | collective-permute-done | bytes 1572896 | tf_op jit(solution)/shard_map/ppermute | solution.py:367
  54.6 1.7 collective-permute-done.9.refs_3_
  56.2 1.5 collective-permute-start.4
  57.7 1.5 collective-permute-start.12
  59.8 0.8 slice_convert_fusion
  60.5 1.3 copy.31
  62.3 0.7 slice_reduce_fusion.2
  63.0 0.6 slice_bitcast_fusion.9
  63.7 0.6 slice_bitcast_fusion.8
  64.3 0.6 slice_bitcast_fusion.5
  64.9 0.6 slice_bitcast_fusion.4
  65.5 37.6 %experts.4 = (f32[512,1536]{1,0:T(8,128)}, f32[512,1536]{1,0:T(8,128)}) custom-call(s32[16,384]{1,0:T(8,128)} %get-tuple-element.68.refs_0_, f32[16,384]{1,0:T(8,128)} %get-tuple-element.66.refs_1_, s32[16]{0:T(128)} %get-tuple-element.59.refs_2_, bf16[512,1536]{1,0:T(8,128)(2,1)} %collective-permute-done.9.refs_3_, ...), custom_call_target="tpu_custom_call" | custom-call | flops 1000000 | bytes 75497472 | tf_op jit(solution)/shard_map/experts/pallas_call | solution.py:329
  103.1 6.4 %collective-permute-start.14 = (f32[512,1536]{1,0:T(8,128)}, f32[512,1536]{1,0:T(8,128)}, u32[]{:S(2)}, u32[]{:S(2)}) collective-permute-start(f32[512,1536]{1,0:T(8,128)} %get-tuple-element.39.refs_11_), channel_id=1, source_target_pairs={{0,6},{1,7},{2,0},{3,1},{4,2},{5,3},{6,4},{7,5},{8,14},{9,15},{10,... | collective-permute-start | bytes 9437192 | tf_op jit(solution)/shard_map/ppermute | solution.py:367
  109.5 17.8 %collective-permute-done.12.refs_4_ = bf16[512,1536]{1,0:T(8,128)(2,1)} collective-permute-done((bf16[512,1536]{1,0:T(8,128)(2,1)}, bf16[512,1536]{1,0:T(8,128)(2,1)}, u32[]{:S(2)}, u32[]{:S(2)}) %collective-permute-start.12) | collective-permute-done | bytes 1572896 | tf_op jit(solution)/shard_map/ppermute | solution.py:367
  127.3 35.7 %experts.5 = (f32[256,1536]{1,0:T(8,128)}, f32[256,1536]{1,0:T(8,128)}, f32[256,1536]{1,0:T(8,128)}, f32[256,1536]{1,0:T(8,128)}) custom-call(s32[16,192]{1,0:T(8,128)} %get-tuple-element.71.refs_0_, f32[16,192]{1,0:T(8,128)} %get-tuple-element.69.refs_1_, s32[16]{0:T(128)} %get-tuple-element.57.refs_2_, bf16[512,1536]{1,0:T(8,128)(2,1)} %collective-permute-done.10.refs_3_, ...), custom_call_target="tpu_custom_call" | custom-call | flops 1000000 | bytes 75497472 | tf_op jit(solution)/shard_map/experts/pallas_call | solution.py:329
  163.0 9.2 %collective-permute-start.13 = (f32[256,1536]{1,0:T(8,128)}, f32[256,1536]{1,0:T(8,128)}, u32[]{:S(2)}, u32[]{:S(2)}) collective-permute-start(f32[256,1536]{1,0:T(8,128)} %get-tuple-element.44), channel_id=1, source_target_pairs={{0,6},{1,7},{2,0},{3,1},{4,2},{5,3},{6,4},{7,5},{8,14},{9,15},{10,... | collective-permute-start | bytes 4718600 | tf_op jit(solution)/shard_map/ppermute | solution.py:367
  172.3 35.5 %experts.6 = (f32[256,1536]{1,0:T(8,128)}, f32[256,1536]{1,0:T(8,128)}, f32[256,1536]{1,0:T(8,128)}, f32[256,1536]{1,0:T(8,128)}) custom-call(s32[16,384]{1,0:T(8,128)} %get-tuple-element.67.refs_0_, f32[16,384]{1,0:T(8,128)} %get-tuple-element.65.refs_1_, s32[16]{0:T(128)} %get-tuple-element.60.refs_2_, bf16[512,1536]{1,0:T(8,128)(2,1)} %collective-permute-done.4.refs_3_, ...), custom_call_target="tpu_custom_call" | custom-call | flops 1000000 | bytes 75497472 | tf_op jit(solution)/shard_map/experts/pallas_call | solution.py:329
  207.8 5.0 %fusion.10 = f32[512,1024]{1,0:T(8,128)} fusion(bf16[512,1536]{1,0:T(8,128)(2,1)S(1)} %copy-done.3, bf16[1536,1024]{1,0:T(8,128)(2,1)} %param.16), kind=kOutput, calls=%fused_computation.50 | convolution fusion | flops 1610612736 | bytes 6815744 | tf_op jit(solution)/shard_map/dot_general | solution.py:68
  213.3 8.2 %collective-permute-start.15 = (f32[512,1536]{1,0:T(8,128)}, f32[512,1536]{1,0:T(8,128)}, u32[]{:S(2)}, u32[]{:S(2)}) collective-permute-start(f32[512,1536]{1,0:T(8,128)} %get-tuple-element.49), channel_id=1, source_target_pairs={{0,2},{1,3},{2,4},{3,5},{4,6},{5,7},{6,0},{7,1},{8,10},{9,11},{10,... | collective-permute-start | bytes 9437192 | tf_op jit(solution)/shard_map/ppermute | solution.py:364
  221.6 1.9 fusion.11
  223.5 8.6 %convolution_multiply_fusion.1 = f32[512,1536]{1,0:T(8,128)} fusion(bf16[1024,1536]{1,0:T(8,128)(2,1)} %param.18, f32[512]{0:T(512)S(1)} %add_divide_fusion.1, f32[512,1024]{1,0:T(8,128)} %fusion.10, bf16[512,1536]{1,0:T(8,128)(2,1)S(1)} %copy-done.3, bf16[1536,1024]{1,0:T(8,128)(2,1)} %param.17), kind=kOutput, calls=%fused_computation.1 | convolution fusion | flops 3225157632 | bytes 13109248 | tf_op jit(solution)/shard_map/dot_general | solution.py:70
  232.1 12.6 %collective-permute-done.20 = f32[256,1536]{1,0:T(8,128)} collective-permute-done((f32[256,1536]{1,0:T(8,128)}, f32[256,1536]{1,0:T(8,128)}, u32[]{:S(2)}, u32[]{:S(2)}) %collective-permute-start.20) | collective-permute-done | bytes 1572896 | tf_op jit(solution)/shard_map/ppermute | solution.py:364
  244.7 5.5 %fusion.12 = f32[512,1024]{1,0:T(8,128)} fusion(bf16[512,1536]{1,0:T(8,128)(2,1)} %get-tuple-element.45.refs_4_, bf16[1536,1024]{1,0:T(8,128)(2,1)} %param.16), kind=kOutput, calls=%fused_computation.52 | convolution fusion | flops 1610612736 | bytes 6815744 | tf_op jit(solution)/shard_map/dot_general | solution.py:68
  250.2 9.1 %convolution_multiply_fusion = f32[512,1536]{1,0:T(8,128)} fusion(bf16[1024,1536]{1,0:T(8,128)(2,1)} %param.18, f32[512]{0:T(512)S(1)} %add_divide_fusion, f32[512,1024]{1,0:T(8,128)} %fusion.12, bf16[512,1536]{1,0:T(8,128)(2,1)} %get-tuple-element.45.refs_4_, bf16[1536,1024]{1,0:T(8,128)(2,1)} %param.17), kind=kOutput, calls=%fused_computation | convolution fusion | flops 3225157632 | bytes 13109248 | tf_op jit(solution)/shard_map/dot_general | solution.py:70
  259.4 2.9 add.129
  262.3 2.8 add.121.refs_11_
  265.1 38.2 %experts.7 = (f32[512,1536]{1,0:T(8,128)}, f32[512,1536]{1,0:T(8,128)}) custom-call(s32[16,192]{1,0:T(8,128)} %get-tuple-element.72.refs_0_, f32[16,192]{1,0:T(8,128)} %get-tuple-element.70.refs_1_, s32[16]{0:T(128)} %get-tuple-element.58.refs_2_, bf16[512,1536]{1,0:T(8,128)(2,1)} %get-tuple-element.42.refs_11_.refs_3_, ...), custom_call_target="tpu_custom_call" | custom-call | flops 1000000 | bytes 75497472 | tf_op jit(solution)/shard_map/experts/pallas_call | solution.py:329
  303.3 3.4 collective-permute-start.21
  306.7 2.9 add.127
  309.5 2.0 collective-permute-start.17
  311.5 3.0 add.128
  314.5 1.2 collective-permute-start.19
  315.7 11.5 %add_add_fusion = (f32[512,1536]{1,0:T(8,128)}, f32[512,1536]{1,0:T(8,128)}) fusion(f32[512,1536]{1,0:T(8,128)} %collective-permute-done.15, f32[512,1536]{1,0:T(8,128)} %get-tuple-element.48, f32[512,1536]{1,0:T(8,128)} %convolution_multiply_fusion, bf16[1024,1536]{1,0:T(8,128)(2,1)S(1)} %copy-done.4, f32[512,1536]{1,0:T(8,128)} %collective-permute-done.14, ...), kind=kLoop, calls=%fused_computation.2 | loop fusion | flops 6291456 | bytes 28311552 | tf_op jit(solution)/shard_map/add | solution.py:419
  327.3 18.6 %collective-permute-done.21.za_ref = f32[256,1536]{1,0:T(8,128)} collective-permute-done((f32[256,1536]{1,0:T(8,128)}, f32[256,1536]{1,0:T(8,128)}, u32[]{:S(2)}, u32[]{:S(2)}) %collective-permute-start.21) | collective-permute-done | bytes 1572896 | tf_op jit(solution)/shard_map/ppermute | solution.py:364
  345.8 4.5 %final.2.rest_0_ = bf16[2,512,1536]{2,1,0:T(8,128)(2,1)} custom-call(f32[512,1536]{1,0:T(8,128)} %get-tuple-element.64.base_a, f32[512,1536]{1,0:T(8,128)} %get-tuple-element.63.base_b, f32[256,1536]{1,0:T(8,128)} %collective-permute-done.21.za_ref, f32[256,1536]{1,0:T(8,128)} %collective-permute-done.22.zb_ref), custom_call_target="tpu_custom_call" | custom-call | flops 1572864 | bytes 7864320 | tf_op jit(solution)/shard_map/final/pallas_call | solution.py:54
  350.3 22.0 %collective-permute-done.17.za_ref = f32[256,1536]{1,0:T(8,128)} collective-permute-done((f32[256,1536]{1,0:T(8,128)}, f32[256,1536]{1,0:T(8,128)}, u32[]{:S(2)}, u32[]{:S(2)}) %collective-permute-start.17) | collective-permute-done | bytes 1572896 | tf_op jit(solution)/shard_map/ppermute | solution.py:364
  372.3 4.5 %final.3 = bf16[2,512,1536]{2,1,0:T(8,128)(2,1)} custom-call(f32[512,1536]{1,0:T(8,128)} %get-tuple-element.64.base_a, f32[512,1536]{1,0:T(8,128)} %get-tuple-element.63.base_b, f32[256,1536]{1,0:T(8,128)} %collective-permute-done.17.za_ref, f32[256,1536]{1,0:T(8,128)} %collective-permute-done.19.zb_ref, ...), custom_call_target="tpu_custom_call", output_to_operand_aliasing={{}: (4, {})} | custom-call | flops 1572864 | bytes 7864320 | tf_op jit(solution)/shard_map/final/pallas_call | solution.py:54
  (78 shorter events, 4.1 us)
Async XLA Ops:
  0.0 4.7 %copy-start = (bf16[1536,64]{0,1:T(8,128)(2,1)S(1)}, bf16[1536,64]{0,1:T(8,128)(2,1)}, u32[]{:S(2)}) copy-start(bf16[1536,64]{0,1:T(8,128)(2,1)} %param.14) | copy-start | bytes 589828
  4.7 2.1 copy-start.2
  4.7 2.9 copy-start.12
  7.9 1.3 collective-permute-start
  9.2 48.5 %collective-permute-start.6 = (bf16[8,1536,512]{2,1,0:T(8,128)(2,1)}, bf16[8,1536,512]{2,1,0:T(8,128)(2,1)}, u32[]{:S(2)}, u32[]{:S(2)}) collective-permute-start(bf16[8,1536,512]{2,1,0:T(8,128)(2,1)} %refs_5_.7), channel_id=1, source_target_pairs={{0,1},{1,0},{2,3},{3,2},{4,5},{5,4},{6,7},{7,6},{8,9},{9,8},{10,11... | collective-permute-start | bytes 37748744 | tf_op jit(solution)/shard_map/ppermute | solution.py:386
  9.4 49.8 %collective-permute-start.7 = (bf16[8,1536,512]{2,1,0:T(8,128)(2,1)}, bf16[8,1536,512]{2,1,0:T(8,128)(2,1)}, u32[]{:S(2)}, u32[]{:S(2)}) collective-permute-start(bf16[8,1536,512]{2,1,0:T(8,128)(2,1)} %refs_6_.7), channel_id=1, source_target_pairs={{0,1},{1,0},{2,3},{3,2},{4,5},{5,4},{6,7},{7,6},{8,9},{9,8},{10,11... | collective-permute-start | bytes 37748744 | tf_op jit(solution)/shard_map/ppermute | solution.py:386
  9.7 55.8 %collective-permute-start.8 = (bf16[8,512,1536]{2,1,0:T(8,128)(2,1)}, bf16[8,512,1536]{2,1,0:T(8,128)(2,1)}, u32[]{:S(2)}, u32[]{:S(2)}) collective-permute-start(bf16[8,512,1536]{2,1,0:T(8,128)(2,1)} %refs_7_.7), channel_id=1, source_target_pairs={{0,1},{1,0},{2,3},{3,2},{4,5},{5,4},{6,7},{7,6},{8,9},{9,8},{10,11... | collective-permute-start | bytes 37748744 | tf_op jit(solution)/shard_map/ppermute | solution.py:386
  9.9 11.6 %copy-start.11 = (f32[16,1024]{1,0:T(8,128)}, f32[16,1024]{1,0:T(8,128)S(1)}, u32[]{:S(2)}) copy-start(f32[16,1024]{1,0:T(8,128)S(1)} %pad_maximum_fusion.1.own_ref) | copy-start | bytes 196612
  9.9 5.9 %collective-permute-start.3 = (f32[16,1024]{1,0:T(8,128)S(1)}, f32[16,1024]{1,0:T(8,128)S(1)}, u32[]{:S(2)}, u32[]{:S(2)}) collective-permute-start(f32[16,1024]{1,0:T(8,128)S(1)} %pad_maximum_fusion.1.own_ref), channel_id=1, source_target_pairs={{0,2},{1,3},{2,4},{3,5},{4,6},{5,7},{6,0},{7,1},{8,10},{9,11},{10,... | collective-permute-start | bytes 196616 | tf_op jit(solution)/shard_map/ppermute | solution.py:364
  11.6 6.7 %collective-permute-start.2 = (f32[16,1024]{1,0:T(8,128)S(1)}, f32[16,1024]{1,0:T(8,128)S(1)}, u32[]{:S(2)}, u32[]{:S(2)}) collective-permute-start(f32[16,1024]{1,0:T(8,128)S(1)} %pad_maximum_fusion.1.own_ref), channel_id=1, source_target_pairs={{0,4},{1,5},{2,6},{3,7},{4,0},{5,1},{6,2},{7,3},{8,12},{9,13},{10,... | collective-permute-start | bytes 196616 | tf_op jit(solution)/shard_map/ppermute | solution.py:388
  15.8 5.7 %copy-start.13 = (f32[16,1024]{1,0:T(8,128)}, f32[16,1024]{1,0:T(8,128)S(1)}, u32[]{:S(2)}) copy-start(f32[16,1024]{1,0:T(8,128)S(1)} %collective-permute-done.3.prev_ref) | copy-start | bytes 196612
  15.8 4.8 %collective-permute-start.1 = (f32[16,1024]{1,0:T(8,128)S(1)}, f32[16,1024]{1,0:T(8,128)S(1)}, u32[]{:S(2)}, u32[]{:S(2)}) collective-permute-start(f32[16,1024]{1,0:T(8,128)S(1)} %pad_maximum_fusion.1.own_ref), channel_id=1, source_target_pairs={{0,6},{1,7},{2,0},{3,1},{4,2},{5,3},{6,4},{7,5},{8,14},{9,15},{10,... | collective-permute-start | bytes 196616 | tf_op jit(solution)/shard_map/ppermute | solution.py:367
  18.3 3.1 copy-start.14
  18.3 36.1 %collective-permute-start.11 = (bf16[512,1536]{1,0:T(8,128)(2,1)}, bf16[512,1536]{1,0:T(8,128)(2,1)}, u32[]{:S(2)}, u32[]{:S(2)}) collective-permute-start(bf16[512,1536]{1,0:T(8,128)(2,1)} %get-tuple-element.45.refs_4_), channel_id=1, source_target_pairs={{0,6},{1,7},{2,0},{3,1},{4,2},{5,3},{6,4},{7,5},{8,14},{9,15},{10,... | collective-permute-start | bytes 4718600 | tf_op jit(solution)/shard_map/ppermute | solution.py:367
  20.6 0.9 copy-start.15
  20.6 35.6 %collective-permute-start.9 = (bf16[512,1536]{1,0:T(8,128)(2,1)S(1)}, bf16[512,1536]{1,0:T(8,128)(2,1)}, u32[]{:S(2)}, u32[]{:S(2)}) collective-permute-start(bf16[512,1536]{1,0:T(8,128)(2,1)S(1)} %copy-done.2), channel_id=1, source_target_pairs={{0,2},{1,3},{2,4},{3,5},{4,6},{5,7},{6,0},{7,1},{8,10},{9,11},{10,... | collective-permute-start | bytes 4718600 | tf_op jit(solution)/shard_map/ppermute | solution.py:364
  36.4 25.4 %copy-start.6 = (s32[4,16,8,384]{3,2,1,0:T(8,128)S(1)}, s32[4,16,8,384]{3,2,1,0:T(8,128)}, u32[]{:S(2)}) copy-start(s32[4,16,8,384]{3,2,1,0:T(8,128)} %get-tuple-element.33) | copy-start | bytes 2359300
  36.4 25.6 %copy-start.5 = (f32[4,16,8,384]{3,2,1,0:T(8,128)S(1)}, f32[4,16,8,384]{3,2,1,0:T(8,128)}, u32[]{:S(2)}) copy-start(f32[4,16,8,384]{3,2,1,0:T(8,128)} %get-tuple-element.34) | copy-start | bytes 2359300
  54.4 117.8 %collective-permute-start.5 = (bf16[512,1536]{1,0:T(8,128)(2,1)}, bf16[512,1536]{1,0:T(8,128)(2,1)}, u32[]{:S(2)}, u32[]{:S(2)}) collective-permute-start(bf16[512,1536]{1,0:T(8,128)(2,1)} %get-tuple-element.45.refs_4_), channel_id=1, source_target_pairs={{0,2},{1,3},{2,4},{3,5},{4,6},{5,7},{6,0},{7,1},{8,10},{9,11},{10,... | collective-permute-start | bytes 4718600 | tf_op jit(solution)/shard_map/ppermute | solution.py:364
  56.2 116.0 %collective-permute-start.4 = (bf16[512,1536]{1,0:T(8,128)(2,1)S(1)}, bf16[512,1536]{1,0:T(8,128)(2,1)}, u32[]{:S(2)}, u32[]{:S(2)}) collective-permute-start(bf16[512,1536]{1,0:T(8,128)(2,1)S(1)} %copy-done.2), channel_id=1, source_target_pairs={{0,6},{1,7},{2,0},{3,1},{4,2},{5,3},{6,4},{7,5},{8,14},{9,15},{10,... | collective-permute-start | bytes 4718600 | tf_op jit(solution)/shard_map/ppermute | solution.py:367
  57.7 69.6 %collective-permute-start.12 = (bf16[512,1536]{1,0:T(8,128)(2,1)}, bf16[512,1536]{1,0:T(8,128)(2,1)}, u32[]{:S(2)}, u32[]{:S(2)}) collective-permute-start(bf16[512,1536]{1,0:T(8,128)(2,1)} %collective-permute-done.11.refs_4_), channel_id=1, source_target_pairs={{0,6},{1,7},{2,0},{3,1},{4,2},{5,3},{6,4},{7,5},{8,14},{9,15},{10,... | collective-permute-start | bytes 4718600 | tf_op jit(solution)/shard_map/ppermute | solution.py:367
  59.2 68.1 %collective-permute-start.10 = (bf16[512,1536]{1,0:T(8,128)(2,1)}, bf16[512,1536]{1,0:T(8,128)(2,1)}, u32[]{:S(2)}, u32[]{:S(2)}) collective-permute-start(bf16[512,1536]{1,0:T(8,128)(2,1)} %collective-permute-done.9.refs_3_), channel_id=1, source_target_pairs={{0,2},{1,3},{2,4},{3,5},{4,6},{5,7},{6,0},{7,1},{8,10},{9,11},{10,... | collective-permute-start | bytes 4718600 | tf_op jit(solution)/shard_map/ppermute | solution.py:364
  103.1 212.6 %collective-permute-start.14 = (f32[512,1536]{1,0:T(8,128)}, f32[512,1536]{1,0:T(8,128)}, u32[]{:S(2)}, u32[]{:S(2)}) collective-permute-start(f32[512,1536]{1,0:T(8,128)} %get-tuple-element.39.refs_11_), channel_id=1, source_target_pairs={{0,6},{1,7},{2,0},{3,1},{4,2},{5,3},{6,4},{7,5},{8,14},{9,15},{10,... | collective-permute-start | bytes 9437192 | tf_op jit(solution)/shard_map/ppermute | solution.py:367
  163.0 99.2 %collective-permute-start.13 = (f32[256,1536]{1,0:T(8,128)}, f32[256,1536]{1,0:T(8,128)}, u32[]{:S(2)}, u32[]{:S(2)}) collective-permute-start(f32[256,1536]{1,0:T(8,128)} %get-tuple-element.44), channel_id=1, source_target_pairs={{0,6},{1,7},{2,0},{3,1},{4,2},{5,3},{6,4},{7,5},{8,14},{9,15},{10,... | collective-permute-start | bytes 4718600 | tf_op jit(solution)/shard_map/ppermute | solution.py:367
  172.2 131.0 %collective-permute-start.16 = (f32[256,1536]{1,0:T(8,128)}, f32[256,1536]{1,0:T(8,128)}, u32[]{:S(2)}, u32[]{:S(2)}) collective-permute-start(f32[256,1536]{1,0:T(8,128)} %get-tuple-element.51), channel_id=1, source_target_pairs={{0,2},{1,3},{2,4},{3,5},{4,6},{5,7},{6,0},{7,1},{8,10},{9,11},{10,... | collective-permute-start | bytes 4718600 | tf_op jit(solution)/shard_map/ppermute | solution.py:364
  172.2 72.5 %collective-permute-start.20 = (f32[256,1536]{1,0:T(8,128)}, f32[256,1536]{1,0:T(8,128)}, u32[]{:S(2)}, u32[]{:S(2)}) collective-permute-start(f32[256,1536]{1,0:T(8,128)} %get-tuple-element.40.refs_11_), channel_id=1, source_target_pairs={{0,2},{1,3},{2,4},{3,5},{4,6},{5,7},{6,0},{7,1},{8,10},{9,11},{10,... | collective-permute-start | bytes 4718600 | tf_op jit(solution)/shard_map/ppermute | solution.py:364
  172.3 35.6 %copy-start.3 = (bf16[512,1536]{1,0:T(8,128)(2,1)S(1)}, bf16[512,1536]{1,0:T(8,128)(2,1)}, u32[]{:S(2)}) copy-start(bf16[512,1536]{1,0:T(8,128)(2,1)} %get-tuple-element.42.refs_11_.refs_3_) | copy-start | bytes 4718596
  207.8 5.0 %copy-start.16 = (bf16[1536,1]{0,1:T(2,128)(2,1)S(1)}, bf16[1536,1]{0,1:T(2,128)(2,1)}, u32[]{:S(2)}) copy-start(bf16[1536,1]{0,1:T(2,128)(2,1)} %param.15) | copy-start | bytes 9220
  213.3 101.2 %collective-permute-start.15 = (f32[512,1536]{1,0:T(8,128)}, f32[512,1536]{1,0:T(8,128)}, u32[]{:S(2)}, u32[]{:S(2)}) collective-permute-start(f32[512,1536]{1,0:T(8,128)} %get-tuple-element.49), channel_id=1, source_target_pairs={{0,2},{1,3},{2,4},{3,5},{4,6},{5,7},{6,0},{7,1},{8,10},{9,11},{10,... | collective-permute-start | bytes 9437192 | tf_op jit(solution)/shard_map/ppermute | solution.py:364
  244.7 58.5 %collective-permute-start.18 = (f32[256,1536]{1,0:T(8,128)}, f32[256,1536]{1,0:T(8,128)}, u32[]{:S(2)}, u32[]{:S(2)}) collective-permute-start(f32[256,1536]{1,0:T(8,128)} %get-tuple-element.54), channel_id=1, source_target_pairs={{0,6},{1,7},{2,0},{3,1},{4,2},{5,3},{6,4},{7,5},{8,14},{9,15},{10,... | collective-permute-start | bytes 4718600 | tf_op jit(solution)/shard_map/ppermute | solution.py:367
  250.2 9.1 %copy-start.10 = (f32[256,1536]{1,0:T(8,128)S(1)}, f32[256,1536]{1,0:T(8,128)}, u32[]{:S(2)}) copy-start(f32[256,1536]{1,0:T(8,128)} %get-tuple-element.41) | copy-start | bytes 4718596
  259.4 2.9 copy-start.9
  265.1 62.2 %collective-permute-start.22 = (f32[256,1536]{1,0:T(8,128)}, f32[256,1536]{1,0:T(8,128)}, u32[]{:S(2)}, u32[]{:S(2)}) collective-permute-start(f32[256,1536]{1,0:T(8,128)} %add.121.refs_11_), channel_id=1, source_target_pairs={{0,6},{1,7},{2,0},{3,1},{4,2},{5,3},{6,4},{7,5},{8,14},{9,15},{10,... | collective-permute-start | bytes 4718600 | tf_op jit(solution)/shard_map/ppermute | solution.py:367
  265.1 41.6 %copy-start.8 = (f32[256,1536]{1,0:T(8,128)S(1)}, f32[256,1536]{1,0:T(8,128)}, u32[]{:S(2)}) copy-start(f32[256,1536]{1,0:T(8,128)} %get-tuple-element.50) | copy-start | bytes 4718596
  303.3 42.6 %collective-permute-start.21 = (f32[256,1536]{1,0:T(8,128)}, f32[256,1536]{1,0:T(8,128)}, u32[]{:S(2)}, u32[]{:S(2)}) collective-permute-start(f32[256,1536]{1,0:T(8,128)} %add.129), channel_id=1, source_target_pairs={{0,2},{1,3},{2,4},{3,5},{4,6},{5,7},{6,0},{7,1},{8,10},{9,11},{10,... | collective-permute-start | bytes 4718600 | tf_op jit(solution)/shard_map/ppermute | solution.py:364
  306.7 4.9 %copy-start.7 = (f32[256,1536]{1,0:T(8,128)S(1)}, f32[256,1536]{1,0:T(8,128)}, u32[]{:S(2)}) copy-start(f32[256,1536]{1,0:T(8,128)} %get-tuple-element.53) | copy-start | bytes 4718596
  309.5 62.8 %collective-permute-start.17 = (f32[256,1536]{1,0:T(8,128)}, f32[256,1536]{1,0:T(8,128)}, u32[]{:S(2)}, u32[]{:S(2)}) collective-permute-start(f32[256,1536]{1,0:T(8,128)} %add.127), channel_id=1, source_target_pairs={{0,2},{1,3},{2,4},{3,5},{4,6},{5,7},{6,0},{7,1},{8,10},{9,11},{10,... | collective-permute-start | bytes 4718600 | tf_op jit(solution)/shard_map/ppermute | solution.py:364
  311.5 4.2 %copy-start.4 = (bf16[1024,1536]{1,0:T(8,128)(2,1)S(1)}, bf16[1024,1536]{1,0:T(8,128)(2,1)}, u32[]{:S(2)}) copy-start(bf16[1024,1536]{1,0:T(8,128)(2,1)} %param.11) | copy-start | bytes 9437188
  314.5 57.8 %collective-permute-start.19 = (f32[256,1536]{1,0:T(8,128)}, f32[256,1536]{1,0:T(8,128)}, u32[]{:S(2)}, u32[]{:S(2)}) collective-permute-start(f32[256,1536]{1,0:T(8,128)} %add.128), channel_id=1, source_target_pairs={{0,6},{1,7},{2,0},{3,1},{4,2},{5,3},{6,4},{7,5},{8,14},{9,15},{10,... | collective-permute-start | bytes 4718600 | tf_op jit(solution)/shard_map/ppermute | solution.py:367
  372.3 4.5 %copy-start.1 = (bf16[1536,64]{0,1:T(8,128)(2,1)S(1)}, bf16[1536,64]{0,1:T(8,128)(2,1)}, u32[]{:S(2)}) copy-start(bf16[1536,64]{0,1:T(8,128)(2,1)} %param.14) | copy-start | bytes 589828

commit v5 on v4

--- a/solution.py
+++ b/solution.py
@@ -44,17 +44,17 @@
     out_ref[1] = (base_b[...] + zb_ref[...]).astype(BF16)
 
 
-def final_call(part, base_a, base_b, za, zb, so_far):
-    size, hidden = za.shape
+def final_call(start, base_a, base_b, za, zb, so_far):
+    (size, hidden), half = za.shape, base_a.shape[0]
     rows = 64
-    first = part * (size // rows)
+    first = start // rows
     block = pl.BlockSpec((rows, hidden), lambda i: (i, 0))
     base = pl.BlockSpec((rows, hidden), lambda i: (i + first, 0))
     more = [] if so_far is None else [so_far]
     return pl.pallas_call(
         final_kernel,
         grid=(size // rows,),
-        out_shape=jax.ShapeDtypeStruct((2, 2 * size, hidden), BF16),
+        out_shape=jax.ShapeDtypeStruct((2, half, hidden), BF16),
         in_specs=[base] * 2 + [block] * 2 + [pl.BlockSpec(memory_space=pl.ANY)] * len(more),
         out_specs=pl.BlockSpec((2, rows, hidden), lambda i: (0, i + first, 0)),
         input_output_aliases={4: 0} if more else {},
@@ -64,11 +64,46 @@
     )(base_a, base_b, za, zb, *more)
 
 
-def shared_expert(normed, w_sgate, s_gate, s_up, s_down):
-    shared_act = (jax.nn.silu(jnp.dot(normed, s_gate, preferred_element_type=F32))
-                  * jnp.dot(normed, s_up, preferred_element_type=F32)).astype(BF16)
-    shared_val = jnp.dot(shared_act, s_down, preferred_element_type=F32)
-    return jax.nn.sigmoid(jnp.dot(normed, w_sgate, preferred_element_type=F32)) * shared_val
+def shared_kernel(x_ref, ha_ref, hb_ref, gate_row, sg_ref, su_ref, sd_ref, outa_ref, outb_ref):
+    step = pl.program_id(0)
+    for i, (h_ref, out_ref) in enumerate(((ha_ref, outa_ref), (hb_ref, outb_ref))):
+        h = h_ref[...]
+        gate_proj = jnp.dot(h, sg_ref[...], preferred_element_type=F32)
+        act = (jax.nn.silu(gate_proj) * jnp.dot(h, su_ref[...], preferred_element_type=F32)).astype(BF16)
+        part = jnp.dot(act, sd_ref[...], preferred_element_type=F32)
+
+        @pl.when(step == 0)
+        def _():
+            out_ref[...] = part
+
+        @pl.when(step > 0)
+        def _():
+            out_ref[...] += part
+
+        @pl.when(step == pl.num_programs(0) - 1)
+        def _():
+            weight = jnp.sum(h.astype(F32) * gate_row[...].astype(F32), axis=1, keepdims=True)
+            out_ref[...] = x_ref[i].astype(F32) + jax.nn.sigmoid(weight) * out_ref[...]
+
+
+def shared_call(hidden_in, ha, hb, w_sgate, s_gate, s_up, s_down):
+    half, hidden = ha.shape
+    ff = s_gate.shape[1]
+    chunk = 256
+    whole = pl.BlockSpec((half, hidden), lambda i: (0, 0), pipeline_mode=pl.Buffered(1))
+    wide = pl.BlockSpec((hidden, chunk), lambda i: (0, i))
+    out = jax.ShapeDtypeStruct((half, hidden), F32)
+    return pl.pallas_call(
+        shared_kernel,
+        grid=(ff // chunk,),
+        out_shape=(out, out),
+        in_specs=[pl.BlockSpec((2, half, hidden), lambda i: (0, 0, 0), pipeline_mode=pl.Buffered(1)), whole, whole,
+                  pl.BlockSpec((1, hidden), lambda i: (0, 0)), wide, wide, pl.BlockSpec((chunk, hidden), lambda i: (i, 0))],
+        out_specs=(whole, whole),
+        compiler_params=pltpu.CompilerParams(dimension_semantics=("arbitrary",), vmem_limit_bytes=60 * 1024 * 1024),
+        cost_estimate=pl.CostEstimate(flops=1_000_000, transcendentals=0, bytes_accessed=6 * ff * hidden),
+        name="shared",
+    )(hidden_in.reshape(2, half, hidden), ha, hb, w_sgate.reshape(1, hidden), s_gate, s_up, s_down)
 
 
 def route_kernel(geom, ids_ref, own_ref, next_ref, far_ref, prev_ref, list_ref, glist_ref, count_ref, slot_ref, gate_ref):
@@ -178,7 +213,7 @@
     )(ids, own, nxt, far, prv)
 
 
-def expert_kernel(pieces, classes, slots_dev, depth, *refs):
+def expert_kernel(sizes, classes, slots_dev, depth, *refs):
     refs = list(refs)
     n_src = 1
 
@@ -191,7 +226,7 @@
     has, hbs = take(n_src), take(n_src)
     own, sib = take(3), take(3)
     take(1)
-    ys = take(pieces)
+    ys = take(len(sizes))
     wg_ref, wu_ref, wd_ref = take(3)
     row_refs, tok_refs, sum_refs = [take(2) for _ in range(n_src)], [take(2) for _ in range(n_src)], [take(2) for _ in range(n_src)]
     stage_ref, sems, out_sems = take(3)
@@ -291,32 +326,31 @@
 
     @pl.when(step == steps - 1)
     def _():
-        size = 2 * half // pieces
-        outs = [(0, ref, n * size) for n, ref in enumerate(ys)]
-
-        def put(n, ref, i):
-            rows = pl.ds(pl.multiple_of(i * group, group), group)
-            return pltpu.make_async_copy(stage_ref.at[i % 2, n], ref.at[rows], out_sems.at[i % 2, n])
-
-        def unpack(i, carry):
-            for n, (q, ref, start) in enumerate(outs):
+        start = 0
+        for n, (ref, size) in enumerate(zip(ys, sizes)):
+            def put(i, n=n, ref=ref):
+                rows = pl.ds(pl.multiple_of(i * group, group), group)
+                return pltpu.make_async_copy(stage_ref.at[i % 2, n], ref.at[rows], out_sems.at[i % 2, n])
+
+            def unpack(i, carry, n=n, start=start, put=put):
                 @pl.when(i >= 2)
                 def _():
-                    put(n, ref, i).wait()
+                    put(i - 2).wait()
 
                 for j, (w, k) in enumerate(split):
                     stage_ref[i % 2, n, :, j * 128:(j + 1) * 128] = (
-                        sum_refs[q][w][pl.ds((start + i * group) * pitch + k, group, stride=pitch), :])
-                put(n, ref, i).start()
-            return carry
-
-        lax.fori_loop(0, size // group, unpack, 0)
-        for i in range(2):
-            for n, (q, ref, start) in enumerate(outs):
-                put(n, ref, i).wait()
-
-
-def expert_call(routes, ha, hb, own, sib, dep, row_max, pieces):
+                        sum_refs[0][w][pl.ds((start + i * group) * pitch + k, group, stride=pitch), :])
+                put(i).start()
+                return carry
+
+            lax.fori_loop(0, size // group, unpack, 0)
+            start += size
+        for n, (ref, size) in enumerate(zip(ys, sizes)):
+            for i in range(2):
+                pltpu.make_async_copy(stage_ref.at[i, n], ref.at[pl.ds(0, group)], out_sems.at[i, n]).wait()
+
+
+def expert_call(routes, ha, hb, own, sib, dep, row_max, sizes):
     half, hidden = ha.shape
     slots_dev, _, ff = own[0].shape
     depth = 4
@@ -324,12 +358,12 @@
     whole = pl.BlockSpec((half, hidden), lambda s: (0, 0), pipeline_mode=pl.Buffered(1))
     smem = pl.BlockSpec(memory_space=pltpu.SMEM)
     hbm = pl.BlockSpec(memory_space=pl.ANY)
-    out = jax.ShapeDtypeStruct((2 * half // pieces, hidden), F32)
+    pieces = len(sizes)
     toks = (2 * half + 8) * 8
     return pl.pallas_call(
-        functools.partial(expert_kernel, pieces, classes, slots_dev, depth),
+        functools.partial(expert_kernel, sizes, classes, slots_dev, depth),
         grid=(2 * slots_dev,),
-        out_shape=(out,) * pieces,
+        out_shape=tuple(jax.ShapeDtypeStruct((n, hidden), F32) for n in sizes),
         in_specs=[smem] * 3 + [whole] * 2 + [hbm] * 7,
         out_specs=(hbm,) * pieces,
         scratch_shapes=[pltpu.VMEM((depth, hidden, ff), BF16), pltpu.VMEM((depth, hidden, ff), BF16), pltpu.VMEM((depth, ff, hidden), BF16)]
@@ -356,6 +390,7 @@
         experts = w_router.shape[1]
         slots_dev = w_gate.shape[0]
         half = tok_dev // 2
+        parts = (3 * half // 4, half // 4)
         capacity = (5 * tok_dev * group_size * top_k + 4 * experts - 1) // (4 * experts)
         local_max = (2 * tok_dev * top_k + experts - 1) // experts
         me = lax.axis_index('ep')
@@ -388,6 +423,8 @@
         t_far = lax.ppermute(table, 'ep', far)
 
         hb_r1, ha_l1 = go_right(hb), go_left(ha)
+        half_sums = shared_call(hidden_in, ha, hb, w_sgate, s_gate, s_up, s_down)
+
         ha_r2, hb_l2 = go_right(ha_r1), go_left(hb_l1)
 
         steps = jnp.arange(group_size // cores)
@@ -400,25 +437,24 @@
         def routes(v, row_max):
             return lists[v, :, :row_max], glists[v, :, :row_max], kept[v]
 
-        d_a, d_b = expert_call(routes(1, 2 * local_max), ha_r1, hb_l1, own_w, sib_w, ha, 2 * local_max, 2)
+        d_a, d_b = expert_call(routes(1, 2 * local_max), ha_r1, hb_l1, own_w, sib_w, ha, 2 * local_max, (half, half))
         d_dep, d_a, d_b = d_a, go_left(d_a), go_right(d_b)
-        y2 = expert_call(routes(2, local_max), ha_r2, hb_l2, own_w, sib_w, d_dep, local_max, 4)
+        y2 = expert_call(routes(2, local_max), ha_r2, hb_l2, own_w, sib_w, d_dep, local_max, parts * 2)
         p = [go_right(y2[0]), go_left(y2[2])]
         p += [go_right(y2[1]), go_left(y2[3])]
-        y1 = expert_call(routes(3, 2 * local_max), ha_l1, hb_r1, own_w, sib_w, y2[0], 2 * local_max, 4)
-        half_sums = [shared_expert(after(h, y1[0]), w_sgate, s_gate, s_up, s_down) for h in (ha, hb)]
+        y1 = expert_call(routes(3, 2 * local_max), ha_l1, hb_r1, own_w, sib_w, y2[0], 2 * local_max, parts * 2)
 
         def relay(i, *deps):
             return y1[i] + after(p[2 * i], *deps), y1[2 + i] + after(p[2 * i + 1], *deps)
 
-        add_a, add_b = relay(0, *half_sums)
+        add_a, add_b = relay(0, y1[0])
         z0 = go_right(add_a), go_left(add_b)
-        y0 = expert_call(routes(0, local_max), ha, hb, own_w, sib_w, add_b, local_max, 2)
+        y0 = expert_call(routes(0, local_max), ha, hb, own_w, sib_w, add_b, local_max, (half, half))
         add_a, add_b = relay(1, y0[0])
         z1 = go_right(add_a), go_left(add_b)
-        base = [hidden_in[i * half:(i + 1) * half].astype(F32) + half_sums[i] + y0[i] + d for i, d in enumerate((d_a, d_b))]
+        base = [half_sums[i] + y0[i] + d for i, d in enumerate((d_a, d_b))]
         out = final_call(0, base[0], base[1], *z0, None)
-        out = final_call(1, base[0], base[1], *z1, out)
+        out = final_call(parts[0], base[0], base[1], *z1, out)
         return out.reshape(tok_dev, hidden)
 
     row_spec = P(('dp', 'ep'), None)

time: 377 us -> 399 us (1.058)
  Pallas kernels: 176 us -> 206 us
  matrix products: 33.3 us -> 4.11 us
  waiting for transfers between devices: 94.7 us -> 118 us
    ppermute x9, waiting for transfers between devices: 56.1 us -> 111 us  [go_right(): return lax.ppermute(v, 'ep', right)]
    ppermute x9, waiting for transfers between devices: 37.3 us -> 2.81 us  [go_left(): return lax.ppermute(v, 'ep', left)]
    pallas_call x4 -> x5, Pallas kernels: 147 us -> 178 us  [the longest x4 156 us: expert_call(): pl.pallas_call(functools.partial(expert_kernel, sizes, classes, slots_dev...]
    dot_general x6 -> x0, matrix products: 30.6 us -> none  [the longest x2 17.8 us: shared_expert(): shared_val = jnp.dot(shared_act, s_down, preferred_element_type=F32)]
    ppermute x9, starting transfers between devices: 16.1 us -> 9.37 us  [go_right(): return lax.ppermute(v, 'ep', right)]
    ppermute x9, starting transfers between devices: 22.9 us -> 29.5 us  [go_left(): return lax.ppermute(v, 'ep', left)]
    add x1 -> x2, other arithmetic: 11.5 us -> 10.2 us  [block(): base = [half_sums[i] + y0[i] + d for i, d in enumerate((d_a, d_b))]]
  transfers between devices with their start and end apart: 23 -> 23, of which waited for: 10 -> 8; matrix products, arithmetic and copies ran while one was open for 16% -> 7% of each run, Pallas kernels for 44% -> 50%
where the time goes in v5:
time: 399 us; the launch traced here: 398 us
  Pallas kernels  206 us (52%)
  waiting for transfers between devices  118 us (30%)
  starting transfers between devices  40.2 us (10%)
  other arithmetic  22.7 us (6%)
  local copies, waits for them, and re-layouts  7.24 us (2%)
  matrix products  4.11 us (1%)
    pallas_call x4, Pallas kernels, expert_call(): pl.pallas_call(functools.partial(expert_kernel, sizes, classes, slots_dev...  156 us
    ppermute x9, waiting for transfers between devices, go_right(): return lax.ppermute(v, 'ep', right)  111 us
    ppermute x9, starting transfers between devices, go_left(): return lax.ppermute(v, 'ep', left)  29.5 us
    pallas_call x1, Pallas kernels, shared_call(): pl.pallas_call(shared_kernel, grid=(ff // chunk,), out_shape=(out, out),...  21.2 us
    pallas_call x1, Pallas kernels, route_call(): pl.pallas_call(functools.partial(route_kernel, (top_k, slots_dev, capacit...  14.9 us
    add x2, other arithmetic, block(): base = [half_sums[i] + y0[i] + d for i, d in enumerate((d_a, d_b))]  10.2 us
    ppermute x9, starting transfers between devices, go_right(): return lax.ppermute(v, 'ep', right)  9.37 us
    pallas_call x2, Pallas kernels, final_call(): pl.pallas_call(final_kernel, grid=(size // rows,), out_shape=jax.ShapeDty...  8.96 us
  transfers between devices with their start and end apart: 23, of which 8 were waited for; matrix products, arithmetic and copies ran while one was open for 7% of the time, Pallas kernels for 50%

profile of v5, /device:TPU:88, one launch (start us, length us, event | category | flops | bytes accessed | tf_op | source)
XLA Modules:
  0.0 398.5 jit_solution(16764923930325343797)
XLA Ops:
  0.0 4.6 %norm.1 = (bf16[512,1536]{1,0:T(8,128)(2,1)}, bf16[512,1536]{1,0:T(8,128)(2,1)}) custom-call(bf16[2,512,1536]{2,1,0:T(8,128)(2,1)} %bitcast.33, bf16[1536]{0:T(1024)(128)(2,1)} %gain_ref.1), custom_call_target="tpu_custom_call" | custom-call | flops 6291456 | bytes 6291456 | tf_op jit(solution)/shard_map/norm/pallas_call | solution.py:29
  4.7 2.1 fusion.5
  6.8 2.0 fusion.6
  8.9 0.4 select_reduce_fusion
  9.4 1.1 collective-permute-done
  10.7 0.3 collective-permute-start.5
  11.1 0.2 collective-permute-start.6
  11.3 3.3 collective-permute-start.1
  14.5 0.5 collective-permute-start.2
  15.1 2.8 collective-permute-done.1.next_ref
  17.8 2.5 collective-permute-done.2.far_ref
  20.3 4.1 %collective-permute-done.3.prev_ref = f32[16,1024]{1,0:T(8,128)S(1)} collective-permute-done((f32[16,1024]{1,0:T(8,128)S(1)}, f32[16,1024]{1,0:T(8,128)S(1)}, u32[]{:S(2)}, u32[]{:S(2)}) %collective-permute-start.3) | collective-permute-done | bytes 65568 | tf_op jit(solution)/shard_map/ppermute | solution.py:399
  24.4 2.0 collective-permute-start.11
  26.6 0.7 pad_add_fusion.1.ids_ref
  27.3 14.9 %route.1 = (s32[4,16,8,384]{3,2,1,0:T(8,128)}, f32[4,16,8,384]{3,2,1,0:T(8,128)}, f32[4,16,128]{2,1,0:T(8,128)}) custom-call(s32[10]{0:T(128)} %pad_add_fusion.1.ids_ref, f32[16,1024]{1,0:T(8,128)} %copy-done.11, f32[16,1024]{1,0:T(8,128)} %copy-done.13, f32[16,1024]{1,0:T(8,128)} %copy-done.14, f32[16,1024]{1,0:T(8,128)} %copy-done.15), custom_call_target="tpu_custom_call" | custom-call | flops 1000000 | bytes 2000000 | tf_op jit(solution)/shard_map/route/pallas_call | solution.py:204
  42.2 1.4 copy.30
  43.6 13.9 %collective-permute-done.9.refs_3_ = bf16[512,1536]{1,0:T(8,128)(2,1)} collective-permute-done((bf16[512,1536]{1,0:T(8,128)(2,1)S(1)}, bf16[512,1536]{1,0:T(8,128)(2,1)}, u32[]{:S(2)}, u32[]{:S(2)}) %collective-permute-start.9) | collective-permute-done | bytes 1572896 | tf_op jit(solution)/shard_map/ppermute | solution.py:399
  57.6 3.2 collective-permute-start.12
  60.8 1.3 copy.29
  62.1 0.6 slice_bitcast_fusion.6
  62.7 0.3 collective-permute-start.7
  63.0 0.7 slice_reduce_fusion.1
  64.1 0.6 slice_bitcast_fusion.7
  64.7 0.6 slice_bitcast_fusion.4
  65.3 0.6 slice_bitcast_fusion.5
  66.0 40.0 %experts.4 = (f32[512,1536]{1,0:T(8,128)}, f32[512,1536]{1,0:T(8,128)}) custom-call(s32[16,384]{1,0:T(8,128)} %get-tuple-element.66.refs_0_, f32[16,384]{1,0:T(8,128)} %get-tuple-element.64.refs_1_, s32[16]{0:T(128)} %get-tuple-element.58.refs_2_, bf16[512,1536]{1,0:T(8,128)(2,1)} %collective-permute-done.9.refs_3_, ...), custom_call_target="tpu_custom_call" | custom-call | flops 1000000 | bytes 75497472 | tf_op jit(solution)/shard_map/experts/pallas_call | solution.py:363
  106.1 38.2 %experts.5 = (f32[384,1536]{1,0:T(8,128)}, f32[128,1536]{1,0:T(8,128)}, f32[384,1536]{1,0:T(8,128)}, f32[128,1536]{1,0:T(8,128)}) custom-call(s32[16,192]{1,0:T(8,128)} %get-tuple-element.69.refs_0_, f32[16,192]{1,0:T(8,128)} %get-tuple-element.67.refs_1_, s32[16]{0:T(128)} %get-tuple-element.57.refs_2_, bf16[512,1536]{1,0:T(8,128)(2,1)} %collective-permute-done.10.refs_3_, ...), custom_call_target="tpu_custom_call" | custom-call | flops 1000000 | bytes 75497472 | tf_op jit(solution)/shard_map/experts/pallas_call | solution.py:363
  144.3 0.6 collective-permute-start.20
  144.9 12.6 %collective-permute-start.14 = (f32[512,1536]{1,0:T(8,128)}, f32[512,1536]{1,0:T(8,128)}, u32[]{:S(2)}, u32[]{:S(2)}) collective-permute-start(f32[512,1536]{1,0:T(8,128)} %get-tuple-element.40.refs_11_), channel_id=1, source_target_pairs={{0,6},{1,7},{2,0},{3,1},{4,2},{5,3},{6,4},{7,5},{8,14},{9,15},{10,... | collective-permute-start | bytes 9437192 | tf_op jit(solution)/shard_map/ppermute | solution.py:402
  157.6 1.9 collective-permute-start.13
  159.6 84.0 %collective-permute-done.8.refs_4_ = bf16[512,1536]{1,0:T(8,128)(2,1)} collective-permute-done((bf16[512,1536]{1,0:T(8,128)(2,1)}, bf16[512,1536]{1,0:T(8,128)(2,1)}, u32[]{:S(2)}, u32[]{:S(2)}) %collective-permute-start.8) | collective-permute-done | bytes 1572896 | tf_op jit(solution)/shard_map/ppermute | solution.py:399
  243.6 2.0 collective-permute-start.18
  245.6 37.7 %experts.6 = (f32[384,1536]{1,0:T(8,128)}, f32[128,1536]{1,0:T(8,128)}, f32[384,1536]{1,0:T(8,128)}, f32[128,1536]{1,0:T(8,128)}) custom-call(s32[16,384]{1,0:T(8,128)} %get-tuple-element.65.refs_0_, f32[16,384]{1,0:T(8,128)} %get-tuple-element.63.refs_1_, s32[16]{0:T(128)} %get-tuple-element.59.refs_2_, bf16[512,1536]{1,0:T(8,128)(2,1)} %collective-permute-done.7.refs_3_, ...), custom_call_target="tpu_custom_call" | custom-call | flops 1000000 | bytes 75497472 | tf_op jit(solution)/shard_map/experts/pallas_call | solution.py:363
  283.3 4.3 %add.102 = f32[384,1536]{1,0:T(8,128)} add(f32[384,1536]{1,0:T(8,128)} %get-tuple-element.44, f32[384,1536]{1,0:T(8,128)} %collective-permute-done.20) | non-fusion elementwise | flops 589824 | bytes 7077888 | tf_op jit(solution)/shard_map/add | solution.py:448
  287.6 6.6 %collective-permute-start.21 = (f32[384,1536]{1,0:T(8,128)}, f32[384,1536]{1,0:T(8,128)}, u32[]{:S(2)}, u32[]{:S(2)}) collective-permute-start(f32[384,1536]{1,0:T(8,128)} %add.102), channel_id=1, source_target_pairs={{0,2},{1,3},{2,4},{3,5},{4,6},{5,7},{6,0},{7,1},{8,10},{9,11},{10,... | collective-permute-start | bytes 7077896 | tf_op jit(solution)/shard_map/ppermute | solution.py:399
  294.2 3.4 add.95.refs_11_
  297.6 4.0 %collective-permute-start.22 = (f32[384,1536]{1,0:T(8,128)}, f32[384,1536]{1,0:T(8,128)}, u32[]{:S(2)}, u32[]{:S(2)}) collective-permute-start(f32[384,1536]{1,0:T(8,128)} %add.95.refs_11_), channel_id=1, source_target_pairs={{0,6},{1,7},{2,0},{3,1},{4,2},{5,3},{6,4},{7,5},{8,14},{9,15},{10,... | collective-permute-start | bytes 7077896 | tf_op jit(solution)/shard_map/ppermute | solution.py:402
  301.7 21.2 %shared.1 = (f32[512,1536]{1,0:T(8,128)}, f32[512,1536]{1,0:T(8,128)}) custom-call(bf16[2,512,1536]{2,1,0:T(8,128)(2,1)} %bitcast.34, bf16[512,1536]{1,0:T(8,128)(2,1)} %get-tuple-element.31.ha_ref.refs_11_.refs_3_, bf16[512,1536]{1,0:T(8,128)(2,1)} %get-tuple-element.32.hb_ref.refs_4_, bf16[1,1536]{1,0:T(2,128)(2,1)} %bitcast.36, ...), custom_call_target="tpu_custom_call" | custom-call | flops 1000000 | bytes 9437184 | tf_op jit(solution)/shard_map/shared/pallas_call | solution.py:96
  322.9 40.5 %experts.7 = (f32[512,1536]{1,0:T(8,128)}, f32[512,1536]{1,0:T(8,128)}) custom-call(s32[16,192]{1,0:T(8,128)} %get-tuple-element.70.refs_0_, f32[16,192]{1,0:T(8,128)} %get-tuple-element.68.refs_1_, s32[16]{0:T(128)} %get-tuple-element.60.refs_2_, bf16[512,1536]{1,0:T(8,128)(2,1)} %get-tuple-element.31.ha_ref.refs_11_.refs_3_, ...), custom_call_target="tpu_custom_call" | custom-call | flops 1000000 | bytes 75497472 | tf_op jit(solution)/shard_map/experts/pallas_call | solution.py:363
  363.4 1.4 add.101
  364.9 2.1 add.100
  367.0 2.0 collective-permute-start.17
  369.0 5.6 %add_add_fusion.1.base_a = f32[512,1536]{1,0:T(8,128)} fusion(f32[512,1536]{1,0:T(8,128)} %collective-permute-done.14, f32[512,1536]{1,0:T(8,128)S(1)} %copy-done.7, f32[512,1536]{1,0:T(8,128)} %get-tuple-element.46), kind=kLoop, calls=%fused_computation.1 | loop fusion | flops 1572864 | bytes 12582912 | tf_op jit(solution)/shard_map/add | solution.py:455
  374.7 4.6 %add_add_fusion.base_b = f32[512,1536]{1,0:T(8,128)} fusion(f32[512,1536]{1,0:T(8,128)} %collective-permute-done.15, f32[512,1536]{1,0:T(8,128)S(1)} %copy-done.5, f32[512,1536]{1,0:T(8,128)S(1)} %copy-done.6), kind=kLoop, calls=%fused_computation | loop fusion | flops 1572864 | bytes 12582912 | tf_op jit(solution)/shard_map/add | solution.py:455
  379.2 6.3 %final.2.rest_0_ = bf16[2,512,1536]{2,1,0:T(8,128)(2,1)} custom-call(f32[512,1536]{1,0:T(8,128)} %add_add_fusion.1.base_a, f32[512,1536]{1,0:T(8,128)} %add_add_fusion.base_b, f32[384,1536]{1,0:T(8,128)} %collective-permute-done.21.za_ref, f32[384,1536]{1,0:T(8,128)} %collective-permute-done.22.zb_ref), custom_call_target="tpu_custom_call" | custom-call | flops 2359296 | bytes 11796480 | tf_op jit(solution)/shard_map/final/pallas_call | solution.py:54
  385.5 9.4 %collective-permute-done.17.za_ref = f32[128,1536]{1,0:T(8,128)S(1)} collective-permute-done((f32[128,1536]{1,0:T(8,128)}, f32[128,1536]{1,0:T(8,128)S(1)}, u32[]{:S(2)}, u32[]{:S(2)}) %collective-permute-start.17) | collective-permute-done | bytes 786464 | tf_op jit(solution)/shard_map/ppermute | solution.py:399
  394.9 0.9 copy-done.10
  395.8 2.7 final.3
  (72 shorter events, 1.4 us)
Async XLA Ops:
  0.0 4.6 %copy-start = (bf16[1536,64]{0,1:T(8,128)(2,1)S(1)}, bf16[1536,64]{0,1:T(8,128)(2,1)}, u32[]{:S(2)}) copy-start(bf16[1536,64]{0,1:T(8,128)(2,1)} %param.14) | copy-start | bytes 589828
  4.6 4.3 %copy-start.12 = (s32[1024,6]{0,1:T(8,128)S(1)}, s32[1024,6]{0,1:T(8,128)}, u32[]{:S(2)}) copy-start(s32[1024,6]{0,1:T(8,128)} %param.12) | copy-start | bytes 73732
  4.6 15.7 %copy-start.2 = (bf16[512,1536]{1,0:T(8,128)(2,1)S(1)}, bf16[512,1536]{1,0:T(8,128)(2,1)}, u32[]{:S(2)}) copy-start(bf16[512,1536]{1,0:T(8,128)(2,1)} %get-tuple-element.31.ha_ref.refs_11_.refs_3_) | copy-start | bytes 4718596
  9.3 1.3 collective-permute-start
  10.6 52.2 %collective-permute-start.4 = (bf16[8,1536,512]{2,1,0:T(8,128)(2,1)}, bf16[8,1536,512]{2,1,0:T(8,128)(2,1)}, u32[]{:S(2)}, u32[]{:S(2)}) collective-permute-start(bf16[8,1536,512]{2,1,0:T(8,128)(2,1)} %refs_5_.7), channel_id=1, source_target_pairs={{0,1},{1,0},{2,3},{3,2},{4,5},{5,4},{6,7},{7,6},{8,9},{9,8},{10,11... | collective-permute-start | bytes 37748744 | tf_op jit(solution)/shard_map/ppermute | solution.py:421
  10.7 55.2 %collective-permute-start.5 = (bf16[8,1536,512]{2,1,0:T(8,128)(2,1)}, bf16[8,1536,512]{2,1,0:T(8,128)(2,1)}, u32[]{:S(2)}, u32[]{:S(2)}) collective-permute-start(bf16[8,1536,512]{2,1,0:T(8,128)(2,1)} %refs_6_.7), channel_id=1, source_target_pairs={{0,1},{1,0},{2,3},{3,2},{4,5},{5,4},{6,7},{7,6},{8,9},{9,8},{10,11... | collective-permute-start | bytes 37748744 | tf_op jit(solution)/shard_map/ppermute | solution.py:421
  11.1 55.0 %collective-permute-start.6 = (bf16[8,512,1536]{2,1,0:T(8,128)(2,1)}, bf16[8,512,1536]{2,1,0:T(8,128)(2,1)}, u32[]{:S(2)}, u32[]{:S(2)}) collective-permute-start(bf16[8,512,1536]{2,1,0:T(8,128)(2,1)} %refs_7_.7), channel_id=1, source_target_pairs={{0,1},{1,0},{2,3},{3,2},{4,5},{5,4},{6,7},{7,6},{8,9},{9,8},{10,11... | collective-permute-start | bytes 37748744 | tf_op jit(solution)/shard_map/ppermute | solution.py:421
  11.3 16.0 %copy-start.11 = (f32[16,1024]{1,0:T(8,128)}, f32[16,1024]{1,0:T(8,128)S(1)}, u32[]{:S(2)}) copy-start(f32[16,1024]{1,0:T(8,128)S(1)} %pad_maximum_fusion.1.own_ref) | copy-start | bytes 196612
  11.3 6.5 %collective-permute-start.1 = (f32[16,1024]{1,0:T(8,128)S(1)}, f32[16,1024]{1,0:T(8,128)S(1)}, u32[]{:S(2)}, u32[]{:S(2)}) collective-permute-start(f32[16,1024]{1,0:T(8,128)S(1)} %pad_maximum_fusion.1.own_ref), channel_id=1, source_target_pairs={{0,6},{1,7},{2,0},{3,1},{4,2},{5,3},{6,4},{7,5},{8,14},{9,15},{10,... | collective-permute-start | bytes 196616 | tf_op jit(solution)/shard_map/ppermute | solution.py:402
  14.5 5.8 %collective-permute-start.2 = (f32[16,1024]{1,0:T(8,128)S(1)}, f32[16,1024]{1,0:T(8,128)S(1)}, u32[]{:S(2)}, u32[]{:S(2)}) collective-permute-start(f32[16,1024]{1,0:T(8,128)S(1)} %pad_maximum_fusion.1.own_ref), channel_id=1, source_target_pairs={{0,4},{1,5},{2,6},{3,7},{4,0},{5,1},{6,2},{7,3},{8,12},{9,13},{10,... | collective-permute-start | bytes 196616 | tf_op jit(solution)/shard_map/ppermute | solution.py:423
  17.8 9.5 %copy-start.13 = (f32[16,1024]{1,0:T(8,128)}, f32[16,1024]{1,0:T(8,128)S(1)}, u32[]{:S(2)}) copy-start(f32[16,1024]{1,0:T(8,128)S(1)} %collective-permute-done.1.next_ref) | copy-start | bytes 196612
  17.8 6.6 %collective-permute-start.3 = (f32[16,1024]{1,0:T(8,128)S(1)}, f32[16,1024]{1,0:T(8,128)S(1)}, u32[]{:S(2)}, u32[]{:S(2)}) collective-permute-start(f32[16,1024]{1,0:T(8,128)S(1)} %pad_maximum_fusion.1.own_ref), channel_id=1, source_target_pairs={{0,2},{1,3},{2,4},{3,5},{4,6},{5,7},{6,0},{7,1},{8,10},{9,11},{10,... | collective-permute-start | bytes 196616 | tf_op jit(solution)/shard_map/ppermute | solution.py:399
  20.3 7.0 %copy-start.14 = (f32[16,1024]{1,0:T(8,128)}, f32[16,1024]{1,0:T(8,128)S(1)}, u32[]{:S(2)}) copy-start(f32[16,1024]{1,0:T(8,128)S(1)} %collective-permute-done.2.far_ref) | copy-start | bytes 196612
  20.3 37.2 %collective-permute-start.9 = (bf16[512,1536]{1,0:T(8,128)(2,1)S(1)}, bf16[512,1536]{1,0:T(8,128)(2,1)}, u32[]{:S(2)}, u32[]{:S(2)}) collective-permute-start(bf16[512,1536]{1,0:T(8,128)(2,1)S(1)} %copy-done.2), channel_id=1, source_target_pairs={{0,2},{1,3},{2,4},{3,5},{4,6},{5,7},{6,0},{7,1},{8,10},{9,11},{10,... | collective-permute-start | bytes 4718600 | tf_op jit(solution)/shard_map/ppermute | solution.py:399
  24.4 2.9 copy-start.15
  24.4 33.1 %collective-permute-start.11 = (bf16[512,1536]{1,0:T(8,128)(2,1)}, bf16[512,1536]{1,0:T(8,128)(2,1)}, u32[]{:S(2)}, u32[]{:S(2)}) collective-permute-start(bf16[512,1536]{1,0:T(8,128)(2,1)} %get-tuple-element.32.hb_ref.refs_4_), channel_id=1, source_target_pairs={{0,6},{1,7},{2,0},{3,1},{4,2},{5,3},{6,4},{7,5},{8,14},{9,15},{10,... | collective-permute-start | bytes 4718600 | tf_op jit(solution)/shard_map/ppermute | solution.py:402
  42.2 20.5 %copy-start.16 = (f32[4,16,128]{2,1,0:T(8,128)S(1)}, f32[4,16,128]{2,1,0:T(8,128)}, u32[]{:S(2)}) copy-start(f32[4,16,128]{2,1,0:T(8,128)} %get-tuple-element.36) | copy-start | bytes 98308
  42.2 21.5 %copy-start.4 = (f32[4,16,8,384]{3,2,1,0:T(8,128)S(1)}, f32[4,16,8,384]{3,2,1,0:T(8,128)}, u32[]{:S(2)}) copy-start(f32[4,16,8,384]{3,2,1,0:T(8,128)} %get-tuple-element.35) | copy-start | bytes 2359300
  42.2 21.7 %copy-start.3 = (s32[4,16,8,384]{3,2,1,0:T(8,128)S(1)}, s32[4,16,8,384]{3,2,1,0:T(8,128)}, u32[]{:S(2)}) copy-start(s32[4,16,8,384]{3,2,1,0:T(8,128)} %get-tuple-element.34) | copy-start | bytes 2359300
  57.5 48.5 %collective-permute-start.10 = (bf16[512,1536]{1,0:T(8,128)(2,1)}, bf16[512,1536]{1,0:T(8,128)(2,1)}, u32[]{:S(2)}, u32[]{:S(2)}) collective-permute-start(bf16[512,1536]{1,0:T(8,128)(2,1)} %collective-permute-done.9.refs_3_), channel_id=1, source_target_pairs={{0,2},{1,3},{2,4},{3,5},{4,6},{5,7},{6,0},{7,1},{8,10},{9,11},{10,... | collective-permute-start | bytes 4718600 | tf_op jit(solution)/shard_map/ppermute | solution.py:399
  57.6 48.5 %collective-permute-start.12 = (bf16[512,1536]{1,0:T(8,128)(2,1)}, bf16[512,1536]{1,0:T(8,128)(2,1)}, u32[]{:S(2)}, u32[]{:S(2)}) collective-permute-start(bf16[512,1536]{1,0:T(8,128)(2,1)} %collective-permute-done.11.refs_4_), channel_id=1, source_target_pairs={{0,6},{1,7},{2,0},{3,1},{4,2},{5,3},{6,4},{7,5},{8,14},{9,15},{10,... | collective-permute-start | bytes 4718600 | tf_op jit(solution)/shard_map/ppermute | solution.py:402
  62.7 96.8 %collective-permute-start.7 = (bf16[512,1536]{1,0:T(8,128)(2,1)S(1)}, bf16[512,1536]{1,0:T(8,128)(2,1)}, u32[]{:S(2)}, u32[]{:S(2)}) collective-permute-start(bf16[512,1536]{1,0:T(8,128)(2,1)S(1)} %copy-done.2), channel_id=1, source_target_pairs={{0,6},{1,7},{2,0},{3,1},{4,2},{5,3},{6,4},{7,5},{8,14},{9,15},{10,... | collective-permute-start | bytes 4718600 | tf_op jit(solution)/shard_map/ppermute | solution.py:402
  144.3 101.3 %collective-permute-start.20 = (f32[384,1536]{1,0:T(8,128)}, f32[384,1536]{1,0:T(8,128)}, u32[]{:S(2)}, u32[]{:S(2)}) collective-permute-start(f32[384,1536]{1,0:T(8,128)} %get-tuple-element.41.refs_11_), channel_id=1, source_target_pairs={{0,2},{1,3},{2,4},{3,5},{4,6},{5,7},{6,0},{7,1},{8,10},{9,11},{10,... | collective-permute-start | bytes 7077896 | tf_op jit(solution)/shard_map/ppermute | solution.py:399
  144.9 222.1 %collective-permute-start.14 = (f32[512,1536]{1,0:T(8,128)}, f32[512,1536]{1,0:T(8,128)}, u32[]{:S(2)}, u32[]{:S(2)}) collective-permute-start(f32[512,1536]{1,0:T(8,128)} %get-tuple-element.40.refs_11_), channel_id=1, source_target_pairs={{0,6},{1,7},{2,0},{3,1},{4,2},{5,3},{6,4},{7,5},{8,14},{9,15},{10,... | collective-permute-start | bytes 9437192 | tf_op jit(solution)/shard_map/ppermute | solution.py:402
  157.6 130.0 %collective-permute-start.13 = (f32[384,1536]{1,0:T(8,128)}, f32[384,1536]{1,0:T(8,128)}, u32[]{:S(2)}, u32[]{:S(2)}) collective-permute-start(f32[384,1536]{1,0:T(8,128)} %get-tuple-element.43), channel_id=1, source_target_pairs={{0,6},{1,7},{2,0},{3,1},{4,2},{5,3},{6,4},{7,5},{8,14},{9,15},{10,... | collective-permute-start | bytes 7077896 | tf_op jit(solution)/shard_map/ppermute | solution.py:402
  159.5 84.1 %collective-permute-start.8 = (bf16[512,1536]{1,0:T(8,128)(2,1)}, bf16[512,1536]{1,0:T(8,128)(2,1)}, u32[]{:S(2)}, u32[]{:S(2)}) collective-permute-start(bf16[512,1536]{1,0:T(8,128)(2,1)} %get-tuple-element.32.hb_ref.refs_4_), channel_id=1, source_target_pairs={{0,2},{1,3},{2,4},{3,5},{4,6},{5,7},{6,0},{7,1},{8,10},{9,11},{10,... | collective-permute-start | bytes 4718600 | tf_op jit(solution)/shard_map/ppermute | solution.py:399
  159.6 215.1 %collective-permute-start.15 = (f32[512,1536]{1,0:T(8,128)}, f32[512,1536]{1,0:T(8,128)}, u32[]{:S(2)}, u32[]{:S(2)}) collective-permute-start(f32[512,1536]{1,0:T(8,128)} %get-tuple-element.49), channel_id=1, source_target_pairs={{0,2},{1,3},{2,4},{3,5},{4,6},{5,7},{6,0},{7,1},{8,10},{9,11},{10,... | collective-permute-start | bytes 9437192 | tf_op jit(solution)/shard_map/ppermute | solution.py:399
  243.6 54.1 %collective-permute-start.18 = (f32[128,1536]{1,0:T(8,128)}, f32[128,1536]{1,0:T(8,128)S(1)}, u32[]{:S(2)}, u32[]{:S(2)}) collective-permute-start(f32[128,1536]{1,0:T(8,128)} %get-tuple-element.54), channel_id=1, source_target_pairs={{0,6},{1,7},{2,0},{3,1},{4,2},{5,3},{6,4},{7,5},{8,14},{9,15},{10,... | collective-permute-start | bytes 2359304 | tf_op jit(solution)/shard_map/ppermute | solution.py:402
  245.6 119.2 %collective-permute-start.16 = (f32[128,1536]{1,0:T(8,128)}, f32[128,1536]{1,0:T(8,128)S(1)}, u32[]{:S(2)}, u32[]{:S(2)}) collective-permute-start(f32[128,1536]{1,0:T(8,128)} %get-tuple-element.51), channel_id=1, source_target_pairs={{0,2},{1,3},{2,4},{3,5},{4,6},{5,7},{6,0},{7,1},{8,10},{9,11},{10,... | collective-permute-start | bytes 2359304 | tf_op jit(solution)/shard_map/ppermute | solution.py:399
  283.3 10.9 %copy-start.8 = (f32[384,1536]{1,0:T(8,128)S(1)}, f32[384,1536]{1,0:T(8,128)}, u32[]{:S(2)}) copy-start(f32[384,1536]{1,0:T(8,128)} %get-tuple-element.42) | copy-start | bytes 7077892
  287.6 91.6 %collective-permute-start.21 = (f32[384,1536]{1,0:T(8,128)}, f32[384,1536]{1,0:T(8,128)}, u32[]{:S(2)}, u32[]{:S(2)}) collective-permute-start(f32[384,1536]{1,0:T(8,128)} %add.102), channel_id=1, source_target_pairs={{0,2},{1,3},{2,4},{3,5},{4,6},{5,7},{6,0},{7,1},{8,10},{9,11},{10,... | collective-permute-start | bytes 7077896 | tf_op jit(solution)/shard_map/ppermute | solution.py:399
  297.6 81.6 %collective-permute-start.22 = (f32[384,1536]{1,0:T(8,128)}, f32[384,1536]{1,0:T(8,128)}, u32[]{:S(2)}, u32[]{:S(2)}) collective-permute-start(f32[384,1536]{1,0:T(8,128)} %add.95.refs_11_), channel_id=1, source_target_pairs={{0,6},{1,7},{2,0},{3,1},{4,2},{5,3},{6,4},{7,5},{8,14},{9,15},{10,... | collective-permute-start | bytes 7077896 | tf_op jit(solution)/shard_map/ppermute | solution.py:402
  363.4 5.6 %copy-start.7 = (f32[512,1536]{1,0:T(8,128)S(1)}, f32[512,1536]{1,0:T(8,128)}, u32[]{:S(2)}) copy-start(f32[512,1536]{1,0:T(8,128)} %get-tuple-element.33) | copy-start | bytes 9437188
  364.8 20.7 %collective-permute-start.19 = (f32[128,1536]{1,0:T(8,128)S(1)}, f32[128,1536]{1,0:T(8,128)S(1)}, u32[]{:S(2)}, u32[]{:S(2)}) collective-permute-start(f32[128,1536]{1,0:T(8,128)S(1)} %add.101), channel_id=1, source_target_pairs={{0,6},{1,7},{2,0},{3,1},{4,2},{5,3},{6,4},{7,5},{8,14},{9,15},{10,... | collective-permute-start | bytes 2359304 | tf_op jit(solution)/shard_map/ppermute | solution.py:402
  367.0 27.8 %collective-permute-start.17 = (f32[128,1536]{1,0:T(8,128)}, f32[128,1536]{1,0:T(8,128)S(1)}, u32[]{:S(2)}, u32[]{:S(2)}) collective-permute-start(f32[128,1536]{1,0:T(8,128)} %add.100), channel_id=1, source_target_pairs={{0,2},{1,3},{2,4},{3,5},{4,6},{5,7},{6,0},{7,1},{8,10},{9,11},{10,... | collective-permute-start | bytes 2359304 | tf_op jit(solution)/shard_map/ppermute | solution.py:399
  369.0 5.6 %copy-start.5 = (f32[512,1536]{1,0:T(8,128)S(1)}, f32[512,1536]{1,0:T(8,128)}, u32[]{:S(2)}) copy-start(f32[512,1536]{1,0:T(8,128)} %get-tuple-element.47) | copy-start | bytes 9437188
  369.0 5.6 %copy-start.6 = (f32[512,1536]{1,0:T(8,128)S(1)}, f32[512,1536]{1,0:T(8,128)}, u32[]{:S(2)}) copy-start(f32[512,1536]{1,0:T(8,128)} %get-tuple-element.48) | copy-start | bytes 9437188
  385.5 9.4 %copy-start.9 = (f32[128,1536]{1,0:T(8,128)}, f32[128,1536]{1,0:T(8,128)S(1)}, u32[]{:S(2)}) copy-start(f32[128,1536]{1,0:T(8,128)S(1)} %collective-permute-done.19.zb_ref) | copy-start | bytes 2359300
  394.9 0.9 copy-start.10
  395.8 2.7 copy-start.1

commit v6 on v5

--- a/solution.py
+++ b/solution.py
@@ -13,29 +13,39 @@
 PAIRS = ((0, 0), (3, 1), (2, 2), (1, 3))
 
 
-def norm_kernel(x_ref, gain_ref, ha_ref, hb_ref):
+def norm_kernel(x_ref, gain_ref, wr_ref, a0_ref, a1_ref, b0_ref, b1_ref, logit_ref):
+    step = pl.program_id(0)
     gain = gain_ref[...].astype(F32)[None, :]
-    for i, out_ref in enumerate((ha_ref, hb_ref)):
+    for i, refs in enumerate(((a0_ref, a1_ref), (b0_ref, b1_ref))):
         x = x_ref[i].astype(F32)
         inv_rms = lax.rsqrt(jnp.mean(x * x, axis=-1, keepdims=True) + 1e-6)
-        out_ref[...] = (x * inv_rms * gain).astype(BF16)
-
-
-def norm_call(hidden_in, norm_gain):
+        h = (x * inv_rms * gain).astype(BF16)
+        logit_ref[i] = jnp.dot(h, wr_ref[...], preferred_element_type=F32)
+        for n, ref in enumerate(refs):
+            @pl.when(step // 2 == n)
+            def _(ref=ref, h=h):
+                ref[...] = h
+
+
+def norm_call(hidden_in, norm_gain, w_router):
     toks, hidden = hidden_in.shape
-    half, rows = toks // 2, 128
-    out = jax.ShapeDtypeStruct((half, hidden), BF16)
-    block = pl.BlockSpec((rows, hidden), lambda i: (i, 0))
+    experts = w_router.shape[1]
+    half = toks // 2
+    rows = half // 4
+    out = jax.ShapeDtypeStruct((half // 2, hidden), BF16)
+    early = pl.BlockSpec((rows, hidden), lambda i: (jnp.minimum(i, 1), 0))
+    late = pl.BlockSpec((rows, hidden), lambda i: (jnp.maximum(i - 2, 0), 0))
     return pl.pallas_call(
         norm_kernel,
-        grid=(half // rows,),
-        out_shape=(out, out),
-        in_specs=[pl.BlockSpec((2, rows, hidden), lambda i: (0, i, 0)), pl.BlockSpec((hidden,), lambda i: (0,))],
-        out_specs=(block, block),
+        grid=(4,),
+        out_shape=(out,) * 4 + (jax.ShapeDtypeStruct((2, half, experts), F32),),
+        in_specs=[pl.BlockSpec((2, rows, hidden), lambda i: (0, i, 0)), pl.BlockSpec((hidden,), lambda i: (0,)),
+                  pl.BlockSpec((hidden, experts), lambda i: (0, 0))],
+        out_specs=(early, late, early, late, pl.BlockSpec((2, rows, experts), lambda i: (0, i, 0))),
         compiler_params=pltpu.CompilerParams(dimension_semantics=("arbitrary",)),
         cost_estimate=pl.CostEstimate(flops=4 * toks * hidden, transcendentals=toks, bytes_accessed=4 * toks * hidden),
         name="norm",
-    )(hidden_in.reshape(2, half, hidden), norm_gain)
+    )(hidden_in.reshape(2, half, hidden), norm_gain, w_router)
 
 
 def final_kernel(base_a, base_b, za_ref, zb_ref, *rest):
@@ -64,10 +74,10 @@
     )(base_a, base_b, za, zb, *more)
 
 
-def shared_kernel(x_ref, ha_ref, hb_ref, gate_row, sg_ref, su_ref, sd_ref, outa_ref, outb_ref):
+def shared_kernel(x_ref, a0_ref, a1_ref, b0_ref, b1_ref, gate_row, sg_ref, su_ref, sd_ref, outa_ref, outb_ref):
     step = pl.program_id(0)
-    for i, (h_ref, out_ref) in enumerate(((ha_ref, outa_ref), (hb_ref, outb_ref))):
-        h = h_ref[...]
+    for i, (h0_ref, h1_ref, out_ref) in enumerate(((a0_ref, a1_ref, outa_ref), (b0_ref, b1_ref, outb_ref))):
+        h = jnp.concatenate([h0_ref[...], h1_ref[...]], axis=0)
         gate_proj = jnp.dot(h, sg_ref[...], preferred_element_type=F32)
         act = (jax.nn.silu(gate_proj) * jnp.dot(h, su_ref[...], preferred_element_type=F32)).astype(BF16)
         part = jnp.dot(act, sd_ref[...], preferred_element_type=F32)
@@ -86,8 +96,9 @@
             out_ref[...] = x_ref[i].astype(F32) + jax.nn.sigmoid(weight) * out_ref[...]
 
 
-def shared_call(hidden_in, ha, hb, w_sgate, s_gate, s_up, s_down):
-    half, hidden = ha.shape
+def shared_call(hidden_in, quarters, w_sgate, s_gate, s_up, s_down):
+    half, hidden = 2 * quarters[0].shape[0], quarters[0].shape[1]
+    quarter = pl.BlockSpec((half // 2, hidden), lambda i: (0, 0), pipeline_mode=pl.Buffered(1))
     ff = s_gate.shape[1]
     chunk = 256
     whole = pl.BlockSpec((half, hidden), lambda i: (0, 0), pipeline_mode=pl.Buffered(1))
@@ -97,13 +108,13 @@
         shared_kernel,
         grid=(ff // chunk,),
         out_shape=(out, out),
-        in_specs=[pl.BlockSpec((2, half, hidden), lambda i: (0, 0, 0), pipeline_mode=pl.Buffered(1)), whole, whole,
-                  pl.BlockSpec((1, hidden), lambda i: (0, 0)), wide, wide, pl.BlockSpec((chunk, hidden), lambda i: (i, 0))],
+        in_specs=[pl.BlockSpec((2, half, hidden), lambda i: (0, 0, 0), pipeline_mode=pl.Buffered(1))] + [quarter] * 4
+        + [pl.BlockSpec((1, hidden), lambda i: (0, 0)), wide, wide, pl.BlockSpec((chunk, hidden), lambda i: (i, 0))],
         out_specs=(whole, whole),
         compiler_params=pltpu.CompilerParams(dimension_semantics=("arbitrary",), vmem_limit_bytes=60 * 1024 * 1024),
         cost_estimate=pl.CostEstimate(flops=1_000_000, transcendentals=0, bytes_accessed=6 * ff * hidden),
         name="shared",
-    )(hidden_in.reshape(2, half, hidden), ha, hb, w_sgate.reshape(1, hidden), s_gate, s_up, s_down)
+    )(hidden_in.reshape(2, half, hidden), *quarters, w_sgate.reshape(1, hidden), s_gate, s_up, s_down)
 
 
 def route_kernel(geom, ids_ref, own_ref, next_ref, far_ref, prev_ref, list_ref, glist_ref, count_ref, slot_ref, gate_ref):
@@ -223,7 +234,7 @@
         return got
 
     lists, glists, counts = take(n_src), take(n_src), take(n_src)
-    has, hbs = take(n_src), take(n_src)
+    quarters = take(4)
     own, sib = take(3), take(3)
     take(1)
     ys = take(len(sizes))
@@ -232,7 +243,7 @@
     stage_ref, sems, out_sems = take(3)
     step = pl.program_id(0)
     steps = 2 * slots_dev
-    half, hidden = has[0].shape
+    half, hidden = 2 * quarters[0].shape[0], quarters[0].shape[1]
     blocks = hidden // 128
     pitch, unroll, group = 8, 8, 64
     split = [(j // pitch, j % pitch) for j in range(blocks)]
@@ -263,13 +274,13 @@
                 ref[pl.ds(2 * half * pitch, pitch), :] = jnp.zeros((pitch, 128), F32)
 
             def spread(i, carry):
-                for src, start in ((has[q], 0), (hbs[q], half)):
+                for src, start in zip(quarters, range(0, 2 * half, half // 2)):
                     v = src[pl.ds(pl.multiple_of(i * group, group), group), :].astype(F32)
                     for j, (w, k) in enumerate(split):
                         tok_refs[q][w][pl.ds((start + i * group) * pitch + k, group, stride=pitch), :] = v[:, j * 128:(j + 1) * 128]
                 return carry
 
-            lax.fori_loop(0, half // group, spread, 0)
+            lax.fori_loop(0, half // 2 // group, spread, 0)
 
     fetch(step + depth - 1)
     buf = step % depth
@@ -350,12 +361,12 @@
                 pltpu.make_async_copy(stage_ref.at[i, n], ref.at[pl.ds(0, group)], out_sems.at[i, n]).wait()
 
 
-def expert_call(routes, ha, hb, own, sib, dep, row_max, sizes):
-    half, hidden = ha.shape
+def expert_call(routes, quarters, own, sib, dep, row_max, sizes):
+    half, hidden = 2 * quarters[0].shape[0], quarters[0].shape[1]
     slots_dev, _, ff = own[0].shape
     depth = 4
     classes = tuple(c for c in CLASSES if c < row_max) + (row_max,)
-    whole = pl.BlockSpec((half, hidden), lambda s: (0, 0), pipeline_mode=pl.Buffered(1))
+    quarter = pl.BlockSpec((half // 2, hidden), lambda s: (0, 0), pipeline_mode=pl.Buffered(1))
     smem = pl.BlockSpec(memory_space=pltpu.SMEM)
     hbm = pl.BlockSpec(memory_space=pl.ANY)
     pieces = len(sizes)
@@ -364,7 +375,7 @@
         functools.partial(expert_kernel, sizes, classes, slots_dev, depth),
         grid=(2 * slots_dev,),
         out_shape=tuple(jax.ShapeDtypeStruct((n, hidden), F32) for n in sizes),
-        in_specs=[smem] * 3 + [whole] * 2 + [hbm] * 7,
+        in_specs=[smem] * 3 + [quarter] * 4 + [hbm] * 7,
         out_specs=(hbm,) * pieces,
         scratch_shapes=[pltpu.VMEM((depth, hidden, ff), BF16), pltpu.VMEM((depth, hidden, ff), BF16), pltpu.VMEM((depth, ff, hidden), BF16)]
         + [pltpu.VMEM((row_max * 8, 128), F32)] * 2 + [pltpu.VMEM((toks, 128), F32)] * 4
@@ -373,7 +384,7 @@
         cost_estimate=pl.CostEstimate(flops=1_000_000, transcendentals=0,
                                       bytes_accessed=2 * slots_dev * 3 * hidden * ff * 2),
         name="experts",
-    )(*routes, ha, hb, *own, *sib, dep)
+    )(*routes, *quarters, *own, *sib, dep)
 
 
 def solution(mesh):
@@ -406,11 +417,11 @@
         def after(v, *deps):
             return lax.optimization_barrier((v,) + deps)[0]
 
-        ha, hb = norm_call(hidden_in, norm_gain)
-        ha_r1, hb_l1 = go_right(ha), go_left(hb)
-
-        logits = jnp.concatenate([jnp.dot(h, w_router, preferred_element_type=F32) for h in (ha, hb)], axis=0)
-        router_probs = jax.nn.softmax(logits, axis=-1)
+        *quarters, logits = norm_call(hidden_in, norm_gain, w_router)
+        ha, hb = quarters[:2], quarters[2:]
+        first = go_right(ha[0]), go_left(hb[0])
+
+        router_probs = jax.nn.softmax(logits.reshape(tok_dev, experts), axis=-1)
         chosen = topk_idx[:, :, None] == jnp.arange(experts)[None, None, :]
         gate_vals = jnp.sum(jnp.where(chosen, router_probs[:, None, :], 0.0), axis=-1)
         own_counts = jnp.sum(chosen.astype(F32), axis=(0, 1)).reshape(1, experts)
@@ -418,14 +429,14 @@
         count_rows = jnp.pad(jnp.concatenate([own_counts, sib_counts], axis=0), ((0, (-2 * top_k - 2) % 8), (0, tok_dev - experts)))
         table = jnp.concatenate([topk_idx.T.astype(F32), gate_vals.T, count_rows], axis=0)
         own_w = (w_gate, w_up, w_down)
-        sib_w = tuple(lax.ppermute(after(w, sib_counts), 'ep', sibling) for w in own_w)
+        sib_w = tuple(lax.ppermute(w, 'ep', sibling) for w in (w_gate, after(w_up, sib_counts), after(w_down, sib_counts)))
         t_r1, t_l1 = go_right(table), go_left(table)
         t_far = lax.ppermute(table, 'ep', far)
 
-        hb_r1, ha_l1 = go_right(hb), go_left(ha)
-        half_sums = shared_call(hidden_in, ha, hb, w_sgate, s_gate, s_up, s_down)
-
-        ha_r2, hb_l2 = go_right(ha_r1), go_left(hb_l1)
+        second = go_right(ha[1]), go_left(hb[1])
+        ha_r1, hb_l1 = [first[0], second[0]], [first[1], second[1]]
+        hb_r1, ha_l1 = [go_right(h) for h in hb], [go_left(h) for h in ha]
+        ha_r2, hb_l2 = [go_right(h) for h in ha_r1], [go_left(h) for h in hb_l1]
 
         steps = jnp.arange(group_size // cores)
         rel = cores * ((chip + steps) % (group_size // cores))
@@ -437,20 +448,21 @@
         def routes(v, row_max):
             return lists[v, :, :row_max], glists[v, :, :row_max], kept[v]
 
-        d_a, d_b = expert_call(routes(1, 2 * local_max), ha_r1, hb_l1, own_w, sib_w, ha, 2 * local_max, (half, half))
+        d_a, d_b = expert_call(routes(1, 2 * local_max), ha_r1 + hb_l1, own_w, sib_w, ha[0], 2 * local_max, (half, half))
         d_dep, d_a, d_b = d_a, go_left(d_a), go_right(d_b)
-        y2 = expert_call(routes(2, local_max), ha_r2, hb_l2, own_w, sib_w, d_dep, local_max, parts * 2)
+        y0 = expert_call(routes(0, local_max), quarters, own_w, sib_w, d_dep, local_max, (half, half))
+        y2 = expert_call(routes(2, local_max), ha_r2 + hb_l2, own_w, sib_w, y0[0], local_max, parts * 2)
         p = [go_right(y2[0]), go_left(y2[2])]
         p += [go_right(y2[1]), go_left(y2[3])]
-        y1 = expert_call(routes(3, 2 * local_max), ha_l1, hb_r1, own_w, sib_w, y2[0], 2 * local_max, parts * 2)
+        y1 = expert_call(routes(3, 2 * local_max), ha_l1 + hb_r1, own_w, sib_w, y2[0], 2 * local_max, parts * 2)
+        half_sums = shared_call(hidden_in, [after(quarters[0], y1[0])] + quarters[1:], w_sgate, s_gate, s_up, s_down)
 
         def relay(i, *deps):
             return y1[i] + after(p[2 * i], *deps), y1[2 + i] + after(p[2 * i + 1], *deps)
 
-        add_a, add_b = relay(0, y1[0])
+        add_a, add_b = relay(0, half_sums[0])
         z0 = go_right(add_a), go_left(add_b)
-        y0 = expert_call(routes(0, local_max), ha, hb, own_w, sib_w, add_b, local_max, (half, half))
-        add_a, add_b = relay(1, y0[0])
+        add_a, add_b = relay(1, add_a, add_b)
         z1 = go_right(add_a), go_left(add_b)
         base = [half_sums[i] + y0[i] + d for i, d in enumerate((d_a, d_b))]
         out = final_call(0, base[0], base[1], *z0, None)

time: 399 us -> 477 us (1.20)
  waiting for transfers between devices: 118 us -> 185 us
  starting transfers between devices: 40.2 us -> 50.2 us
    ppermute x9 -> x12, waiting for transfers between devices: 2.81 us -> 58.8 us  [go_left(): return lax.ppermute(v, 'ep', left)]
    ppermute x9 -> x12, waiting for transfers between devices: 111 us -> 124 us  [go_right(): return lax.ppermute(v, 'ep', right)]
    ppermute x9 -> x12, starting transfers between devices: 9.37 us -> 15 us  [go_right(): return lax.ppermute(v, 'ep', right)]
    ppermute x9 -> x12, starting transfers between devices: 29.5 us -> 31 us  [go_left(): return lax.ppermute(v, 'ep', left)]
  transfers between devices with their start and end apart: 23 -> 29, of which waited for: 8 -> 13; matrix products, arithmetic and copies ran while one was open for 7% -> 5% of each run, Pallas kernels for 50% -> 42%
where the time goes in v6:
time: 477 us; the launch traced here: 476 us
  Pallas kernels  209 us (44%)
  waiting for transfers between devices  185 us (39%)
  starting transfers between devices  50.2 us (11%)
  other arithmetic  23.1 us (5%)
  local copies, waits for them, and re-layouts  9.29 us (2%)
    pallas_call x4, Pallas kernels, expert_call(): pl.pallas_call(functools.partial(expert_kernel, sizes, classes, slots_dev...  157 us
    ppermute x12, waiting for transfers between devices, go_right(): return lax.ppermute(v, 'ep', right)  124 us
    ppermute x12, waiting for transfers between devices, go_left(): return lax.ppermute(v, 'ep', left)  58.8 us
    ppermute x12, starting transfers between devices, go_left(): return lax.ppermute(v, 'ep', left)  31 us
    pallas_call x1, Pallas kernels, shared_call(): pl.pallas_call(shared_kernel, grid=(ff // chunk,), out_shape=(out, out),...  21.2 us
    ppermute x12, starting transfers between devices, go_right(): return lax.ppermute(v, 'ep', right)  15 us
    pallas_call x1, Pallas kernels, route_call(): pl.pallas_call(functools.partial(route_kernel, (top_k, slots_dev, capacit...  14.9 us
  transfers between devices with their start and end apart: 29, of which 13 were waited for; matrix products, arithmetic and copies ran while one was open for 5% of the time, Pallas kernels for 42%

profile of v6, /device:TPU:88, one launch (start us, length us, event | category | flops | bytes accessed | tf_op | source)
XLA Modules:
  0.0 476.4 jit_solution(15842245931652978169)
XLA Ops:
  0.0 1.9 copy.29.wr_ref
  1.9 6.4 %norm.1 = (bf16[256,1536]{1,0:T(8,128)(2,1)}, bf16[256,1536]{1,0:T(8,128)(2,1)}, bf16[256,1536]{1,0:T(8,128)(2,1)}, bf16[256,1536]{1,0:T(8,128)(2,1)}, f32[2,512,64]{2,1,0:T(8,128)}) custom-call(bf16[2,512,1536]{2,1,0:T(8,128)(2,1)} %bitcast.39, bf16[1536]{0:T(1024)(128)(2,1)} %gain_ref.1, bf16[1536,64]{1,0:T(8,128)(2,1)} %copy.29.wr_ref), custom_call_target="tpu_custom_call" | custom-call | flops 6291456 | bytes 6291456 | tf_op jit(solution)/shard_map/norm/pallas_call | solution.py:38
  8.3 1.4 reduce_max.9
  9.7 1.4 exponential_reduce_fusion
  11.2 1.4 fusion.1
  14.9 1.7 collective-permute-start.3
  16.7 3.0 collective-permute-start.2
  19.7 1.0 collective-permute-done.3.prev_ref
  20.6 2.4 collective-permute-start.1
  23.2 1.3 collective-permute-start.13
  25.0 3.6 collective-permute-start.15
  29.4 14.9 %route.1 = (s32[4,16,8,384]{3,2,1,0:T(8,128)}, f32[4,16,8,384]{3,2,1,0:T(8,128)}, f32[4,16,128]{2,1,0:T(8,128)}) custom-call(s32[10]{0:T(128)} %pad_add_fusion.1.ids_ref, f32[16,1024]{1,0:T(8,128)} %copy-done.21, f32[16,1024]{1,0:T(8,128)} %copy-done.25, f32[16,1024]{1,0:T(8,128)} %copy-done.24, f32[16,1024]{1,0:T(8,128)} %copy-done.23), custom_call_target="tpu_custom_call" | custom-call | flops 1000000 | bytes 2000000 | tf_op jit(solution)/shard_map/route/pallas_call | solution.py:215
  44.3 1.4 copy.33
  45.8 2.0 collective-permute-start.11
  47.8 1.3 copy.34
  49.8 13.9 %collective-permute-done.17.refs_6_ = bf16[256,1536]{1,0:T(8,128)(2,1)} collective-permute-done((bf16[256,1536]{1,0:T(8,128)(2,1)}, bf16[256,1536]{1,0:T(8,128)(2,1)}, u32[]{:S(2)}, u32[]{:S(2)}) %collective-permute-start.17) | collective-permute-done | bytes 786464 | tf_op jit(solution)/shard_map/ppermute | solution.py:413
  64.1 1.7 collective-permute-start.14
  65.7 1.6 collective-permute-start.16
  67.4 1.4 collective-permute-done.10.refs_12_
  68.8 1.6 collective-permute-start.12
  73.4 40.2 %experts.4 = (f32[512,1536]{1,0:T(8,128)}, f32[512,1536]{1,0:T(8,128)}) custom-call(s32[16,384]{1,0:T(8,128)} %get-tuple-element.72.refs_0_, f32[16,384]{1,0:T(8,128)} %get-tuple-element.70.refs_1_, s32[16]{0:T(128)} %get-tuple-element.64.refs_2_, bf16[256,1536]{1,0:T(8,128)(2,1)} %copy-done.13, bf16[256,1536]{1,0:T(8,128)(2,1)} %collective-permute-done.13.refs_4_, ...), custom_call_target="tpu_custom_call" | custom-call | flops 1000000 | bytes 75497472 | tf_op jit(solution)/shard_map/experts/pallas_call | solution.py:374
  113.5 40.6 %experts.5 = (f32[512,1536]{1,0:T(8,128)}, f32[512,1536]{1,0:T(8,128)}) custom-call(s32[16,192]{1,0:T(8,128)} %get-tuple-element.75.refs_0_, f32[16,192]{1,0:T(8,128)} %get-tuple-element.73.refs_1_, s32[16]{0:T(128)} %get-tuple-element.63.refs_2_, bf16[256,1536]{1,0:T(8,128)(2,1)} %get-tuple-element.48.refs_13_.refs_3_.a0_ref, ...), custom_call_target="tpu_custom_call" | custom-call | flops 1000000 | bytes 75497472 | tf_op jit(solution)/shard_map/experts/pallas_call | solution.py:374
  154.2 38.4 %experts.6 = (f32[384,1536]{1,0:T(8,128)}, f32[128,1536]{1,0:T(8,128)}, f32[384,1536]{1,0:T(8,128)}, f32[128,1536]{1,0:T(8,128)}) custom-call(s32[16,192]{1,0:T(8,128)} %get-tuple-element.76.refs_0_, f32[16,192]{1,0:T(8,128)} %get-tuple-element.74.refs_1_, s32[16]{0:T(128)} %get-tuple-element.65.refs_2_, bf16[256,1536]{1,0:T(8,128)(2,1)} %collective-permute-done.12.refs_3_, ...), custom_call_target="tpu_custom_call" | custom-call | flops 1000000 | bytes 75497472 | tf_op jit(solution)/shard_map/experts/pallas_call | solution.py:374
  192.7 3.9 collective-permute-start.23
  196.6 6.2 %collective-permute-start.19 = (f32[512,1536]{1,0:T(8,128)}, f32[512,1536]{1,0:T(8,128)}, u32[]{:S(2)}, u32[]{:S(2)}) collective-permute-start(f32[512,1536]{1,0:T(8,128)} %get-tuple-element.44.refs_13_), channel_id=1, source_target_pairs={{0,6},{1,7},{2,0},{3,1},{4,2},{5,3},{6,4},{7,5},{8,14},{9,15},{10,... | collective-permute-start | bytes 9437192 | tf_op jit(solution)/shard_map/ppermute | solution.py:413
  202.8 1.5 collective-permute-start.7
  204.3 20.3 %collective-permute-done.6.refs_5_ = bf16[256,1536]{1,0:T(8,128)(2,1)S(1)} collective-permute-done((bf16[256,1536]{1,0:T(8,128)(2,1)}, bf16[256,1536]{1,0:T(8,128)(2,1)S(1)}, u32[]{:S(2)}, u32[]{:S(2)}) %collective-permute-start.6) | collective-permute-done | bytes 786464 | tf_op jit(solution)/shard_map/ppermute | solution.py:410
  224.6 67.4 %collective-permute-done.7.refs_6_ = bf16[256,1536]{1,0:T(8,128)(2,1)S(1)} collective-permute-done((bf16[256,1536]{1,0:T(8,128)(2,1)}, bf16[256,1536]{1,0:T(8,128)(2,1)S(1)}, u32[]{:S(2)}, u32[]{:S(2)}) %collective-permute-start.7) | collective-permute-done | bytes 786464 | tf_op jit(solution)/shard_map/ppermute | solution.py:410
  292.0 40.6 %collective-permute-done.4.refs_3_ = bf16[256,1536]{1,0:T(8,128)(2,1)S(1)} collective-permute-done((bf16[256,1536]{1,0:T(8,128)(2,1)S(1)}, bf16[256,1536]{1,0:T(8,128)(2,1)S(1)}, u32[]{:S(2)}, u32[]{:S(2)}) %collective-permute-start.4) | collective-permute-done | bytes 786464 | tf_op jit(solution)/shard_map/ppermute | solution.py:413
  332.6 0.9 copy-done.16
  333.5 3.7 collective-permute-start.25
  337.2 37.9 %experts.7 = (f32[384,1536]{1,0:T(8,128)}, f32[128,1536]{1,0:T(8,128)}, f32[384,1536]{1,0:T(8,128)}, f32[128,1536]{1,0:T(8,128)}) custom-call(s32[16,384]{1,0:T(8,128)} %get-tuple-element.71.refs_0_, f32[16,384]{1,0:T(8,128)} %get-tuple-element.69.refs_1_, s32[16]{0:T(128)} %get-tuple-element.66.refs_2_, bf16[256,1536]{1,0:T(8,128)(2,1)} %copy-done.16, ...), custom_call_target="tpu_custom_call" | custom-call | flops 1000000 | bytes 75497472 | tf_op jit(solution)/shard_map/experts/pallas_call | solution.py:374
  375.1 21.2 %shared.1 = (f32[512,1536]{1,0:T(8,128)}, f32[512,1536]{1,0:T(8,128)}) custom-call(bf16[2,512,1536]{2,1,0:T(8,128)(2,1)} %bitcast.40, bf16[256,1536]{1,0:T(8,128)(2,1)} %get-tuple-element.48.refs_13_.refs_3_.a0_ref, bf16[256,1536]{1,0:T(8,128)(2,1)} %get-tuple-element.39.refs_4_.a1_ref, bf16[256,1536]{1,0:T(8,128)(2,1)} %get-tuple-element.40.refs_5_.b0_ref, ...), custom_call_target="tpu_custom_call" | custom-call | flops 1000000 | bytes 9437184 | tf_op jit(solution)/shard_map/shared/pallas_call | solution.py:107
  396.4 2.2 add.99
  398.6 5.2 %collective-permute-start.27 = (f32[384,1536]{1,0:T(8,128)S(1)}, f32[384,1536]{1,0:T(8,128)S(1)}, u32[]{:S(2)}, u32[]{:S(2)}) collective-permute-start(f32[384,1536]{1,0:T(8,128)S(1)} %add.99), channel_id=1, source_target_pairs={{0,2},{1,3},{2,4},{3,5},{4,6},{5,7},{6,0},{7,1},{8,10},{9,11},{10,... | collective-permute-start | bytes 7077896 | tf_op jit(solution)/shard_map/ppermute | solution.py:410
  403.8 2.2 add.100
  406.0 5.6 %collective-permute-start.28 = (f32[384,1536]{1,0:T(8,128)S(1)}, f32[384,1536]{1,0:T(8,128)}, u32[]{:S(2)}, u32[]{:S(2)}) collective-permute-start(f32[384,1536]{1,0:T(8,128)S(1)} %add.100), channel_id=1, source_target_pairs={{0,6},{1,7},{2,0},{3,1},{4,2},{5,3},{6,4},{7,5},{8,14},{9,15},{10,... | collective-permute-start | bytes 7077896 | tf_op jit(solution)/shard_map/ppermute | solution.py:413
  411.5 2.1 add.101
  413.7 2.1 add.102
  415.8 3.6 collective-permute-start.26
  419.4 4.6 add_add_fusion.1.base_a
  424.1 4.5 add_add_fusion.base_b
  428.6 32.7 %collective-permute-done.27.za_ref = f32[384,1536]{1,0:T(8,128)S(1)} collective-permute-done((f32[384,1536]{1,0:T(8,128)S(1)}, f32[384,1536]{1,0:T(8,128)S(1)}, u32[]{:S(2)}, u32[]{:S(2)}) %collective-permute-start.27) | collective-permute-done | bytes 2359328 | tf_op jit(solution)/shard_map/ppermute | solution.py:410
  461.3 1.9 collective-permute-done.28.zb_ref
  463.2 6.3 %final.2.rest_0_ = bf16[2,512,1536]{2,1,0:T(8,128)(2,1)} custom-call(f32[512,1536]{1,0:T(8,128)} %add_add_fusion.1.base_a, f32[512,1536]{1,0:T(8,128)} %add_add_fusion.base_b, f32[384,1536]{1,0:T(8,128)} %copy-done.10, f32[384,1536]{1,0:T(8,128)} %collective-permute-done.28.zb_ref), custom_call_target="tpu_custom_call" | custom-call | flops 2359296 | bytes 11796480 | tf_op jit(solution)/shard_map/final/pallas_call | solution.py:64
  469.4 2.4 collective-permute-done.24.za_ref
  471.8 1.9 collective-permute-done.26.zb_ref
  473.7 2.7 final.3
  (106 shorter events, 7.9 us)
Async XLA Ops:
  1.9 10.9 %copy-start.22 = (s32[1024,6]{0,1:T(8,128)S(1)}, s32[1024,6]{0,1:T(8,128)}, u32[]{:S(2)}) copy-start(s32[1024,6]{0,1:T(8,128)} %param.12) | copy-start | bytes 73732
  8.3 14.9 %copy-start.3 = (bf16[256,1536]{1,0:T(8,128)(2,1)S(1)}, bf16[256,1536]{1,0:T(8,128)(2,1)}, u32[]{:S(2)}) copy-start(bf16[256,1536]{1,0:T(8,128)(2,1)} %get-tuple-element.39.refs_4_.a1_ref) | copy-start | bytes 2359300
  8.3 16.7 %copy-start.4 = (bf16[256,1536]{1,0:T(8,128)(2,1)S(1)}, bf16[256,1536]{1,0:T(8,128)(2,1)}, u32[]{:S(2)}) copy-start(bf16[256,1536]{1,0:T(8,128)(2,1)} %get-tuple-element.40.refs_5_.b0_ref) | copy-start | bytes 2359300
  8.3 37.5 %copy-start.1 = (bf16[256,1536]{1,0:T(8,128)(2,1)S(1)}, bf16[256,1536]{1,0:T(8,128)(2,1)}, u32[]{:S(2)}) copy-start(bf16[256,1536]{1,0:T(8,128)(2,1)} %get-tuple-element.48.refs_13_.refs_3_.a0_ref) | copy-start | bytes 2359300
  13.1 1.3 collective-permute-start
  13.2 52.5 %collective-permute-start.8 = (bf16[8,1536,512]{2,1,0:T(8,128)(2,1)}, bf16[8,1536,512]{2,1,0:T(8,128)(2,1)}, u32[]{:S(2)}, u32[]{:S(2)}) collective-permute-start(bf16[8,1536,512]{2,1,0:T(8,128)(2,1)} %refs_7_.7), channel_id=1, source_target_pairs={{0,1},{1,0},{2,3},{3,2},{4,5},{5,4},{6,7},{7,6},{8,9},{9,8},{10,11... | collective-permute-start | bytes 37748744 | tf_op jit(solution)/shard_map/ppermute | solution.py:432
  14.4 52.9 %collective-permute-start.9 = (bf16[8,1536,512]{2,1,0:T(8,128)(2,1)}, bf16[8,1536,512]{2,1,0:T(8,128)(2,1)}, u32[]{:S(2)}, u32[]{:S(2)}) collective-permute-start(bf16[8,1536,512]{2,1,0:T(8,128)(2,1)} %refs_8_.7), channel_id=1, source_target_pairs={{0,1},{1,0},{2,3},{3,2},{4,5},{5,4},{6,7},{7,6},{8,9},{9,8},{10,11... | collective-permute-start | bytes 37748744 | tf_op jit(solution)/shard_map/ppermute | solution.py:432
  14.5 54.3 %collective-permute-start.10 = (bf16[8,512,1536]{2,1,0:T(8,128)(2,1)}, bf16[8,512,1536]{2,1,0:T(8,128)(2,1)}, u32[]{:S(2)}, u32[]{:S(2)}) collective-permute-start(bf16[8,512,1536]{2,1,0:T(8,128)(2,1)} %refs_9_.7), channel_id=1, source_target_pairs={{0,1},{1,0},{2,3},{3,2},{4,5},{5,4},{6,7},{7,6},{8,9},{9,8},{10,11... | collective-permute-start | bytes 37748744 | tf_op jit(solution)/shard_map/ppermute | solution.py:432
  14.9 14.4 %copy-start.21 = (f32[16,1024]{1,0:T(8,128)}, f32[16,1024]{1,0:T(8,128)S(1)}, u32[]{:S(2)}) copy-start(f32[16,1024]{1,0:T(8,128)S(1)} %pad_maximum_fusion.own_ref) | copy-start | bytes 196612
  14.9 5.7 %collective-permute-start.3 = (f32[16,1024]{1,0:T(8,128)S(1)}, f32[16,1024]{1,0:T(8,128)S(1)}, u32[]{:S(2)}, u32[]{:S(2)}) collective-permute-start(f32[16,1024]{1,0:T(8,128)S(1)} %pad_maximum_fusion.own_ref), channel_id=1, source_target_pairs={{0,2},{1,3},{2,4},{3,5},{4,6},{5,7},{6,0},{7,1},{8,10},{9,11},{10,... | collective-permute-start | bytes 196616 | tf_op jit(solution)/shard_map/ppermute | solution.py:410
  16.7 6.5 %collective-permute-start.2 = (f32[16,1024]{1,0:T(8,128)S(1)}, f32[16,1024]{1,0:T(8,128)S(1)}, u32[]{:S(2)}, u32[]{:S(2)}) collective-permute-start(f32[16,1024]{1,0:T(8,128)S(1)} %pad_maximum_fusion.own_ref), channel_id=1, source_target_pairs={{0,4},{1,5},{2,6},{3,7},{4,0},{5,1},{6,2},{7,3},{8,12},{9,13},{10,... | collective-permute-start | bytes 196616 | tf_op jit(solution)/shard_map/ppermute | solution.py:434
  20.6 8.7 %copy-start.23 = (f32[16,1024]{1,0:T(8,128)}, f32[16,1024]{1,0:T(8,128)S(1)}, u32[]{:S(2)}) copy-start(f32[16,1024]{1,0:T(8,128)S(1)} %collective-permute-done.3.prev_ref) | copy-start | bytes 196612
  20.6 4.3 collective-permute-start.1
  23.2 22.5 %collective-permute-start.13 = (bf16[256,1536]{1,0:T(8,128)(2,1)S(1)}, bf16[256,1536]{1,0:T(8,128)(2,1)}, u32[]{:S(2)}, u32[]{:S(2)}) collective-permute-start(bf16[256,1536]{1,0:T(8,128)(2,1)S(1)} %copy-done.3), channel_id=1, source_target_pairs={{0,2},{1,3},{2,4},{3,5},{4,6},{5,7},{6,0},{7,1},{8,10},{9,11},{10,... | collective-permute-start | bytes 2359304 | tf_op jit(solution)/shard_map/ppermute | solution.py:410
  25.0 20.9 %collective-permute-start.15 = (bf16[256,1536]{1,0:T(8,128)(2,1)S(1)}, bf16[256,1536]{1,0:T(8,128)(2,1)}, u32[]{:S(2)}, u32[]{:S(2)}) collective-permute-start(bf16[256,1536]{1,0:T(8,128)(2,1)S(1)} %copy-done.4), channel_id=1, source_target_pairs={{0,6},{1,7},{2,0},{3,1},{4,2},{5,3},{6,4},{7,5},{8,14},{9,15},{10,... | collective-permute-start | bytes 2359304 | tf_op jit(solution)/shard_map/ppermute | solution.py:413
  44.3 26.8 %copy-start.6 = (s32[4,16,8,384]{3,2,1,0:T(8,128)S(1)}, s32[4,16,8,384]{3,2,1,0:T(8,128)}, u32[]{:S(2)}) copy-start(s32[4,16,8,384]{3,2,1,0:T(8,128)} %get-tuple-element.36) | copy-start | bytes 2359300
  44.3 26.9 %copy-start.5 = (f32[4,16,8,384]{3,2,1,0:T(8,128)S(1)}, f32[4,16,8,384]{3,2,1,0:T(8,128)}, u32[]{:S(2)}) copy-start(f32[4,16,8,384]{3,2,1,0:T(8,128)} %get-tuple-element.37) | copy-start | bytes 2359300
  45.7 18.0 %collective-permute-start.17 = (bf16[256,1536]{1,0:T(8,128)(2,1)}, bf16[256,1536]{1,0:T(8,128)(2,1)}, u32[]{:S(2)}, u32[]{:S(2)}) collective-permute-start(bf16[256,1536]{1,0:T(8,128)(2,1)} %get-tuple-element.41.refs_6_.b1_ref), channel_id=1, source_target_pairs={{0,6},{1,7},{2,0},{3,1},{4,2},{5,3},{6,4},{7,5},{8,14},{9,15},{10,... | collective-permute-start | bytes 2359304 | tf_op jit(solution)/shard_map/ppermute | solution.py:413
  45.8 18.2 %collective-permute-start.11 = (bf16[256,1536]{1,0:T(8,128)(2,1)S(1)}, bf16[256,1536]{1,0:T(8,128)(2,1)S(1)}, u32[]{:S(2)}, u32[]{:S(2)}) collective-permute-start(bf16[256,1536]{1,0:T(8,128)(2,1)S(1)} %copy-done.1), channel_id=1, source_target_pairs={{0,2},{1,3},{2,4},{3,5},{4,6},{5,7},{6,0},{7,1},{8,10},{9,11},{10,... | collective-permute-start | bytes 2359304 | tf_op jit(solution)/shard_map/ppermute | solution.py:410
  63.7 139.0 %collective-permute-start.5 = (bf16[256,1536]{1,0:T(8,128)(2,1)S(1)}, bf16[256,1536]{1,0:T(8,128)(2,1)}, u32[]{:S(2)}, u32[]{:S(2)}) collective-permute-start(bf16[256,1536]{1,0:T(8,128)(2,1)S(1)} %copy-done.3), channel_id=1, source_target_pairs={{0,6},{1,7},{2,0},{3,1},{4,2},{5,3},{6,4},{7,5},{8,14},{9,15},{10,... | collective-permute-start | bytes 2359304 | tf_op jit(solution)/shard_map/ppermute | solution.py:413
  64.1 9.3 %copy-start.13 = (bf16[256,1536]{1,0:T(8,128)(2,1)}, bf16[256,1536]{1,0:T(8,128)(2,1)S(1)}, u32[]{:S(2)}) copy-start(bf16[256,1536]{1,0:T(8,128)(2,1)S(1)} %collective-permute-done.11.refs_3_) | copy-start | bytes 2359300
  64.1 90.1 %collective-permute-start.14 = (bf16[256,1536]{1,0:T(8,128)(2,1)}, bf16[256,1536]{1,0:T(8,128)(2,1)}, u32[]{:S(2)}, u32[]{:S(2)}) collective-permute-start(bf16[256,1536]{1,0:T(8,128)(2,1)} %collective-permute-done.13.refs_4_), channel_id=1, source_target_pairs={{0,2},{1,3},{2,4},{3,5},{4,6},{5,7},{6,0},{7,1},{8,10},{9,11},{10,... | collective-permute-start | bytes 2359304 | tf_op jit(solution)/shard_map/ppermute | solution.py:410
  65.7 88.4 %collective-permute-start.16 = (bf16[256,1536]{1,0:T(8,128)(2,1)}, bf16[256,1536]{1,0:T(8,128)(2,1)}, u32[]{:S(2)}, u32[]{:S(2)}) collective-permute-start(bf16[256,1536]{1,0:T(8,128)(2,1)} %collective-permute-done.15.refs_5_), channel_id=1, source_target_pairs={{0,6},{1,7},{2,0},{3,1},{4,2},{5,3},{6,4},{7,5},{8,14},{9,15},{10,... | collective-permute-start | bytes 2359304 | tf_op jit(solution)/shard_map/ppermute | solution.py:413
  67.3 86.9 %collective-permute-start.18 = (bf16[256,1536]{1,0:T(8,128)(2,1)}, bf16[256,1536]{1,0:T(8,128)(2,1)}, u32[]{:S(2)}, u32[]{:S(2)}) collective-permute-start(bf16[256,1536]{1,0:T(8,128)(2,1)} %collective-permute-done.17.refs_6_), channel_id=1, source_target_pairs={{0,6},{1,7},{2,0},{3,1},{4,2},{5,3},{6,4},{7,5},{8,14},{9,15},{10,... | collective-permute-start | bytes 2359304 | tf_op jit(solution)/shard_map/ppermute | solution.py:413
  68.8 85.4 %collective-permute-start.12 = (bf16[256,1536]{1,0:T(8,128)(2,1)S(1)}, bf16[256,1536]{1,0:T(8,128)(2,1)}, u32[]{:S(2)}, u32[]{:S(2)}) collective-permute-start(bf16[256,1536]{1,0:T(8,128)(2,1)S(1)} %collective-permute-done.11.refs_3_), channel_id=1, source_target_pairs={{0,2},{1,3},{2,4},{3,5},{4,6},{5,7},{6,0},{7,1},{8,10},{9,11},{10,... | collective-permute-start | bytes 2359304 | tf_op jit(solution)/shard_map/ppermute | solution.py:410
  154.2 137.8 %copy-start.2 = (bf16[256,1536]{1,0:T(8,128)(2,1)S(1)}, bf16[256,1536]{1,0:T(8,128)(2,1)}, u32[]{:S(2)}) copy-start(bf16[256,1536]{1,0:T(8,128)(2,1)} %get-tuple-element.48.refs_13_.refs_3_.a0_ref) | copy-start | bytes 2359300
  192.7 144.5 %collective-permute-start.23 = (f32[384,1536]{1,0:T(8,128)}, f32[384,1536]{1,0:T(8,128)}, u32[]{:S(2)}, u32[]{:S(2)}) collective-permute-start(f32[384,1536]{1,0:T(8,128)} %get-tuple-element.57), channel_id=1, source_target_pairs={{0,6},{1,7},{2,0},{3,1},{4,2},{5,3},{6,4},{7,5},{8,14},{9,15},{10,... | collective-permute-start | bytes 7077896 | tf_op jit(solution)/shard_map/ppermute | solution.py:413
  196.6 219.3 %collective-permute-start.19 = (f32[512,1536]{1,0:T(8,128)}, f32[512,1536]{1,0:T(8,128)}, u32[]{:S(2)}, u32[]{:S(2)}) collective-permute-start(f32[512,1536]{1,0:T(8,128)} %get-tuple-element.44.refs_13_), channel_id=1, source_target_pairs={{0,6},{1,7},{2,0},{3,1},{4,2},{5,3},{6,4},{7,5},{8,14},{9,15},{10,... | collective-permute-start | bytes 9437192 | tf_op jit(solution)/shard_map/ppermute | solution.py:413
  202.7 21.8 %collective-permute-start.6 = (bf16[256,1536]{1,0:T(8,128)(2,1)}, bf16[256,1536]{1,0:T(8,128)(2,1)S(1)}, u32[]{:S(2)}, u32[]{:S(2)}) collective-permute-start(bf16[256,1536]{1,0:T(8,128)(2,1)} %get-tuple-element.40.refs_5_.b0_ref), channel_id=1, source_target_pairs={{0,2},{1,3},{2,4},{3,5},{4,6},{5,7},{6,0},{7,1},{8,10},{9,11},{10,... | collective-permute-start | bytes 2359304 | tf_op jit(solution)/shard_map/ppermute | solution.py:410
  202.7 193.6 %collective-permute-start.22 = (f32[384,1536]{1,0:T(8,128)}, f32[384,1536]{1,0:T(8,128)}, u32[]{:S(2)}, u32[]{:S(2)}) collective-permute-start(f32[384,1536]{1,0:T(8,128)} %get-tuple-element.46.refs_13_), channel_id=1, source_target_pairs={{0,2},{1,3},{2,4},{3,5},{4,6},{5,7},{6,0},{7,1},{8,10},{9,11},{10,... | collective-permute-start | bytes 7077896 | tf_op jit(solution)/shard_map/ppermute | solution.py:410
  202.8 89.2 %collective-permute-start.7 = (bf16[256,1536]{1,0:T(8,128)(2,1)}, bf16[256,1536]{1,0:T(8,128)(2,1)S(1)}, u32[]{:S(2)}, u32[]{:S(2)}) collective-permute-start(bf16[256,1536]{1,0:T(8,128)(2,1)} %get-tuple-element.41.refs_6_.b1_ref), channel_id=1, source_target_pairs={{0,2},{1,3},{2,4},{3,5},{4,6},{5,7},{6,0},{7,1},{8,10},{9,11},{10,... | collective-permute-start | bytes 2359304 | tf_op jit(solution)/shard_map/ppermute | solution.py:410
  224.6 108.0 %copy-start.14 = (bf16[256,1536]{1,0:T(8,128)(2,1)}, bf16[256,1536]{1,0:T(8,128)(2,1)S(1)}, u32[]{:S(2)}) copy-start(bf16[256,1536]{1,0:T(8,128)(2,1)S(1)} %collective-permute-done.6.refs_5_) | copy-start | bytes 2359300
  224.6 199.5 %collective-permute-start.20 = (f32[512,1536]{1,0:T(8,128)}, f32[512,1536]{1,0:T(8,128)}, u32[]{:S(2)}, u32[]{:S(2)}) collective-permute-start(f32[512,1536]{1,0:T(8,128)} %get-tuple-element.52), channel_id=1, source_target_pairs={{0,2},{1,3},{2,4},{3,5},{4,6},{5,7},{6,0},{7,1},{8,10},{9,11},{10,... | collective-permute-start | bytes 9437192 | tf_op jit(solution)/shard_map/ppermute | solution.py:410
  292.0 45.2 %copy-start.15 = (bf16[256,1536]{1,0:T(8,128)(2,1)}, bf16[256,1536]{1,0:T(8,128)(2,1)S(1)}, u32[]{:S(2)}) copy-start(bf16[256,1536]{1,0:T(8,128)(2,1)S(1)} %collective-permute-done.7.refs_6_) | copy-start | bytes 2359300
  292.0 40.6 %collective-permute-start.4 = (bf16[256,1536]{1,0:T(8,128)(2,1)S(1)}, bf16[256,1536]{1,0:T(8,128)(2,1)S(1)}, u32[]{:S(2)}, u32[]{:S(2)}) collective-permute-start(bf16[256,1536]{1,0:T(8,128)(2,1)S(1)} %copy-done.2), channel_id=1, source_target_pairs={{0,6},{1,7},{2,0},{3,1},{4,2},{5,3},{6,4},{7,5},{8,14},{9,15},{10,... | collective-permute-start | bytes 2359304 | tf_op jit(solution)/shard_map/ppermute | solution.py:413
  333.5 72.5 %collective-permute-start.25 = (f32[128,1536]{1,0:T(8,128)}, f32[128,1536]{1,0:T(8,128)S(1)}, u32[]{:S(2)}, u32[]{:S(2)}) collective-permute-start(f32[128,1536]{1,0:T(8,128)} %get-tuple-element.61), channel_id=1, source_target_pairs={{0,6},{1,7},{2,0},{3,1},{4,2},{5,3},{6,4},{7,5},{8,14},{9,15},{10,... | collective-permute-start | bytes 2359304 | tf_op jit(solution)/shard_map/ppermute | solution.py:413
  337.2 74.3 %collective-permute-start.21 = (f32[128,1536]{1,0:T(8,128)}, f32[128,1536]{1,0:T(8,128)}, u32[]{:S(2)}, u32[]{:S(2)}) collective-permute-start(f32[128,1536]{1,0:T(8,128)} %get-tuple-element.54), channel_id=1, source_target_pairs={{0,2},{1,3},{2,4},{3,5},{4,6},{5,7},{6,0},{7,1},{8,10},{9,11},{10,... | collective-permute-start | bytes 2359304 | tf_op jit(solution)/shard_map/ppermute | solution.py:410
  375.1 21.3 %copy-start.12 = (f32[384,1536]{1,0:T(8,128)S(1)}, f32[384,1536]{1,0:T(8,128)}, u32[]{:S(2)}) copy-start(f32[384,1536]{1,0:T(8,128)} %get-tuple-element.47) | copy-start | bytes 7077892
  398.6 62.7 %collective-permute-start.27 = (f32[384,1536]{1,0:T(8,128)S(1)}, f32[384,1536]{1,0:T(8,128)S(1)}, u32[]{:S(2)}, u32[]{:S(2)}) collective-permute-start(f32[384,1536]{1,0:T(8,128)S(1)} %add.99), channel_id=1, source_target_pairs={{0,2},{1,3},{2,4},{3,5},{4,6},{5,7},{6,0},{7,1},{8,10},{9,11},{10,... | collective-permute-start | bytes 7077896 | tf_op jit(solution)/shard_map/ppermute | solution.py:410
  403.7 7.8 %copy-start.20 = (f32[128,1536]{1,0:T(8,128)S(1)}, f32[128,1536]{1,0:T(8,128)}, u32[]{:S(2)}) copy-start(f32[128,1536]{1,0:T(8,128)} %get-tuple-element.53) | copy-start | bytes 2359300
  403.8 9.9 %copy-start.19 = (f32[128,1536]{1,0:T(8,128)S(1)}, f32[128,1536]{1,0:T(8,128)}, u32[]{:S(2)}) copy-start(f32[128,1536]{1,0:T(8,128)} %get-tuple-element.60) | copy-start | bytes 2359300
  403.8 15.7 %copy-start.9 = (f32[512,1536]{1,0:T(8,128)S(1)}, f32[512,1536]{1,0:T(8,128)}, u32[]{:S(2)}) copy-start(f32[512,1536]{1,0:T(8,128)} %get-tuple-element.49) | copy-start | bytes 9437188
  406.0 13.5 %copy-start = (f32[512,1536]{1,0:T(8,128)S(1)}, f32[512,1536]{1,0:T(8,128)}, u32[]{:S(2)}) copy-start(f32[512,1536]{1,0:T(8,128)} %get-tuple-element.45.refs_13_) | copy-start | bytes 9437188
  406.0 57.2 %collective-permute-start.28 = (f32[384,1536]{1,0:T(8,128)S(1)}, f32[384,1536]{1,0:T(8,128)}, u32[]{:S(2)}, u32[]{:S(2)}) collective-permute-start(f32[384,1536]{1,0:T(8,128)S(1)} %add.100), channel_id=1, source_target_pairs={{0,6},{1,7},{2,0},{3,1},{4,2},{5,3},{6,4},{7,5},{8,14},{9,15},{10,... | collective-permute-start | bytes 7077896 | tf_op jit(solution)/shard_map/ppermute | solution.py:413
  413.7 58.2 %collective-permute-start.24 = (f32[128,1536]{1,0:T(8,128)}, f32[128,1536]{1,0:T(8,128)S(1)}, u32[]{:S(2)}, u32[]{:S(2)}) collective-permute-start(f32[128,1536]{1,0:T(8,128)} %add.101), channel_id=1, source_target_pairs={{0,2},{1,3},{2,4},{3,5},{4,6},{5,7},{6,0},{7,1},{8,10},{9,11},{10,... | collective-permute-start | bytes 2359304 | tf_op jit(solution)/shard_map/ppermute | solution.py:410
  415.8 8.2 %copy-start.7 = (f32[512,1536]{1,0:T(8,128)S(1)}, f32[512,1536]{1,0:T(8,128)}, u32[]{:S(2)}) copy-start(f32[512,1536]{1,0:T(8,128)} %get-tuple-element.51) | copy-start | bytes 9437188
  415.8 8.2 %copy-start.8 = (f32[512,1536]{1,0:T(8,128)S(1)}, f32[512,1536]{1,0:T(8,128)}, u32[]{:S(2)}) copy-start(f32[512,1536]{1,0:T(8,128)} %get-tuple-element.50) | copy-start | bytes 9437188
  415.8 57.9 %collective-permute-start.26 = (f32[128,1536]{1,0:T(8,128)}, f32[128,1536]{1,0:T(8,128)}, u32[]{:S(2)}, u32[]{:S(2)}) collective-permute-start(f32[128,1536]{1,0:T(8,128)} %add.102), channel_id=1, source_target_pairs={{0,6},{1,7},{2,0},{3,1},{4,2},{5,3},{6,4},{7,5},{8,14},{9,15},{10,... | collective-permute-start | bytes 2359304 | tf_op jit(solution)/shard_map/ppermute | solution.py:413
  (8 other events, 33.7 us)

commit v7 on v5

--- a/solution.py
+++ b/solution.py
@@ -390,7 +390,7 @@
         experts = w_router.shape[1]
         slots_dev = w_gate.shape[0]
         half = tok_dev // 2
-        parts = (3 * half // 4, half // 4)
+        parts = (5 * half // 8, 3 * half // 8)
         capacity = (5 * tok_dev * group_size * top_k + 4 * experts - 1) // (4 * experts)
         local_max = (2 * tok_dev * top_k + experts - 1) // experts
         me = lax.axis_index('ep')
@@ -406,6 +406,7 @@
         def after(v, *deps):
             return lax.optimization_barrier((v,) + deps)[0]
 
+        sib_gate = lax.ppermute(w_gate, 'ep', sibling)
         ha, hb = norm_call(hidden_in, norm_gain)
         ha_r1, hb_l1 = go_right(ha), go_left(hb)
 
@@ -418,13 +419,11 @@
         count_rows = jnp.pad(jnp.concatenate([own_counts, sib_counts], axis=0), ((0, (-2 * top_k - 2) % 8), (0, tok_dev - experts)))
         table = jnp.concatenate([topk_idx.T.astype(F32), gate_vals.T, count_rows], axis=0)
         own_w = (w_gate, w_up, w_down)
-        sib_w = tuple(lax.ppermute(after(w, sib_counts), 'ep', sibling) for w in own_w)
+        sib_w = (sib_gate, *(lax.ppermute(after(w, sib_counts), 'ep', sibling) for w in own_w[1:]))
         t_r1, t_l1 = go_right(table), go_left(table)
         t_far = lax.ppermute(table, 'ep', far)
 
         hb_r1, ha_l1 = go_right(hb), go_left(ha)
-        half_sums = shared_call(hidden_in, ha, hb, w_sgate, s_gate, s_up, s_down)
-
         ha_r2, hb_l2 = go_right(ha_r1), go_left(hb_l1)
 
         steps = jnp.arange(group_size // cores)
@@ -443,11 +442,12 @@
         p = [go_right(y2[0]), go_left(y2[2])]
         p += [go_right(y2[1]), go_left(y2[3])]
         y1 = expert_call(routes(3, 2 * local_max), ha_l1, hb_r1, own_w, sib_w, y2[0], 2 * local_max, parts * 2)
+        half_sums = shared_call(hidden_in, after(ha, y1[0]), hb, w_sgate, s_gate, s_up, s_down)
 
         def relay(i, *deps):
             return y1[i] + after(p[2 * i], *deps), y1[2 + i] + after(p[2 * i + 1], *deps)
 
-        add_a, add_b = relay(0, y1[0])
+        add_a, add_b = relay(0, half_sums[0])
         z0 = go_right(add_a), go_left(add_b)
         y0 = expert_call(routes(0, local_max), ha, hb, own_w, sib_w, add_b, local_max, (half, half))
         add_a, add_b = relay(1, y0[0])

time: 399 us -> 420 us (1.053)
  waiting for transfers between devices: 118 us -> 128 us
  starting transfers between devices: 40.2 us -> 48.1 us
    ppermute x9, waiting for transfers between devices: 2.81 us -> 116 us  [go_left(): return lax.ppermute(v, 'ep', left)]
    ppermute x9, waiting for transfers between devices: 111 us -> 0.97 us  [go_right(): return lax.ppermute(v, 'ep', right)]
    ppermute x9, starting transfers between devices: 29.5 us -> 41.3 us  [go_left(): return lax.ppermute(v, 'ep', left)]
    ppermute x1, waiting for transfers between devices: 1.13 us -> 11 us  [block(): sib_counts = lax.ppermute(own_counts, 'ep', sibling)]
    ppermute x9, starting transfers between devices: 9.37 us -> 2.77 us  [go_right(): return lax.ppermute(v, 'ep', right)]
  transfers between devices with their start and end apart: 23 -> 23, of which waited for: 8 -> 7; matrix products, arithmetic and copies ran while one was open for 7% -> 7% of each run, Pallas kernels for 50% -> 49%
where the time goes in v7:
time: 420 us; the launch traced here: 418 us
  Pallas kernels  210 us (50%)
  waiting for transfers between devices  128 us (30%)
  starting transfers between devices  48.1 us (11%)
  other arithmetic  21.5 us (5%)
  local copies, waits for them, and re-layouts  7.59 us (2%)
    pallas_call x4, Pallas kernels, expert_call(): pl.pallas_call(functools.partial(expert_kernel, sizes, classes, slots_dev...  159 us
    ppermute x9, waiting for transfers between devices, go_left(): return lax.ppermute(v, 'ep', left)  116 us
    ppermute x9, starting transfers between devices, go_left(): return lax.ppermute(v, 'ep', left)  41.3 us
    pallas_call x1, Pallas kernels, shared_call(): pl.pallas_call(shared_kernel, grid=(ff // chunk,), out_shape=(out, out),...  21.3 us
    pallas_call x1, Pallas kernels, route_call(): pl.pallas_call(functools.partial(route_kernel, (top_k, slots_dev, capacit...  14.9 us
    ppermute x1, waiting for transfers between devices, block(): sib_counts = lax.ppermute(own_counts, 'ep', sibling)  11 us
    pallas_call x2, Pallas kernels, final_call(): pl.pallas_call(final_kernel, grid=(size // rows,), out_shape=jax.ShapeDty...  9.84 us
    add x2, other arithmetic, block(): base = [half_sums[i] + y0[i] + d for i, d in enumerate((d_a, d_b))]  9.35 us
  transfers between devices with their start and end apart: 23, of which 7 were waited for; matrix products, arithmetic and copies ran while one was open for 7% of the time, Pallas kernels for 49%

profile of v7, /device:TPU:88, one launch (start us, length us, event | category | flops | bytes accessed | tf_op | source)
XLA Modules:
  0.0 417.6 jit_solution(8179304964202804175)
XLA Ops:
  0.0 4.7 %norm.1 = (bf16[512,1536]{1,0:T(8,128)(2,1)}, bf16[512,1536]{1,0:T(8,128)(2,1)}) custom-call(bf16[2,512,1536]{2,1,0:T(8,128)(2,1)} %bitcast.33, bf16[1536]{0:T(1024)(128)(2,1)} %gain_ref.1), custom_call_target="tpu_custom_call" | custom-call | flops 6291456 | bytes 6291456 | tf_op jit(solution)/shard_map/norm/pallas_call | solution.py:29
  4.7 2.1 fusion.6
  6.8 0.6 fusion.5
  7.6 0.4 select_reduce_fusion
  8.0 0.5 collective-permute-start
  8.5 11.0 %collective-permute-done = f32[1,64]{1,0:T(1,128)S(1)} collective-permute-done((f32[1,64]{1,0:T(1,128)S(1)}, f32[1,64]{1,0:T(1,128)S(1)}, u32[]{:S(2)}, u32[]{:S(2)}) %collective-permute-start) | collective-permute-done | bytes 288 | tf_op jit(solution)/shard_map/ppermute | solution.py:418
  19.6 0.4 collective-permute-start.8
  20.1 1.7 collective-permute-start.3
  21.8 3.0 collective-permute-start.2
  24.8 0.9 collective-permute-done.3.prev_ref
  25.7 2.4 collective-permute-start.1
  28.3 0.9 collective-permute-start.11
  29.2 1.4 collective-permute-done.1.next_ref
  30.8 0.6 pad_add_fusion.1.ids_ref
  31.5 14.9 %route.1 = (s32[4,16,8,384]{3,2,1,0:T(8,128)}, f32[4,16,8,384]{3,2,1,0:T(8,128)}, f32[4,16,128]{2,1,0:T(8,128)}) custom-call(s32[10]{0:T(128)} %pad_add_fusion.1.ids_ref, f32[16,1024]{1,0:T(8,128)} %copy-done.16, f32[16,1024]{1,0:T(8,128)} %copy-done.20, f32[16,1024]{1,0:T(8,128)} %copy-done.19, f32[16,1024]{1,0:T(8,128)} %copy-done.18), custom_call_target="tpu_custom_call" | custom-call | flops 1000000 | bytes 2000000 | tf_op jit(solution)/shard_map/route/pallas_call | solution.py:204
  46.4 1.4 copy.31
  47.8 16.1 %collective-permute-done.11.refs_4_ = bf16[512,1536]{1,0:T(8,128)(2,1)} collective-permute-done((bf16[512,1536]{1,0:T(8,128)(2,1)}, bf16[512,1536]{1,0:T(8,128)(2,1)}, u32[]{:S(2)}, u32[]{:S(2)}) %collective-permute-start.11) | collective-permute-done | bytes 1572896 | tf_op jit(solution)/shard_map/ppermute | solution.py:402
  63.9 2.8 collective-permute-start.12
  66.9 0.6 slice_bitcast_fusion.7
  67.6 0.5 collective-permute-start.5
  68.1 0.6 slice_bitcast_fusion.6
  69.0 0.7 slice_reduce_fusion
  69.7 0.6 slice_bitcast_fusion.5
  70.3 0.6 slice_bitcast_fusion.4
  70.9 40.0 %experts.4 = (f32[512,1536]{1,0:T(8,128)}, f32[512,1536]{1,0:T(8,128)}) custom-call(s32[16,384]{1,0:T(8,128)} %get-tuple-element.66.refs_0_, f32[16,384]{1,0:T(8,128)} %get-tuple-element.64.refs_1_, s32[16]{0:T(128)} %get-tuple-element.58.refs_2_, bf16[512,1536]{1,0:T(8,128)(2,1)} %collective-permute-done.9.refs_3_, ...), custom_call_target="tpu_custom_call" | custom-call | flops 1000000 | bytes 75497472 | tf_op jit(solution)/shard_map/experts/pallas_call | solution.py:363
  111.0 1.1 copy-done.13
  112.2 39.4 %experts.5 = (f32[320,1536]{1,0:T(8,128)}, f32[192,1536]{1,0:T(8,128)}, f32[320,1536]{1,0:T(8,128)}, f32[192,1536]{1,0:T(8,128)}) custom-call(s32[16,192]{1,0:T(8,128)} %get-tuple-element.70.refs_0_, f32[16,192]{1,0:T(8,128)} %get-tuple-element.68.refs_1_, s32[16]{0:T(128)} %get-tuple-element.59.refs_2_, bf16[512,1536]{1,0:T(8,128)(2,1)} %copy-done.13, ...), custom_call_target="tpu_custom_call" | custom-call | flops 1000000 | bytes 75497472 | tf_op jit(solution)/shard_map/experts/pallas_call | solution.py:363
  151.5 0.4 collective-permute-start.20
  152.0 12.7 %collective-permute-start.14 = (f32[512,1536]{1,0:T(8,128)}, f32[512,1536]{1,0:T(8,128)}, u32[]{:S(2)}, u32[]{:S(2)}) collective-permute-start(f32[512,1536]{1,0:T(8,128)} %get-tuple-element.38.refs_11_), channel_id=1, source_target_pairs={{0,6},{1,7},{2,0},{3,1},{4,2},{5,3},{6,4},{7,5},{8,14},{9,15},{10,... | collective-permute-start | bytes 9437192 | tf_op jit(solution)/shard_map/ppermute | solution.py:402
  164.6 1.9 collective-permute-start.4
  166.7 3.1 collective-permute-start.13
  169.8 97.3 %collective-permute-done.4.refs_3_ = bf16[512,1536]{1,0:T(8,128)(2,1)S(1)} collective-permute-done((bf16[512,1536]{1,0:T(8,128)(2,1)S(1)}, bf16[512,1536]{1,0:T(8,128)(2,1)S(1)}, u32[]{:S(2)}, u32[]{:S(2)}) %collective-permute-start.4) | collective-permute-done | bytes 1572896 | tf_op jit(solution)/shard_map/ppermute | solution.py:402
  267.0 1.1 copy-done.14
  268.2 3.7 collective-permute-start.18
  271.9 38.8 %experts.6 = (f32[320,1536]{1,0:T(8,128)}, f32[192,1536]{1,0:T(8,128)}, f32[320,1536]{1,0:T(8,128)}, f32[192,1536]{1,0:T(8,128)}) custom-call(s32[16,384]{1,0:T(8,128)} %get-tuple-element.65.refs_0_, f32[16,384]{1,0:T(8,128)} %get-tuple-element.63.refs_1_, s32[16]{0:T(128)} %get-tuple-element.60.refs_2_, bf16[512,1536]{1,0:T(8,128)(2,1)} %copy-done.14, ...), custom_call_target="tpu_custom_call" | custom-call | flops 1000000 | bytes 75497472 | tf_op jit(solution)/shard_map/experts/pallas_call | solution.py:363
  310.7 21.3 %shared.1 = (f32[512,1536]{1,0:T(8,128)}, f32[512,1536]{1,0:T(8,128)}) custom-call(bf16[2,512,1536]{2,1,0:T(8,128)(2,1)} %bitcast.34, bf16[512,1536]{1,0:T(8,128)(2,1)} %get-tuple-element.41.refs_11_.ha_ref.refs_3_, bf16[512,1536]{1,0:T(8,128)(2,1)} %get-tuple-element.32.hb_ref.refs_4_, bf16[1,1536]{1,0:T(2,128)(2,1)} %bitcast.36, ...), custom_call_target="tpu_custom_call" | custom-call | flops 1000000 | bytes 9437184 | tf_op jit(solution)/shard_map/shared/pallas_call | solution.py:96
  332.1 3.2 add.102
  335.3 1.8 add.95.refs_11_
  337.1 10.7 %collective-permute-start.22 = (f32[320,1536]{1,0:T(8,128)S(1)}, f32[320,1536]{1,0:T(8,128)}, u32[]{:S(2)}, u32[]{:S(2)}) collective-permute-start(f32[320,1536]{1,0:T(8,128)S(1)} %add.95.refs_11_), channel_id=1, source_target_pairs={{0,6},{1,7},{2,0},{3,1},{4,2},{5,3},{6,4},{7,5},{8,14},{9,15},{10,... | collective-permute-start | bytes 5898248 | tf_op jit(solution)/shard_map/ppermute | solution.py:402
  347.8 40.5 %experts.7 = (f32[512,1536]{1,0:T(8,128)}, f32[512,1536]{1,0:T(8,128)}) custom-call(s32[16,192]{1,0:T(8,128)} %get-tuple-element.69.refs_0_, f32[16,192]{1,0:T(8,128)} %get-tuple-element.67.refs_1_, s32[16]{0:T(128)} %get-tuple-element.57.refs_2_, bf16[512,1536]{1,0:T(8,128)(2,1)} %get-tuple-element.41.refs_11_.ha_ref.refs_3_, ...), custom_call_target="tpu_custom_call" | custom-call | flops 1000000 | bytes 75497472 | tf_op jit(solution)/shard_map/experts/pallas_call | solution.py:363
  388.3 2.9 add.100
  391.2 3.0 add.101
  394.2 3.1 collective-permute-start.19
  397.3 4.7 %add_add_fusion.1.base_a = f32[512,1536]{1,0:T(8,128)} fusion(f32[512,1536]{1,0:T(8,128)} %collective-permute-done.14, f32[512,1536]{1,0:T(8,128)S(1)} %copy-done.8, f32[512,1536]{1,0:T(8,128)S(1)} %copy-done.10), kind=kLoop, calls=%fused_computation.1 | loop fusion | flops 1572864 | bytes 12582912 | tf_op jit(solution)/shard_map/add | solution.py:455
  402.0 4.7 %add_add_fusion.base_b = f32[512,1536]{1,0:T(8,128)} fusion(f32[512,1536]{1,0:T(8,128)} %collective-permute-done.15, f32[512,1536]{1,0:T(8,128)S(1)} %copy-done.7, f32[512,1536]{1,0:T(8,128)S(1)} %copy-done.9), kind=kLoop, calls=%fused_computation | loop fusion | flops 1572864 | bytes 12582912 | tf_op jit(solution)/shard_map/add | solution.py:455
  406.7 5.8 %final.2.rest_0_ = bf16[2,512,1536]{2,1,0:T(8,128)(2,1)} custom-call(f32[512,1536]{1,0:T(8,128)} %add_add_fusion.1.base_a, f32[512,1536]{1,0:T(8,128)} %add_add_fusion.base_b, f32[320,1536]{1,0:T(8,128)} %collective-permute-done.21.za_ref, f32[320,1536]{1,0:T(8,128)} %collective-permute-done.22.zb_ref), custom_call_target="tpu_custom_call" | custom-call | flops 1966080 | bytes 9830400 | tf_op jit(solution)/shard_map/final/pallas_call | solution.py:54
  412.5 0.9 collective-permute-done.19.zb_ref
  413.5 4.0 final.3
  (82 shorter events, 1.4 us)
Async XLA Ops:
  0.0 4.7 %copy-start = (bf16[1536,64]{0,1:T(8,128)(2,1)S(1)}, bf16[1536,64]{0,1:T(8,128)(2,1)}, u32[]{:S(2)}) copy-start(bf16[1536,64]{0,1:T(8,128)(2,1)} %param.14) | copy-start | bytes 589828
  0.0 67.6 %collective-permute-start.6 = (bf16[8,1536,512]{2,1,0:T(8,128)(2,1)}, bf16[8,1536,512]{2,1,0:T(8,128)(2,1)}, u32[]{:S(2)}, u32[]{:S(2)}) collective-permute-start(bf16[8,1536,512]{2,1,0:T(8,128)(2,1)} %refs_5_.7), channel_id=1, source_target_pairs={{0,1},{1,0},{2,3},{3,2},{4,5},{5,4},{6,7},{7,6},{8,9},{9,8},{10,11... | collective-permute-start | bytes 37748744 | tf_op jit(solution)/shard_map/ppermute | solution.py:409
  4.7 2.1 copy-start.2
  4.7 2.9 copy-start.17
  8.0 11.5 %collective-permute-start = (f32[1,64]{1,0:T(1,128)S(1)}, f32[1,64]{1,0:T(1,128)S(1)}, u32[]{:S(2)}, u32[]{:S(2)}) collective-permute-start(f32[1,64]{1,0:T(1,128)S(1)} %bitcast.37), channel_id=1, source_target_pairs={{0,1},{1,0},{2,3},{3,2},{4,5},{5,4},{6,7},{7,6},{8,9},{9,8},{10,11... | collective-permute-start | bytes 776 | tf_op jit(solution)/shard_map/ppermute | solution.py:418
  19.5 51.4 %collective-permute-start.7 = (bf16[8,1536,512]{2,1,0:T(8,128)(2,1)}, bf16[8,1536,512]{2,1,0:T(8,128)(2,1)}, u32[]{:S(2)}, u32[]{:S(2)}) collective-permute-start(bf16[8,1536,512]{2,1,0:T(8,128)(2,1)} %refs_6_.7), channel_id=1, source_target_pairs={{0,1},{1,0},{2,3},{3,2},{4,5},{5,4},{6,7},{7,6},{8,9},{9,8},{10,11... | collective-permute-start | bytes 37748744 | tf_op jit(solution)/shard_map/ppermute | solution.py:422
  19.6 51.3 %collective-permute-start.8 = (bf16[8,512,1536]{2,1,0:T(8,128)(2,1)}, bf16[8,512,1536]{2,1,0:T(8,128)(2,1)}, u32[]{:S(2)}, u32[]{:S(2)}) collective-permute-start(bf16[8,512,1536]{2,1,0:T(8,128)(2,1)} %refs_7_.7), channel_id=1, source_target_pairs={{0,1},{1,0},{2,3},{3,2},{4,5},{5,4},{6,7},{7,6},{8,9},{9,8},{10,11... | collective-permute-start | bytes 37748744 | tf_op jit(solution)/shard_map/ppermute | solution.py:422
  20.1 11.4 %copy-start.16 = (f32[16,1024]{1,0:T(8,128)}, f32[16,1024]{1,0:T(8,128)S(1)}, u32[]{:S(2)}) copy-start(f32[16,1024]{1,0:T(8,128)S(1)} %pad_maximum_fusion.1.own_ref) | copy-start | bytes 196612
  20.1 5.7 %collective-permute-start.3 = (f32[16,1024]{1,0:T(8,128)S(1)}, f32[16,1024]{1,0:T(8,128)S(1)}, u32[]{:S(2)}, u32[]{:S(2)}) collective-permute-start(f32[16,1024]{1,0:T(8,128)S(1)} %pad_maximum_fusion.1.own_ref), channel_id=1, source_target_pairs={{0,2},{1,3},{2,4},{3,5},{4,6},{5,7},{6,0},{7,1},{8,10},{9,11},{10,... | collective-permute-start | bytes 196616 | tf_op jit(solution)/shard_map/ppermute | solution.py:399
  21.8 6.5 %collective-permute-start.2 = (f32[16,1024]{1,0:T(8,128)S(1)}, f32[16,1024]{1,0:T(8,128)S(1)}, u32[]{:S(2)}, u32[]{:S(2)}) collective-permute-start(f32[16,1024]{1,0:T(8,128)S(1)} %pad_maximum_fusion.1.own_ref), channel_id=1, source_target_pairs={{0,4},{1,5},{2,6},{3,7},{4,0},{5,1},{6,2},{7,3},{8,12},{9,13},{10,... | collective-permute-start | bytes 196616 | tf_op jit(solution)/shard_map/ppermute | solution.py:424
  25.7 5.7 %copy-start.18 = (f32[16,1024]{1,0:T(8,128)}, f32[16,1024]{1,0:T(8,128)S(1)}, u32[]{:S(2)}) copy-start(f32[16,1024]{1,0:T(8,128)S(1)} %collective-permute-done.3.prev_ref) | copy-start | bytes 196612
  25.7 4.9 %collective-permute-start.1 = (f32[16,1024]{1,0:T(8,128)S(1)}, f32[16,1024]{1,0:T(8,128)S(1)}, u32[]{:S(2)}, u32[]{:S(2)}) collective-permute-start(f32[16,1024]{1,0:T(8,128)S(1)} %pad_maximum_fusion.1.own_ref), channel_id=1, source_target_pairs={{0,6},{1,7},{2,0},{3,1},{4,2},{5,3},{6,4},{7,5},{8,14},{9,15},{10,... | collective-permute-start | bytes 196616 | tf_op jit(solution)/shard_map/ppermute | solution.py:402
  28.3 3.2 copy-start.19
  28.3 35.6 %collective-permute-start.11 = (bf16[512,1536]{1,0:T(8,128)(2,1)}, bf16[512,1536]{1,0:T(8,128)(2,1)}, u32[]{:S(2)}, u32[]{:S(2)}) collective-permute-start(bf16[512,1536]{1,0:T(8,128)(2,1)} %get-tuple-element.32.hb_ref.refs_4_), channel_id=1, source_target_pairs={{0,6},{1,7},{2,0},{3,1},{4,2},{5,3},{6,4},{7,5},{8,14},{9,15},{10,... | collective-permute-start | bytes 4718600 | tf_op jit(solution)/shard_map/ppermute | solution.py:402
  30.6 0.8 copy-start.20
  30.6 36.1 %collective-permute-start.9 = (bf16[512,1536]{1,0:T(8,128)(2,1)S(1)}, bf16[512,1536]{1,0:T(8,128)(2,1)}, u32[]{:S(2)}, u32[]{:S(2)}) collective-permute-start(bf16[512,1536]{1,0:T(8,128)(2,1)S(1)} %copy-done.2), channel_id=1, source_target_pairs={{0,2},{1,3},{2,4},{3,5},{4,6},{5,7},{6,0},{7,1},{8,10},{9,11},{10,... | collective-permute-start | bytes 4718600 | tf_op jit(solution)/shard_map/ppermute | solution.py:399
  46.4 20.4 %copy-start.5 = (f32[4,16,8,384]{3,2,1,0:T(8,128)S(1)}, f32[4,16,8,384]{3,2,1,0:T(8,128)}, u32[]{:S(2)}) copy-start(f32[4,16,8,384]{3,2,1,0:T(8,128)} %get-tuple-element.34) | copy-start | bytes 2359300
  46.4 21.2 %copy-start.21 = (f32[4,16,128]{2,1,0:T(8,128)S(1)}, f32[4,16,128]{2,1,0:T(8,128)}, u32[]{:S(2)}) copy-start(f32[4,16,128]{2,1,0:T(8,128)} %get-tuple-element.35) | copy-start | bytes 98308
  46.4 22.3 %copy-start.6 = (s32[4,16,8,384]{3,2,1,0:T(8,128)S(1)}, s32[4,16,8,384]{3,2,1,0:T(8,128)}, u32[]{:S(2)}) copy-start(s32[4,16,8,384]{3,2,1,0:T(8,128)} %get-tuple-element.33) | copy-start | bytes 2359300
  63.9 47.1 %collective-permute-start.12 = (bf16[512,1536]{1,0:T(8,128)(2,1)}, bf16[512,1536]{1,0:T(8,128)(2,1)}, u32[]{:S(2)}, u32[]{:S(2)}) collective-permute-start(bf16[512,1536]{1,0:T(8,128)(2,1)} %collective-permute-done.11.refs_4_), channel_id=1, source_target_pairs={{0,6},{1,7},{2,0},{3,1},{4,2},{5,3},{6,4},{7,5},{8,14},{9,15},{10,... | collective-permute-start | bytes 4718600 | tf_op jit(solution)/shard_map/ppermute | solution.py:402
  66.7 44.3 %collective-permute-start.10 = (bf16[512,1536]{1,0:T(8,128)(2,1)}, bf16[512,1536]{1,0:T(8,128)(2,1)S(1)}, u32[]{:S(2)}, u32[]{:S(2)}) collective-permute-start(bf16[512,1536]{1,0:T(8,128)(2,1)} %collective-permute-done.9.refs_3_), channel_id=1, source_target_pairs={{0,2},{1,3},{2,4},{3,5},{4,6},{5,7},{6,0},{7,1},{8,10},{9,11},{10,... | collective-permute-start | bytes 4718600 | tf_op jit(solution)/shard_map/ppermute | solution.py:399
  67.6 99.1 %collective-permute-start.5 = (bf16[512,1536]{1,0:T(8,128)(2,1)}, bf16[512,1536]{1,0:T(8,128)(2,1)}, u32[]{:S(2)}, u32[]{:S(2)}) collective-permute-start(bf16[512,1536]{1,0:T(8,128)(2,1)} %get-tuple-element.32.hb_ref.refs_4_), channel_id=1, source_target_pairs={{0,2},{1,3},{2,4},{3,5},{4,6},{5,7},{6,0},{7,1},{8,10},{9,11},{10,... | collective-permute-start | bytes 4718600 | tf_op jit(solution)/shard_map/ppermute | solution.py:399
  111.0 1.1 copy-start.13
  112.2 52.5 %copy-start.3 = (bf16[512,1536]{1,0:T(8,128)(2,1)S(1)}, bf16[512,1536]{1,0:T(8,128)(2,1)}, u32[]{:S(2)}) copy-start(bf16[512,1536]{1,0:T(8,128)(2,1)} %get-tuple-element.41.refs_11_.ha_ref.refs_3_) | copy-start | bytes 4718596
  151.5 120.3 %collective-permute-start.20 = (f32[320,1536]{1,0:T(8,128)}, f32[320,1536]{1,0:T(8,128)}, u32[]{:S(2)}, u32[]{:S(2)}) collective-permute-start(f32[320,1536]{1,0:T(8,128)} %get-tuple-element.39.refs_11_), channel_id=1, source_target_pairs={{0,2},{1,3},{2,4},{3,5},{4,6},{5,7},{6,0},{7,1},{8,10},{9,11},{10,... | collective-permute-start | bytes 5898248 | tf_op jit(solution)/shard_map/ppermute | solution.py:399
  152.0 242.3 %collective-permute-start.14 = (f32[512,1536]{1,0:T(8,128)}, f32[512,1536]{1,0:T(8,128)}, u32[]{:S(2)}, u32[]{:S(2)}) collective-permute-start(f32[512,1536]{1,0:T(8,128)} %get-tuple-element.38.refs_11_), channel_id=1, source_target_pairs={{0,6},{1,7},{2,0},{3,1},{4,2},{5,3},{6,4},{7,5},{8,14},{9,15},{10,... | collective-permute-start | bytes 9437192 | tf_op jit(solution)/shard_map/ppermute | solution.py:402
  164.6 102.4 %collective-permute-start.4 = (bf16[512,1536]{1,0:T(8,128)(2,1)S(1)}, bf16[512,1536]{1,0:T(8,128)(2,1)S(1)}, u32[]{:S(2)}, u32[]{:S(2)}) collective-permute-start(bf16[512,1536]{1,0:T(8,128)(2,1)S(1)} %copy-done.3), channel_id=1, source_target_pairs={{0,6},{1,7},{2,0},{3,1},{4,2},{5,3},{6,4},{7,5},{8,14},{9,15},{10,... | collective-permute-start | bytes 4718600 | tf_op jit(solution)/shard_map/ppermute | solution.py:402
  166.5 235.5 %collective-permute-start.15 = (f32[512,1536]{1,0:T(8,128)}, f32[512,1536]{1,0:T(8,128)}, u32[]{:S(2)}, u32[]{:S(2)}) collective-permute-start(f32[512,1536]{1,0:T(8,128)} %get-tuple-element.49), channel_id=1, source_target_pairs={{0,2},{1,3},{2,4},{3,5},{4,6},{5,7},{6,0},{7,1},{8,10},{9,11},{10,... | collective-permute-start | bytes 9437192 | tf_op jit(solution)/shard_map/ppermute | solution.py:399
  166.7 168.6 %collective-permute-start.13 = (f32[320,1536]{1,0:T(8,128)}, f32[320,1536]{1,0:T(8,128)}, u32[]{:S(2)}, u32[]{:S(2)}) collective-permute-start(f32[320,1536]{1,0:T(8,128)} %get-tuple-element.44), channel_id=1, source_target_pairs={{0,6},{1,7},{2,0},{3,1},{4,2},{5,3},{6,4},{7,5},{8,14},{9,15},{10,... | collective-permute-start | bytes 5898248 | tf_op jit(solution)/shard_map/ppermute | solution.py:402
  267.0 1.1 copy-start.14
  268.2 79.6 %collective-permute-start.18 = (f32[192,1536]{1,0:T(8,128)}, f32[192,1536]{1,0:T(8,128)}, u32[]{:S(2)}, u32[]{:S(2)}) collective-permute-start(f32[192,1536]{1,0:T(8,128)} %get-tuple-element.54), channel_id=1, source_target_pairs={{0,6},{1,7},{2,0},{3,1},{4,2},{5,3},{6,4},{7,5},{8,14},{9,15},{10,... | collective-permute-start | bytes 3538952 | tf_op jit(solution)/shard_map/ppermute | solution.py:402
  271.9 116.4 %collective-permute-start.16 = (f32[192,1536]{1,0:T(8,128)}, f32[192,1536]{1,0:T(8,128)}, u32[]{:S(2)}, u32[]{:S(2)}) collective-permute-start(f32[192,1536]{1,0:T(8,128)} %get-tuple-element.51), channel_id=1, source_target_pairs={{0,2},{1,3},{2,4},{3,5},{4,6},{5,7},{6,0},{7,1},{8,10},{9,11},{10,... | collective-permute-start | bytes 3538952 | tf_op jit(solution)/shard_map/ppermute | solution.py:399
  310.7 21.4 %copy-start.12 = (f32[320,1536]{1,0:T(8,128)S(1)}, f32[320,1536]{1,0:T(8,128)}, u32[]{:S(2)}) copy-start(f32[320,1536]{1,0:T(8,128)} %get-tuple-element.40) | copy-start | bytes 5898244
  332.1 3.2 copy-start.11
  337.1 10.7 %copy-start.4 = (f32[320,1536]{1,0:T(8,128)}, f32[320,1536]{1,0:T(8,128)S(1)}, u32[]{:S(2)}) copy-start(f32[320,1536]{1,0:T(8,128)S(1)} %add.95.refs_11_) | copy-start | bytes 5898244
  337.1 69.6 %collective-permute-start.22 = (f32[320,1536]{1,0:T(8,128)S(1)}, f32[320,1536]{1,0:T(8,128)}, u32[]{:S(2)}, u32[]{:S(2)}) collective-permute-start(f32[320,1536]{1,0:T(8,128)S(1)} %add.95.refs_11_), channel_id=1, source_target_pairs={{0,6},{1,7},{2,0},{3,1},{4,2},{5,3},{6,4},{7,5},{8,14},{9,15},{10,... | collective-permute-start | bytes 5898248 | tf_op jit(solution)/shard_map/ppermute | solution.py:402
  347.8 58.9 %collective-permute-start.21 = (f32[320,1536]{1,0:T(8,128)}, f32[320,1536]{1,0:T(8,128)}, u32[]{:S(2)}, u32[]{:S(2)}) collective-permute-start(f32[320,1536]{1,0:T(8,128)} %add.102), channel_id=1, source_target_pairs={{0,2},{1,3},{2,4},{3,5},{4,6},{5,7},{6,0},{7,1},{8,10},{9,11},{10,... | collective-permute-start | bytes 5898248 | tf_op jit(solution)/shard_map/ppermute | solution.py:399
  388.3 9.0 %copy-start.10 = (f32[512,1536]{1,0:T(8,128)S(1)}, f32[512,1536]{1,0:T(8,128)}, u32[]{:S(2)}) copy-start(f32[512,1536]{1,0:T(8,128)} %get-tuple-element.46) | copy-start | bytes 9437188
  391.2 6.1 %copy-start.8 = (f32[512,1536]{1,0:T(8,128)S(1)}, f32[512,1536]{1,0:T(8,128)}, u32[]{:S(2)}) copy-start(f32[512,1536]{1,0:T(8,128)} %get-tuple-element.42) | copy-start | bytes 9437188
  391.2 21.3 %collective-permute-start.17 = (f32[192,1536]{1,0:T(8,128)}, f32[192,1536]{1,0:T(8,128)S(1)}, u32[]{:S(2)}, u32[]{:S(2)}) collective-permute-start(f32[192,1536]{1,0:T(8,128)} %add.100), channel_id=1, source_target_pairs={{0,2},{1,3},{2,4},{3,5},{4,6},{5,7},{6,0},{7,1},{8,10},{9,11},{10,... | collective-permute-start | bytes 3538952 | tf_op jit(solution)/shard_map/ppermute | solution.py:399
  394.2 19.2 %collective-permute-start.19 = (f32[192,1536]{1,0:T(8,128)}, f32[192,1536]{1,0:T(8,128)}, u32[]{:S(2)}, u32[]{:S(2)}) collective-permute-start(f32[192,1536]{1,0:T(8,128)} %add.101), channel_id=1, source_target_pairs={{0,6},{1,7},{2,0},{3,1},{4,2},{5,3},{6,4},{7,5},{8,14},{9,15},{10,... | collective-permute-start | bytes 3538952 | tf_op jit(solution)/shard_map/ppermute | solution.py:402
  397.3 4.7 %copy-start.7 = (f32[512,1536]{1,0:T(8,128)S(1)}, f32[512,1536]{1,0:T(8,128)}, u32[]{:S(2)}) copy-start(f32[512,1536]{1,0:T(8,128)} %get-tuple-element.47) | copy-start | bytes 9437188
  397.3 4.7 %copy-start.9 = (f32[512,1536]{1,0:T(8,128)S(1)}, f32[512,1536]{1,0:T(8,128)}, u32[]{:S(2)}) copy-start(f32[512,1536]{1,0:T(8,128)} %get-tuple-element.48) | copy-start | bytes 9437188
  412.5 1.0 copy-start.15
  413.5 4.0 copy-start.1

commit v8 on v7

--- a/solution.py
+++ b/solution.py
@@ -106,7 +106,7 @@
     )(hidden_in.reshape(2, half, hidden), ha, hb, w_sgate.reshape(1, hidden), s_gate, s_up, s_down)
 
 
-def route_kernel(geom, ids_ref, own_ref, next_ref, far_ref, prev_ref, list_ref, glist_ref, count_ref, slot_ref, gate_ref):
+def route_kernel(geom, which, ids_ref, own_ref, next_ref, far_ref, prev_ref, list_ref, glist_ref, count_ref, slot_ref, gate_ref):
     top_k, slots_dev, capacity, local_max = geom
     toks = own_ref.shape[1]
     slots = 2 * slots_dev
@@ -157,7 +157,7 @@
             slot_ref[j, :, c * tile:(c + 1) * tile] = jnp.where(kept, 1.0, 0.0)
     joined = []
     gates = [gate_ref[j] for j in range(4)]
-    for v, (ja, jb) in enumerate(PAIRS):
+    for v, (ja, jb) in enumerate(PAIRS[w] for w in which):
         joined.append(jnp.concatenate([slot_ref[ja][:, :half], slot_ref[jb][:, half:]], axis=1))
         gate_ref[v] = jnp.concatenate([gates[ja][:, :half], gates[jb][:, half:]], axis=1)
         count_ref[v] = jnp.broadcast_to(jnp.sum(joined[v], axis=1, keepdims=True), (slots, 128))
@@ -165,7 +165,7 @@
     kept_bf = kept_all.astype(BF16)
     for c in range(toks // tile):
         pos = jnp.dot(kept_bf, before(c), preferred_element_type=F32)
-        for v in range(4):
+        for v in range(len(which)):
             kept = kept_all[v * slots:(v + 1) * slots, c * tile:(c + 1) * tile] > 0.0
             slot_ref[v, :, c * tile:(c + 1) * tile] = jnp.where(kept, pos[v * slots:(v + 1) * slots], -1.0)
     token = lax.broadcasted_iota(jnp.int32, (8, toks), 1)
@@ -175,14 +175,14 @@
     count_row = lax.broadcasted_iota(jnp.int32, (slots, 128), 0)
 
     def lists(e, carry):
-        for j in range(4):
+        for j, w in enumerate(which):
             pos = jnp.sum(jnp.where(row_of == e, slot_ref[j], 0.0), axis=0, keepdims=True)
             gate = jnp.sum(jnp.where(row_of == e, gate_ref[j], 0.0), axis=0, keepdims=True)
             g1 = gate.astype(BF16).astype(F32)
             g2 = (gate - g1).astype(BF16).astype(F32)
             g3 = gate - g1 - g2
             left = jnp.where(row8 < 2, digits, jnp.where(row8 == 2, g1, jnp.where(row8 == 3, g2, g3))).astype(BF16)
-            width = local_max if PAIRS[j][0] == PAIRS[j][1] else 2 * local_max
+            width = local_max if PAIRS[w][0] == PAIRS[w][1] else 2 * local_max
             want = lax.broadcasted_iota(jnp.int32, (width, toks), 0).astype(F32)
             pick = jnp.where(want == pos, 1.0, 0.0).astype(BF16)
             got = lax.dot_general(left, pick, (((1,), (1,)), ((), ())), preferred_element_type=F32)
@@ -197,14 +197,14 @@
     lax.fori_loop(0, slots, lists, 0)
 
 
-def route_call(ids, own, nxt, far, prv, top_k, slots_dev, capacity, local_max):
+def route_call(which, ids, own, nxt, far, prv, top_k, slots_dev, capacity, local_max):
     toks = own.shape[1]
     slots = 2 * slots_dev
     vmem = pl.BlockSpec(memory_space=pltpu.VMEM)
     return pl.pallas_call(
-        functools.partial(route_kernel, (top_k, slots_dev, capacity, local_max)),
-        out_shape=(jax.ShapeDtypeStruct((4, slots, 8, 2 * local_max), jnp.int32), jax.ShapeDtypeStruct((4, slots, 8, 2 * local_max), F32),
-                   jax.ShapeDtypeStruct((4, slots, 128), F32)),
+        functools.partial(route_kernel, (top_k, slots_dev, capacity, local_max), which),
+        out_shape=(jax.ShapeDtypeStruct((len(which), slots, 8, 2 * local_max), jnp.int32),
+                   jax.ShapeDtypeStruct((len(which), slots, 8, 2 * local_max), F32), jax.ShapeDtypeStruct((len(which), slots, 128), F32)),
         in_specs=[pl.BlockSpec(memory_space=pltpu.SMEM)] + [vmem] * 4,
         out_specs=(vmem,) * 3,
         scratch_shapes=[pltpu.VMEM((4, slots, toks), F32), pltpu.VMEM((4, slots, toks), F32)],
@@ -326,28 +326,29 @@
 
     @pl.when(step == steps - 1)
     def _():
-        start = 0
-        for n, (ref, size) in enumerate(zip(ys, sizes)):
-            def put(i, n=n, ref=ref):
-                rows = pl.ds(pl.multiple_of(i * group, group), group)
-                return pltpu.make_async_copy(stage_ref.at[i % 2, n], ref.at[rows], out_sems.at[i % 2, n])
-
-            def unpack(i, carry, n=n, start=start, put=put):
+        size = sizes[0]
+        outs = [(0, ref, n * size) for n, ref in enumerate(ys)]
+
+        def put(n, ref, i):
+            rows = pl.ds(pl.multiple_of(i * group, group), group)
+            return pltpu.make_async_copy(stage_ref.at[i % 2, n], ref.at[rows], out_sems.at[i % 2, n])
+
+        def unpack(i, carry):
+            for n, (q, ref, start) in enumerate(outs):
                 @pl.when(i >= 2)
                 def _():
-                    put(i - 2).wait()
+                    put(n, ref, i).wait()
 
                 for j, (w, k) in enumerate(split):
                     stage_ref[i % 2, n, :, j * 128:(j + 1) * 128] = (
-                        sum_refs[0][w][pl.ds((start + i * group) * pitch + k, group, stride=pitch), :])
-                put(i).start()
-                return carry
-
-            lax.fori_loop(0, size // group, unpack, 0)
-            start += size
-        for n, (ref, size) in enumerate(zip(ys, sizes)):
-            for i in range(2):
-                pltpu.make_async_copy(stage_ref.at[i, n], ref.at[pl.ds(0, group)], out_sems.at[i, n]).wait()
+                        sum_refs[q][w][pl.ds((start + i * group) * pitch + k, group, stride=pitch), :])
+                put(n, ref, i).start()
+            return carry
+
+        lax.fori_loop(0, size // group, unpack, 0)
+        for i in range(2):
+            for n, (q, ref, start) in enumerate(outs):
+                put(n, ref, i).wait()
 
 
 def expert_call(routes, ha, hb, own, sib, dep, row_max, sizes):
@@ -390,7 +391,7 @@
         experts = w_router.shape[1]
         slots_dev = w_gate.shape[0]
         half = tok_dev // 2
-        parts = (5 * half // 8, 3 * half // 8)
+        parts = (half // 2, half // 2)
         capacity = (5 * tok_dev * group_size * top_k + 4 * experts - 1) // (4 * experts)
         local_max = (2 * tok_dev * top_k + experts - 1) // experts
         me = lax.axis_index('ep')
@@ -429,15 +430,20 @@
         steps = jnp.arange(group_size // cores)
         rel = cores * ((chip + steps) % (group_size // cores))
         ids = jnp.concatenate([jnp.stack([rel + core, rel + 1 - core], axis=1).reshape(-1), jnp.stack([chip, core])]).astype(jnp.int32)
-        lists, glists, kept = route_call(ids, table, t_l1, t_far, t_r1, top_k, slots_dev, capacity, local_max)
-        lists, glists = lists[:, :, 0, :], glists[:, :, 0, :]
-        kept = kept[:, :, 0].astype(jnp.int32)
+
+        def plan(which, *deps):
+            got = route_call(which, ids, after(table, *deps), t_l1, t_far, t_r1, top_k, slots_dev, capacity, local_max)
+            lists, glists, kept = got[0][:, :, 0, :], got[1][:, :, 0, :], got[2][:, :, 0].astype(jnp.int32)
+            return {v: (lists[n], glists[n], kept[n]) for n, v in enumerate(which)}
+
+        plans = plan((1,))
 
         def routes(v, row_max):
-            return lists[v, :, :row_max], glists[v, :, :row_max], kept[v]
+            return plans[v][0][:, :row_max], plans[v][1][:, :row_max], plans[v][2]
 
         d_a, d_b = expert_call(routes(1, 2 * local_max), ha_r1, hb_l1, own_w, sib_w, ha, 2 * local_max, (half, half))
         d_dep, d_a, d_b = d_a, go_left(d_a), go_right(d_b)
+        plans.update(plan((2, 3, 0), d_dep))
         y2 = expert_call(routes(2, local_max), ha_r2, hb_l2, own_w, sib_w, d_dep, local_max, parts * 2)
         p = [go_right(y2[0]), go_left(y2[2])]
         p += [go_right(y2[1]), go_left(y2[3])]

time: 420 us -> 400 us (0.952)
  Pallas kernels: 210 us -> 201 us
  starting transfers between devices: 48.1 us -> 39.2 us
  waiting for transfers between devices: 128 us -> 122 us
    ppermute x9, waiting for transfers between devices: 0.97 us -> 76.2 us  [go_right(): return lax.ppermute(v, 'ep', right)]
    ppermute x9, waiting for transfers between devices: 116 us -> 44.9 us  [go_left(): return lax.ppermute(v, 'ep', left)]
    pallas_call x4, Pallas kernels: 159 us -> 147 us  [expert_call(): pl.pallas_call(functools.partial(expert_kernel, sizes, classes, slots_dev...]
    ppermute x1, waiting for transfers between devices: 11 us -> 0.65 us  [block(): sib_counts = lax.ppermute(own_counts, 'ep', sibling)]
    ppermute x9, starting transfers between devices: 41.3 us -> 33.1 us  [go_left(): return lax.ppermute(v, 'ep', left)]
    pallas_call x1 -> x2, Pallas kernels: 14.9 us -> 19.3 us  [route_call(): pl.pallas_call(functools.partial(route_kernel, (top_k, slots_dev, capacit...]
  transfers between devices with their start and end apart: 23 -> 23, of which waited for: 7 -> 9; matrix products, arithmetic and copies ran while one was open for 7% -> 8% of each run, Pallas kernels for 49% -> 48%
where the time goes in v8:
time: 400 us; the launch traced here: 397 us
  Pallas kernels  201 us (50%)
  waiting for transfers between devices  122 us (30%)
  starting transfers between devices  39.2 us (10%)
  other arithmetic  22.9 us (6%)
  local copies, waits for them, and re-layouts  8.98 us (2%)
    pallas_call x4, Pallas kernels, expert_call(): pl.pallas_call(functools.partial(expert_kernel, sizes, classes, slots_dev...  147 us
    ppermute x9, waiting for transfers between devices, go_right(): return lax.ppermute(v, 'ep', right)  76.2 us
    ppermute x9, waiting for transfers between devices, go_left(): return lax.ppermute(v, 'ep', left)  44.9 us
    ppermute x9, starting transfers between devices, go_left(): return lax.ppermute(v, 'ep', left)  33.1 us
    pallas_call x1, Pallas kernels, shared_call(): pl.pallas_call(shared_kernel, grid=(ff // chunk,), out_shape=(out, out),...  21.3 us
    pallas_call x2, Pallas kernels, route_call(): pl.pallas_call(functools.partial(route_kernel, (top_k, slots_dev, capacit...  19.3 us
    add x2, other arithmetic, block(): base = [half_sums[i] + y0[i] + d for i, d in enumerate((d_a, d_b))]  9.32 us
    pallas_call x2, Pallas kernels, final_call(): pl.pallas_call(final_kernel, grid=(size // rows,), out_shape=jax.ShapeDty...  8.98 us
  transfers between devices with their start and end apart: 23, of which 9 were waited for; matrix products, arithmetic and copies ran while one was open for 8% of the time, Pallas kernels for 48%

profile of v8, /device:TPU:88, one launch (start us, length us, event | category | flops | bytes accessed | tf_op | source)
XLA Modules:
  0.0 396.9 jit_solution(7278498818507170264)
XLA Ops:
  0.0 4.7 %norm.1 = (bf16[512,1536]{1,0:T(8,128)(2,1)}, bf16[512,1536]{1,0:T(8,128)(2,1)}) custom-call(bf16[2,512,1536]{2,1,0:T(8,128)(2,1)} %bitcast.29, bf16[1536]{0:T(1024)(128)(2,1)} %gain_ref.1), custom_call_target="tpu_custom_call" | custom-call | flops 6291456 | bytes 6291456 | tf_op jit(solution)/shard_map/norm/pallas_call | solution.py:29
  4.7 2.1 fusion.6
  8.5 0.7 collective-permute-done
  9.8 1.7 collective-permute-start.3
  11.5 3.0 collective-permute-start.2
  14.5 1.0 collective-permute-done.3.prev_ref
  15.5 2.4 collective-permute-start.1
  18.0 0.9 collective-permute-start.5
  18.9 1.5 collective-permute-done.1.next_ref
  20.4 33.3 %collective-permute-done.5.refs_4_ = bf16[512,1536]{1,0:T(8,128)(2,1)} collective-permute-done((bf16[512,1536]{1,0:T(8,128)(2,1)}, bf16[512,1536]{1,0:T(8,128)(2,1)}, u32[]{:S(2)}, u32[]{:S(2)}) %collective-permute-start.5) | collective-permute-done | bytes 1572896 | tf_op jit(solution)/shard_map/ppermute | solution.py:403
  53.6 2.8 collective-permute-start.12
  56.6 0.7 pad_add_fusion.1.ids_ref
  57.3 7.8 %route.2 = (s32[1,16,8,384]{3,2,1,0:T(8,128)}, f32[1,16,8,384]{3,2,1,0:T(8,128)}, f32[1,16,128]{2,1,0:T(8,128)}) custom-call(s32[10]{0:T(128)} %pad_add_fusion.1.ids_ref, f32[16,1024]{1,0:T(8,128)} %copy-done.13, f32[16,1024]{1,0:T(8,128)} %copy-done.16, f32[16,1024]{1,0:T(8,128)} %copy-done.15, f32[16,1024]{1,0:T(8,128)} %copy-done.14), custom_call_target="tpu_custom_call" | custom-call | flops 1000000 | bytes 2000000 | tf_op jit(solution)/shard_map/route/pallas_call | solution.py:204
  65.1 1.0 copy.33
  66.1 1.0 copy.34
  67.1 1.4 convert_reduce_fusion.1.refs_2_
  68.4 0.6 slice_bitcast_fusion.7.refs_0_
  69.0 0.6 slice_bitcast_fusion.6.refs_1_
  69.9 3.3 collective-permute-start.9
  73.2 37.6 %experts.4 = (f32[512,1536]{1,0:T(8,128)}, f32[512,1536]{1,0:T(8,128)}) custom-call(s32[16,384]{1,0:T(8,128)} %slice_bitcast_fusion.7.refs_0_, f32[16,384]{1,0:T(8,128)} %slice_bitcast_fusion.6.refs_1_, s32[16]{0:T(128)} %convert_reduce_fusion.1.refs_2_, bf16[512,1536]{1,0:T(8,128)(2,1)} %collective-permute-done.4.refs_3_, ...), custom_call_target="tpu_custom_call" | custom-call | flops 1000000 | bytes 75497472 | tf_op jit(solution)/shard_map/experts/pallas_call | solution.py:364
  110.7 11.5 %route.3 = (s32[3,16,8,384]{3,2,1,0:T(8,128)}, f32[3,16,8,384]{3,2,1,0:T(8,128)}, f32[3,16,128]{2,1,0:T(8,128)}) custom-call(s32[10]{0:T(128)} %pad_add_fusion.1.ids_ref, f32[16,1024]{1,0:T(8,128)} %copy-done.13, f32[16,1024]{1,0:T(8,128)} %copy-done.16, f32[16,1024]{1,0:T(8,128)} %copy-done.15, f32[16,1024]{1,0:T(8,128)} %copy-done.14), custom_call_target="tpu_custom_call" | custom-call | flops 1000000 | bytes 2000000 | tf_op jit(solution)/shard_map/route/pallas_call | solution.py:204
  122.2 1.2 copy.35
  123.6 0.6 slice_bitcast_fusion.1
  124.2 0.6 slice_bitcast_fusion
  124.8 0.7 slice_reduce_fusion
  125.6 0.6 slice.91.refs_0_
  126.8 35.8 %experts.5 = (f32[256,1536]{1,0:T(8,128)}, f32[256,1536]{1,0:T(8,128)}, f32[256,1536]{1,0:T(8,128)}, f32[256,1536]{1,0:T(8,128)}) custom-call(s32[16,192]{1,0:T(8,128)} %slice.91.refs_0_, f32[16,192]{1,0:T(8,128)} %slice.93.refs_1_, s32[16]{0:T(128)} %get-tuple-element.68.refs_2_, bf16[512,1536]{1,0:T(8,128)(2,1)} %collective-permute-done.11.refs_3_, ...), custom_call_target="tpu_custom_call" | custom-call | flops 1000000 | bytes 75497472 | tf_op jit(solution)/shard_map/experts/pallas_call | solution.py:364
  162.7 11.7 %collective-permute-start.14 = (f32[512,1536]{1,0:T(8,128)}, f32[512,1536]{1,0:T(8,128)}, u32[]{:S(2)}, u32[]{:S(2)}) collective-permute-start(f32[512,1536]{1,0:T(8,128)} %get-tuple-element.42.refs_11_), channel_id=1, source_target_pairs={{0,6},{1,7},{2,0},{3,1},{4,2},{5,3},{6,4},{7,5},{8,14},{9,15},{10,... | collective-permute-start | bytes 9437192 | tf_op jit(solution)/shard_map/ppermute | solution.py:403
  174.4 3.2 collective-permute-start.13
  177.7 0.7 collective-permute-start.18
  178.4 31.5 %collective-permute-done.20 = f32[256,1536]{1,0:T(8,128)} collective-permute-done((f32[256,1536]{1,0:T(8,128)}, f32[256,1536]{1,0:T(8,128)}, u32[]{:S(2)}, u32[]{:S(2)}) %collective-permute-start.20) | collective-permute-done | bytes 1572896 | tf_op jit(solution)/shard_map/ppermute | solution.py:400
  209.9 0.6 slice.96.refs_0_
  211.1 35.4 %experts.6 = (f32[256,1536]{1,0:T(8,128)}, f32[256,1536]{1,0:T(8,128)}, f32[256,1536]{1,0:T(8,128)}, f32[256,1536]{1,0:T(8,128)}) custom-call(s32[16,384]{1,0:T(8,128)} %get-tuple-element.75.refs_0_, f32[16,384]{1,0:T(8,128)} %get-tuple-element.72.refs_1_, s32[16]{0:T(128)} %get-tuple-element.69.refs_2_, bf16[512,1536]{1,0:T(8,128)(2,1)} %collective-permute-done.9.refs_3_, ...), custom_call_target="tpu_custom_call" | custom-call | flops 1000000 | bytes 75497472 | tf_op jit(solution)/shard_map/experts/pallas_call | solution.py:364
  246.5 21.3 %shared.1 = (f32[512,1536]{1,0:T(8,128)}, f32[512,1536]{1,0:T(8,128)}) custom-call(bf16[2,512,1536]{2,1,0:T(8,128)(2,1)} %bitcast.30, bf16[512,1536]{1,0:T(8,128)(2,1)} %get-tuple-element.49.refs_11_.ha_ref.refs_3_, bf16[512,1536]{1,0:T(8,128)(2,1)} %get-tuple-element.36.hb_ref.refs_4_, bf16[1,1536]{1,0:T(2,128)(2,1)} %bitcast.32, ...), custom_call_target="tpu_custom_call" | custom-call | flops 1000000 | bytes 9437184 | tf_op jit(solution)/shard_map/shared/pallas_call | solution.py:96
  267.8 2.9 add.102
  270.7 6.2 %collective-permute-done.13 = f32[256,1536]{1,0:T(8,128)} collective-permute-done((f32[256,1536]{1,0:T(8,128)}, f32[256,1536]{1,0:T(8,128)}, u32[]{:S(2)}, u32[]{:S(2)}) %collective-permute-start.13) | collective-permute-done | bytes 1572896 | tf_op jit(solution)/shard_map/ppermute | solution.py:403
  276.9 1.7 add.95.refs_11_
  278.6 4.7 %collective-permute-start.22 = (f32[256,1536]{1,0:T(8,128)S(1)}, f32[256,1536]{1,0:T(8,128)}, u32[]{:S(2)}, u32[]{:S(2)}) collective-permute-start(f32[256,1536]{1,0:T(8,128)S(1)} %add.95.refs_11_), channel_id=1, source_target_pairs={{0,6},{1,7},{2,0},{3,1},{4,2},{5,3},{6,4},{7,5},{8,14},{9,15},{10,... | collective-permute-start | bytes 4718600 | tf_op jit(solution)/shard_map/ppermute | solution.py:403
  283.3 38.0 %experts.7 = (f32[512,1536]{1,0:T(8,128)}, f32[512,1536]{1,0:T(8,128)}) custom-call(s32[16,192]{1,0:T(8,128)} %slice.96.refs_0_, f32[16,192]{1,0:T(8,128)} %slice.98.refs_1_, s32[16]{0:T(128)} %get-tuple-element.67.refs_2_, bf16[512,1536]{1,0:T(8,128)(2,1)} %get-tuple-element.49.refs_11_.ha_ref.refs_3_, bf16[512,1536]{1,0:T(8,128)(2,1)} %get-tuple-element.36.hb_ref.refs_4_, ...), custom_call_target="tpu_custom_call" | custom-call | flops 1000000 | bytes 75497472 | tf_op jit(solution)/shard_map/experts/pallas_call | solution.py:364
  321.4 3.4 add.100
  324.8 2.9 add.101
  327.7 3.2 collective-permute-start.19
  331.0 4.7 %add_add_fusion.1.base_a = f32[512,1536]{1,0:T(8,128)} fusion(f32[512,1536]{1,0:T(8,128)} %collective-permute-done.14, f32[512,1536]{1,0:T(8,128)S(1)} %copy-done.5, f32[512,1536]{1,0:T(8,128)S(1)} %copy-done.7), kind=kLoop, calls=%fused_computation.1 | loop fusion | flops 1572864 | bytes 12582912 | tf_op jit(solution)/shard_map/add | solution.py:461
  335.7 4.6 %add_add_fusion.base_b = f32[512,1536]{1,0:T(8,128)} fusion(f32[512,1536]{1,0:T(8,128)} %collective-permute-done.15, f32[512,1536]{1,0:T(8,128)S(1)} %copy-done.4, f32[512,1536]{1,0:T(8,128)S(1)} %copy-done.6), kind=kLoop, calls=%fused_computation | loop fusion | flops 1572864 | bytes 12582912 | tf_op jit(solution)/shard_map/add | solution.py:461
  340.3 3.9 collective-permute-done.22.zb_ref
  344.2 43.7 %collective-permute-done.21.za_ref = f32[256,1536]{1,0:T(8,128)} collective-permute-done((f32[256,1536]{1,0:T(8,128)S(1)}, f32[256,1536]{1,0:T(8,128)}, u32[]{:S(2)}, u32[]{:S(2)}) %collective-permute-start.21) | collective-permute-done | bytes 1572896 | tf_op jit(solution)/shard_map/ppermute | solution.py:400
  387.9 4.5 %final.2.rest_0_ = bf16[2,512,1536]{2,1,0:T(8,128)(2,1)} custom-call(f32[512,1536]{1,0:T(8,128)} %add_add_fusion.1.base_a, f32[512,1536]{1,0:T(8,128)} %add_add_fusion.base_b, f32[256,1536]{1,0:T(8,128)} %collective-permute-done.21.za_ref, f32[256,1536]{1,0:T(8,128)} %collective-permute-done.22.zb_ref), custom_call_target="tpu_custom_call" | custom-call | flops 1572864 | bytes 7864320 | tf_op jit(solution)/shard_map/final/pallas_call | solution.py:54
  392.4 4.5 %final.3 = bf16[2,512,1536]{2,1,0:T(8,128)(2,1)} custom-call(f32[512,1536]{1,0:T(8,128)} %add_add_fusion.1.base_a, f32[512,1536]{1,0:T(8,128)} %add_add_fusion.base_b, f32[256,1536]{1,0:T(8,128)} %collective-permute-done.17.za_ref, f32[256,1536]{1,0:T(8,128)} %collective-permute-done.19.zb_ref, ...), custom_call_target="tpu_custom_call", output_to_operand_aliasing={{}: (4, {})} | custom-call | flops 1572864 | bytes 7864320 | tf_op jit(solution)/shard_map/final/pallas_call | solution.py:54
  (80 shorter events, 4.3 us)
Async XLA Ops:
  0.0 4.7 %copy-start = (bf16[1536,64]{0,1:T(8,128)(2,1)S(1)}, bf16[1536,64]{0,1:T(8,128)(2,1)}, u32[]{:S(2)}) copy-start(bf16[1536,64]{0,1:T(8,128)(2,1)} %param.14) | copy-start | bytes 589828
  4.7 2.1 copy-start.2
  6.8 0.8 copy-start.17
  7.9 1.3 collective-permute-start
  8.1 61.6 %collective-permute-start.6 = (bf16[8,1536,512]{2,1,0:T(8,128)(2,1)}, bf16[8,1536,512]{2,1,0:T(8,128)(2,1)}, u32[]{:S(2)}, u32[]{:S(2)}) collective-permute-start(bf16[8,1536,512]{2,1,0:T(8,128)(2,1)} %refs_5_.7), channel_id=1, source_target_pairs={{0,1},{1,0},{2,3},{3,2},{4,5},{5,4},{6,7},{7,6},{8,9},{9,8},{10,11... | collective-permute-start | bytes 37748744 | tf_op jit(solution)/shard_map/ppermute | solution.py:410
  9.2 60.7 %collective-permute-start.7 = (bf16[8,1536,512]{2,1,0:T(8,128)(2,1)}, bf16[8,1536,512]{2,1,0:T(8,128)(2,1)}, u32[]{:S(2)}, u32[]{:S(2)}) collective-permute-start(bf16[8,1536,512]{2,1,0:T(8,128)(2,1)} %refs_6_.7), channel_id=1, source_target_pairs={{0,1},{1,0},{2,3},{3,2},{4,5},{5,4},{6,7},{7,6},{8,9},{9,8},{10,11... | collective-permute-start | bytes 37748744 | tf_op jit(solution)/shard_map/ppermute | solution.py:423
  9.4 63.8 %collective-permute-start.8 = (bf16[8,512,1536]{2,1,0:T(8,128)(2,1)}, bf16[8,512,1536]{2,1,0:T(8,128)(2,1)}, u32[]{:S(2)}, u32[]{:S(2)}) collective-permute-start(bf16[8,512,1536]{2,1,0:T(8,128)(2,1)} %refs_7_.7), channel_id=1, source_target_pairs={{0,1},{1,0},{2,3},{3,2},{4,5},{5,4},{6,7},{7,6},{8,9},{9,8},{10,11... | collective-permute-start | bytes 37748744 | tf_op jit(solution)/shard_map/ppermute | solution.py:423
  9.7 47.5 %copy-start.13 = (f32[16,1024]{1,0:T(8,128)}, f32[16,1024]{1,0:T(8,128)S(1)}, u32[]{:S(2)}) copy-start(f32[16,1024]{1,0:T(8,128)S(1)} %pad_maximum_fusion.1.own_ref) | copy-start | bytes 196612
  9.8 5.7 %collective-permute-start.3 = (f32[16,1024]{1,0:T(8,128)S(1)}, f32[16,1024]{1,0:T(8,128)S(1)}, u32[]{:S(2)}, u32[]{:S(2)}) collective-permute-start(f32[16,1024]{1,0:T(8,128)S(1)} %pad_maximum_fusion.1.own_ref), channel_id=1, source_target_pairs={{0,2},{1,3},{2,4},{3,5},{4,6},{5,7},{6,0},{7,1},{8,10},{9,11},{10,... | collective-permute-start | bytes 196616 | tf_op jit(solution)/shard_map/ppermute | solution.py:400
  11.5 6.5 %collective-permute-start.2 = (f32[16,1024]{1,0:T(8,128)S(1)}, f32[16,1024]{1,0:T(8,128)S(1)}, u32[]{:S(2)}, u32[]{:S(2)}) collective-permute-start(f32[16,1024]{1,0:T(8,128)S(1)} %pad_maximum_fusion.1.own_ref), channel_id=1, source_target_pairs={{0,4},{1,5},{2,6},{3,7},{4,0},{5,1},{6,2},{7,3},{8,12},{9,13},{10,... | collective-permute-start | bytes 196616 | tf_op jit(solution)/shard_map/ppermute | solution.py:425
  15.4 41.8 %copy-start.14 = (f32[16,1024]{1,0:T(8,128)}, f32[16,1024]{1,0:T(8,128)S(1)}, u32[]{:S(2)}) copy-start(f32[16,1024]{1,0:T(8,128)S(1)} %collective-permute-done.3.prev_ref) | copy-start | bytes 196612
  15.5 4.9 %collective-permute-start.1 = (f32[16,1024]{1,0:T(8,128)S(1)}, f32[16,1024]{1,0:T(8,128)S(1)}, u32[]{:S(2)}, u32[]{:S(2)}) collective-permute-start(f32[16,1024]{1,0:T(8,128)S(1)} %pad_maximum_fusion.1.own_ref), channel_id=1, source_target_pairs={{0,6},{1,7},{2,0},{3,1},{4,2},{5,3},{6,4},{7,5},{8,14},{9,15},{10,... | collective-permute-start | bytes 196616 | tf_op jit(solution)/shard_map/ppermute | solution.py:403
  18.0 39.3 %copy-start.15 = (f32[16,1024]{1,0:T(8,128)}, f32[16,1024]{1,0:T(8,128)S(1)}, u32[]{:S(2)}) copy-start(f32[16,1024]{1,0:T(8,128)S(1)} %collective-permute-done.2.far_ref) | copy-start | bytes 196612
  18.0 35.6 %collective-permute-start.5 = (bf16[512,1536]{1,0:T(8,128)(2,1)}, bf16[512,1536]{1,0:T(8,128)(2,1)}, u32[]{:S(2)}, u32[]{:S(2)}) collective-permute-start(bf16[512,1536]{1,0:T(8,128)(2,1)} %get-tuple-element.36.hb_ref.refs_4_), channel_id=1, source_target_pairs={{0,6},{1,7},{2,0},{3,1},{4,2},{5,3},{6,4},{7,5},{8,14},{9,15},{10,... | collective-permute-start | bytes 4718600 | tf_op jit(solution)/shard_map/ppermute | solution.py:403
  20.4 36.9 %copy-start.16 = (f32[16,1024]{1,0:T(8,128)}, f32[16,1024]{1,0:T(8,128)S(1)}, u32[]{:S(2)}) copy-start(f32[16,1024]{1,0:T(8,128)S(1)} %collective-permute-done.1.next_ref) | copy-start | bytes 196612
  20.4 36.1 %collective-permute-start.4 = (bf16[512,1536]{1,0:T(8,128)(2,1)S(1)}, bf16[512,1536]{1,0:T(8,128)(2,1)}, u32[]{:S(2)}, u32[]{:S(2)}) collective-permute-start(bf16[512,1536]{1,0:T(8,128)(2,1)S(1)} %copy-done.2), channel_id=1, source_target_pairs={{0,2},{1,3},{2,4},{3,5},{4,6},{5,7},{6,0},{7,1},{8,10},{9,11},{10,... | collective-permute-start | bytes 4718600 | tf_op jit(solution)/shard_map/ppermute | solution.py:400
  53.6 73.1 %collective-permute-start.12 = (bf16[512,1536]{1,0:T(8,128)(2,1)}, bf16[512,1536]{1,0:T(8,128)(2,1)}, u32[]{:S(2)}, u32[]{:S(2)}) collective-permute-start(bf16[512,1536]{1,0:T(8,128)(2,1)} %collective-permute-done.5.refs_4_), channel_id=1, source_target_pairs={{0,6},{1,7},{2,0},{3,1},{4,2},{5,3},{6,4},{7,5},{8,14},{9,15},{10,... | collective-permute-start | bytes 4718600 | tf_op jit(solution)/shard_map/ppermute | solution.py:403
  56.5 70.3 %collective-permute-start.11 = (bf16[512,1536]{1,0:T(8,128)(2,1)}, bf16[512,1536]{1,0:T(8,128)(2,1)}, u32[]{:S(2)}, u32[]{:S(2)}) collective-permute-start(bf16[512,1536]{1,0:T(8,128)(2,1)} %collective-permute-done.4.refs_3_), channel_id=1, source_target_pairs={{0,2},{1,3},{2,4},{3,5},{4,6},{5,7},{6,0},{7,1},{8,10},{9,11},{10,... | collective-permute-start | bytes 4718600 | tf_op jit(solution)/shard_map/ppermute | solution.py:400
  69.7 104.8 %collective-permute-start.10 = (bf16[512,1536]{1,0:T(8,128)(2,1)}, bf16[512,1536]{1,0:T(8,128)(2,1)}, u32[]{:S(2)}, u32[]{:S(2)}) collective-permute-start(bf16[512,1536]{1,0:T(8,128)(2,1)} %get-tuple-element.36.hb_ref.refs_4_), channel_id=1, source_target_pairs={{0,2},{1,3},{2,4},{3,5},{4,6},{5,7},{6,0},{7,1},{8,10},{9,11},{10,... | collective-permute-start | bytes 4718600 | tf_op jit(solution)/shard_map/ppermute | solution.py:400
  69.9 107.8 %collective-permute-start.9 = (bf16[512,1536]{1,0:T(8,128)(2,1)S(1)}, bf16[512,1536]{1,0:T(8,128)(2,1)}, u32[]{:S(2)}, u32[]{:S(2)}) collective-permute-start(bf16[512,1536]{1,0:T(8,128)(2,1)S(1)} %copy-done.2), channel_id=1, source_target_pairs={{0,6},{1,7},{2,0},{3,1},{4,2},{5,3},{6,4},{7,5},{8,14},{9,15},{10,... | collective-permute-start | bytes 4718600 | tf_op jit(solution)/shard_map/ppermute | solution.py:403
  122.2 1.2 copy-start.12
  122.2 1.4 copy-start.18
  162.6 47.3 %collective-permute-start.20 = (f32[256,1536]{1,0:T(8,128)}, f32[256,1536]{1,0:T(8,128)}, u32[]{:S(2)}, u32[]{:S(2)}) collective-permute-start(f32[256,1536]{1,0:T(8,128)} %get-tuple-element.47.refs_11_), channel_id=1, source_target_pairs={{0,2},{1,3},{2,4},{3,5},{4,6},{5,7},{6,0},{7,1},{8,10},{9,11},{10,... | collective-permute-start | bytes 4718600 | tf_op jit(solution)/shard_map/ppermute | solution.py:400
  162.7 168.3 %collective-permute-start.14 = (f32[512,1536]{1,0:T(8,128)}, f32[512,1536]{1,0:T(8,128)}, u32[]{:S(2)}, u32[]{:S(2)}) collective-permute-start(f32[512,1536]{1,0:T(8,128)} %get-tuple-element.42.refs_11_), channel_id=1, source_target_pairs={{0,6},{1,7},{2,0},{3,1},{4,2},{5,3},{6,4},{7,5},{8,14},{9,15},{10,... | collective-permute-start | bytes 9437192 | tf_op jit(solution)/shard_map/ppermute | solution.py:403
  174.4 161.3 %collective-permute-start.15 = (f32[512,1536]{1,0:T(8,128)}, f32[512,1536]{1,0:T(8,128)}, u32[]{:S(2)}, u32[]{:S(2)}) collective-permute-start(f32[512,1536]{1,0:T(8,128)} %get-tuple-element.57), channel_id=1, source_target_pairs={{0,2},{1,3},{2,4},{3,5},{4,6},{5,7},{6,0},{7,1},{8,10},{9,11},{10,... | collective-permute-start | bytes 9437192 | tf_op jit(solution)/shard_map/ppermute | solution.py:400
  174.4 102.5 %collective-permute-start.13 = (f32[256,1536]{1,0:T(8,128)}, f32[256,1536]{1,0:T(8,128)}, u32[]{:S(2)}, u32[]{:S(2)}) collective-permute-start(f32[256,1536]{1,0:T(8,128)} %get-tuple-element.52), channel_id=1, source_target_pairs={{0,6},{1,7},{2,0},{3,1},{4,2},{5,3},{6,4},{7,5},{8,14},{9,15},{10,... | collective-permute-start | bytes 4718600 | tf_op jit(solution)/shard_map/ppermute | solution.py:403
  177.7 143.7 %collective-permute-start.18 = (f32[256,1536]{1,0:T(8,128)}, f32[256,1536]{1,0:T(8,128)}, u32[]{:S(2)}, u32[]{:S(2)}) collective-permute-start(f32[256,1536]{1,0:T(8,128)} %get-tuple-element.62), channel_id=1, source_target_pairs={{0,6},{1,7},{2,0},{3,1},{4,2},{5,3},{6,4},{7,5},{8,14},{9,15},{10,... | collective-permute-start | bytes 4718600 | tf_op jit(solution)/shard_map/ppermute | solution.py:403
  209.9 111.5 %collective-permute-start.16 = (f32[256,1536]{1,0:T(8,128)}, f32[256,1536]{1,0:T(8,128)}, u32[]{:S(2)}, u32[]{:S(2)}) collective-permute-start(f32[256,1536]{1,0:T(8,128)} %get-tuple-element.59), channel_id=1, source_target_pairs={{0,2},{1,3},{2,4},{3,5},{4,6},{5,7},{6,0},{7,1},{8,10},{9,11},{10,... | collective-permute-start | bytes 4718600 | tf_op jit(solution)/shard_map/ppermute | solution.py:400
  246.4 21.3 %copy-start.11 = (f32[256,1536]{1,0:T(8,128)S(1)}, f32[256,1536]{1,0:T(8,128)}, u32[]{:S(2)}) copy-start(f32[256,1536]{1,0:T(8,128)} %get-tuple-element.48) | copy-start | bytes 4718596
  267.8 9.2 %copy-start.10 = (f32[256,1536]{1,0:T(8,128)S(1)}, f32[256,1536]{1,0:T(8,128)}, u32[]{:S(2)}) copy-start(f32[256,1536]{1,0:T(8,128)} %get-tuple-element.51) | copy-start | bytes 4718596
  278.6 4.8 %copy-start.3 = (f32[256,1536]{1,0:T(8,128)}, f32[256,1536]{1,0:T(8,128)S(1)}, u32[]{:S(2)}) copy-start(f32[256,1536]{1,0:T(8,128)S(1)} %add.95.refs_11_) | copy-start | bytes 4718596
  278.6 65.6 %collective-permute-start.22 = (f32[256,1536]{1,0:T(8,128)S(1)}, f32[256,1536]{1,0:T(8,128)}, u32[]{:S(2)}, u32[]{:S(2)}) collective-permute-start(f32[256,1536]{1,0:T(8,128)S(1)} %add.95.refs_11_), channel_id=1, source_target_pairs={{0,6},{1,7},{2,0},{3,1},{4,2},{5,3},{6,4},{7,5},{8,14},{9,15},{10,... | collective-permute-start | bytes 4718600 | tf_op jit(solution)/shard_map/ppermute | solution.py:403
  321.4 3.4 copy-start.9
  321.4 9.6 %copy-start.7 = (f32[512,1536]{1,0:T(8,128)S(1)}, f32[512,1536]{1,0:T(8,128)}, u32[]{:S(2)}) copy-start(f32[512,1536]{1,0:T(8,128)} %get-tuple-element.54) | copy-start | bytes 9437188
  324.8 67.6 %collective-permute-start.17 = (f32[256,1536]{1,0:T(8,128)}, f32[256,1536]{1,0:T(8,128)}, u32[]{:S(2)}, u32[]{:S(2)}) collective-permute-start(f32[256,1536]{1,0:T(8,128)} %add.100), channel_id=1, source_target_pairs={{0,2},{1,3},{2,4},{3,5},{4,6},{5,7},{6,0},{7,1},{8,10},{9,11},{10,... | collective-permute-start | bytes 4718600 | tf_op jit(solution)/shard_map/ppermute | solution.py:400
  324.8 6.2 %copy-start.8 = (f32[256,1536]{1,0:T(8,128)S(1)}, f32[256,1536]{1,0:T(8,128)}, u32[]{:S(2)}) copy-start(f32[256,1536]{1,0:T(8,128)} %add.102) | copy-start | bytes 4718596
  324.8 6.2 %copy-start.5 = (f32[512,1536]{1,0:T(8,128)S(1)}, f32[512,1536]{1,0:T(8,128)}, u32[]{:S(2)}) copy-start(f32[512,1536]{1,0:T(8,128)} %get-tuple-element.50) | copy-start | bytes 9437188
  327.7 64.7 %collective-permute-start.19 = (f32[256,1536]{1,0:T(8,128)}, f32[256,1536]{1,0:T(8,128)}, u32[]{:S(2)}, u32[]{:S(2)}) collective-permute-start(f32[256,1536]{1,0:T(8,128)} %add.101), channel_id=1, source_target_pairs={{0,6},{1,7},{2,0},{3,1},{4,2},{5,3},{6,4},{7,5},{8,14},{9,15},{10,... | collective-permute-start | bytes 4718600 | tf_op jit(solution)/shard_map/ppermute | solution.py:403
  331.0 57.0 %collective-permute-start.21 = (f32[256,1536]{1,0:T(8,128)S(1)}, f32[256,1536]{1,0:T(8,128)}, u32[]{:S(2)}, u32[]{:S(2)}) collective-permute-start(f32[256,1536]{1,0:T(8,128)S(1)} %copy-done.8), channel_id=1, source_target_pairs={{0,2},{1,3},{2,4},{3,5},{4,6},{5,7},{6,0},{7,1},{8,10},{9,11},{10,... | collective-permute-start | bytes 4718600 | tf_op jit(solution)/shard_map/ppermute | solution.py:400
  331.0 4.7 %copy-start.4 = (f32[512,1536]{1,0:T(8,128)S(1)}, f32[512,1536]{1,0:T(8,128)}, u32[]{:S(2)}) copy-start(f32[512,1536]{1,0:T(8,128)} %get-tuple-element.55) | copy-start | bytes 9437188
  331.0 4.7 %copy-start.6 = (f32[512,1536]{1,0:T(8,128)S(1)}, f32[512,1536]{1,0:T(8,128)}, u32[]{:S(2)}) copy-start(f32[512,1536]{1,0:T(8,128)} %get-tuple-element.56) | copy-start | bytes 9437188
  392.4 4.5 %copy-start.1 = (bf16[1536,64]{0,1:T(8,128)(2,1)S(1)}, bf16[1536,64]{0,1:T(8,128)(2,1)}, u32[]{:S(2)}) copy-start(bf16[1536,64]{0,1:T(8,128)(2,1)} %param.14) | copy-start | bytes 589828
